TPU v7x, 64 devices: a 2x2x8 block of a 4x4x8 slice. The times are simulated.
64 devices in a mesh: dp: 4 (over x, y), tp: 16 (over z, core).
Axes of the slice: x: 2, y: 2, z: 8, core: 2. Of those that a mesh axis runs over, the one named last changes fastest.
The devices are a block of a 4x4x8 slice.
Arguments:
- tok_ids: int32 [16, 512], P('dp'), parts along dimension 0
- embed: bfloat16 [2048, 4096], P('tp')
- norm_gain: float32 [4096], replicated
- q_gain: float32 [128], replicated
- k_gain: float32 [128], replicated
- w_query: bfloat16 [4096, 8192], P(None, 'tp')
- w_key: bfloat16 [4096, 512], P(None, 'tp')
- w_value: bfloat16 [4096, 512], P(None, 'tp')
- w_out: bfloat16 [8192, 4096], P('tp')
- grad_y: bfloat16 [16, 512, 4096], P('dp', 'tp'), parts along dimension 0
Outputs:
- output 1: bfloat16 [16, 512, 4096], P('dp', 'tp'), parts along dimension 0
- output 2: float32 [8192, 4096], P(('dp', 'tp')), parts along dimension 0
- output 3: float32 [16384], P('dp'), parts along dimension 0
- output 4: float32 [512], P('dp'), parts along dimension 0
- output 5: float32 [512], P('dp'), parts along dimension 0
- output 6: float32 [16384, 8192], P('dp', 'tp'), parts along dimension 0
- output 7: float32 [16384, 512], P('dp', 'tp'), parts along dimension 0
- output 8: float32 [16384, 512], P('dp', 'tp'), parts along dimension 0
- output 9: float32 [32768, 4096], P(('dp', 'tp')), parts along dimension 0
There are 4 independent parts. A program takes and returns all parts, laid end to end along the dimension named above; an argument that names none is the same for every part.
All inputs are finite; a program needn't handle non-finite values.
Results may differ from a plain program's by a relative error of at most 0.02.
Values are sent between devices in bfloat16 or wider.
A program may use at most 768 MiB of HBM per device.

v0:
```python
import functools
import jax
import jax.numpy as jnp
from jax import lax
from jax.sharding import PartitionSpec as P

EPS = 1.0e-6
ROPE_BASE = 1.0e6
NEG_BIG = -1.0e30


def rope_tables(seq_len, head_dim):
    half_dim = head_dim // 2
    inv_freq = ROPE_BASE ** (-2.0 * jnp.arange(half_dim, dtype=jnp.float32) / head_dim)
    angles = jnp.arange(seq_len, dtype=jnp.float32)[:, None] * inv_freq[None, :]
    angles = jnp.concatenate([angles, angles], axis=-1)
    return jnp.cos(angles), jnp.sin(angles)


def rms_scale(wide_in, gain_vec):
    return wide_in * lax.rsqrt(jnp.mean(wide_in * wide_in, axis=-1, keepdims=True) + EPS) * gain_vec


def norm_rope(raw_heads, gain_vec, cos_tab, sin_tab):
    normed = rms_scale(raw_heads.astype(jnp.float32), gain_vec)
    half_dim = normed.shape[-1] // 2
    rotated = jnp.concatenate([-normed[..., half_dim:], normed[..., :half_dim]], axis=-1)
    return normed * cos_tab[:, None, :] + rotated * sin_tab[:, None, :]


def attention_core(q_five, k_rot, v_four):
    seq_len = q_five.shape[1]
    scores = jnp.einsum('bqkgh,bskh->bkgqs', q_five, k_rot, preferred_element_type=jnp.float32) * q_five.shape[-1] ** -0.5
    causal = jnp.arange(seq_len)[:, None] >= jnp.arange(seq_len)[None, :]
    attn_prob = jax.nn.softmax(jnp.where(causal, scores, NEG_BIG), axis=-1)
    prob_bf = attn_prob.astype(jnp.bfloat16)
    attn_out = jnp.einsum('bkgqs,bskh->bqkgh', prob_bf, v_four, preferred_element_type=jnp.float32).astype(jnp.bfloat16)
    return attn_prob, prob_bf, attn_out


def attention_grad(attn_prob, prob_bf, q_five, k_rot, v_four, grad_five):
    attn_scale = q_five.shape[-1] ** -0.5
    grad_prob = jnp.einsum('bqkgh,bskh->bkgqs', grad_five, v_four, preferred_element_type=jnp.float32)
    grad_values = jnp.einsum('bkgqs,bqkgh->bskh', prob_bf, grad_five, preferred_element_type=jnp.float32).astype(jnp.bfloat16)
    grad_scores = (attn_prob * (grad_prob - jnp.sum(attn_prob * grad_prob, axis=-1, keepdims=True)) * attn_scale).astype(jnp.bfloat16)
    grad_q_rot = jnp.einsum('bkgqs,bskh->bqkgh', grad_scores, k_rot, preferred_element_type=jnp.float32)
    grad_k_rot = jnp.einsum('bkgqs,bqkgh->bskh', grad_scores, q_five, preferred_element_type=jnp.float32)
    return grad_q_rot, grad_k_rot, grad_values


def attention_block(x_loc, grad_y_loc, norm_gain, q_gain, k_gain, wq_loc, wk_loc, wv_loc, wo_loc, tp_size):
    my_rank = lax.axis_index('tp')
    batch_rows, seq_dev, d_model = x_loc.shape
    seq_len = seq_dev * tp_size
    head_dim = q_gain.shape[0]
    q_local = wq_loc.shape[1] // head_dim
    kv_total = wk_loc.shape[1] * tp_size // head_dim
    kv_local = max(kv_total // tp_size, 1)
    group_size = q_local // kv_local
    x_wide = x_loc.astype(jnp.float32)
    h_wide, norm_pull = jax.vjp(rms_scale, x_wide, norm_gain)
    hidden = lax.all_gather(h_wide.astype(jnp.bfloat16), 'tp', axis=1, tiled=True)
    if kv_total < tp_size:
        kv_index = my_rank // (tp_size // kv_total)
        wk_head = lax.dynamic_slice_in_dim(lax.all_gather(wk_loc, 'tp', axis=1, tiled=True), kv_index * head_dim, head_dim, axis=1)
        wv_head = lax.dynamic_slice_in_dim(lax.all_gather(wv_loc, 'tp', axis=1, tiled=True), kv_index * head_dim, head_dim, axis=1)
    else:
        wk_head = wk_loc
        wv_head = wv_loc
    queries = jnp.einsum('bsd,dn->bsn', hidden, wq_loc, preferred_element_type=jnp.float32).astype(jnp.bfloat16)
    keys_raw = jnp.einsum('bsd,dn->bsn', hidden, wk_head, preferred_element_type=jnp.float32).astype(jnp.bfloat16)
    values = jnp.einsum('bsd,dn->bsn', hidden, wv_head, preferred_element_type=jnp.float32).astype(jnp.bfloat16)
    cos_tab, sin_tab = rope_tables(seq_len, head_dim)
    rope_fn = functools.partial(norm_rope, cos_tab=cos_tab, sin_tab=sin_tab)
    q_wide, q_pull = jax.vjp(rope_fn, queries.reshape(batch_rows, seq_len, q_local, head_dim), q_gain)
    k_wide, k_pull = jax.vjp(rope_fn, keys_raw.reshape(batch_rows, seq_len, kv_local, head_dim), k_gain)
    q_five = q_wide.astype(jnp.bfloat16).reshape(batch_rows, seq_len, kv_local, group_size, head_dim)
    k_rot = k_wide.astype(jnp.bfloat16)
    v_four = values.reshape(batch_rows, seq_len, kv_local, head_dim)
    attn_prob, prob_bf, attn_out = attention_core(q_five, k_rot, v_four)
    attn_flat = attn_out.reshape(batch_rows, seq_len, q_local * head_dim)
    out_part = jnp.einsum('bsn,nd->bsd', attn_flat, wo_loc, preferred_element_type=jnp.float32).astype(jnp.bfloat16)
    attn_sum = lax.psum_scatter(out_part, 'tp', scatter_dimension=1, tiled=True)
    y_loc = (x_wide + attn_sum.astype(jnp.float32)).astype(jnp.bfloat16)
    grad_y_full = lax.all_gather(grad_y_loc, 'tp', axis=1, tiled=True)
    grad_w_out = jnp.einsum('bsn,bsd->nd', attn_flat, grad_y_full, preferred_element_type=jnp.float32)
    grad_attn = jnp.einsum('bsd,nd->bsn', grad_y_full, wo_loc, preferred_element_type=jnp.float32).astype(jnp.bfloat16)
    grad_five = grad_attn.reshape(batch_rows, seq_len, kv_local, group_size, head_dim)
    grad_q_rot, grad_k_rot, grad_values = attention_grad(attn_prob, prob_bf, q_five, k_rot, v_four, grad_five)
    grad_q_raw, grad_q_gain = q_pull(grad_q_rot.astype(jnp.bfloat16).astype(jnp.float32).reshape(batch_rows, seq_len, q_local, head_dim))
    grad_k_raw, grad_k_gain = k_pull(grad_k_rot.astype(jnp.bfloat16).astype(jnp.float32))
    grad_q_flat = grad_q_raw.reshape(batch_rows, seq_len, q_local * head_dim)
    grad_k_flat = grad_k_raw.reshape(batch_rows, seq_len, kv_local * head_dim)
    grad_v_flat = grad_values.reshape(batch_rows, seq_len, kv_local * head_dim)
    grad_w_query = jnp.einsum('bsd,bsn->dn', hidden, grad_q_flat, preferred_element_type=jnp.float32)
    grad_wk_head = jnp.einsum('bsd,bsn->dn', hidden, grad_k_flat, preferred_element_type=jnp.float32)
    grad_wv_head = jnp.einsum('bsd,bsn->dn', hidden, grad_v_flat, preferred_element_type=jnp.float32)
    if kv_total < tp_size:
        zero_cols = jnp.zeros((d_model, kv_total * head_dim), jnp.float32)
        grad_w_key = lax.psum_scatter(lax.dynamic_update_slice_in_dim(zero_cols, grad_wk_head, kv_index * head_dim, axis=1), 'tp', scatter_dimension=1, tiled=True)
        grad_w_value = lax.psum_scatter(lax.dynamic_update_slice_in_dim(zero_cols, grad_wv_head, kv_index * head_dim, axis=1), 'tp', scatter_dimension=1, tiled=True)
    else:
        grad_w_key = grad_wk_head
        grad_w_value = grad_wv_head
    grad_hidden_part = (jnp.einsum('bsn,dn->bsd', grad_q_flat, wq_loc, preferred_element_type=jnp.float32) + jnp.einsum('bsn,dn->bsd', grad_k_flat, wk_head, preferred_element_type=jnp.float32) + jnp.einsum('bsn,dn->bsd', grad_v_flat, wv_head, preferred_element_type=jnp.float32)).astype(jnp.bfloat16)
    grad_hidden = lax.psum_scatter(grad_hidden_part, 'tp', scatter_dimension=1, tiled=True)
    grad_x_norm, grad_gain_part = norm_pull(grad_hidden.astype(jnp.float32))
    grad_x = (grad_y_loc.astype(jnp.float32) + grad_x_norm).astype(jnp.bfloat16)
    grad_norm_gain = lax.psum(grad_gain_part, 'tp')
    grad_q_gain = lax.psum(grad_q_gain, 'tp')
    grad_k_gain = lax.psum(grad_k_gain, 'tp')
    return y_loc, grad_x, (grad_norm_gain, grad_q_gain, grad_k_gain, grad_w_query, grad_w_key, grad_w_value, grad_w_out)


def solution(mesh):
    tp_size = mesh.shape['tp']

    def local_step(tok_ids, embed_loc, norm_gain, q_gain, k_gain, wq_loc, wk_loc, wv_loc, wo_loc, grad_y_loc):
        my_rank = lax.axis_index('tp')
        vocab_rows, d_model = embed_loc.shape
        local_ids = tok_ids - my_rank * vocab_rows
        in_range = (local_ids >= 0) & (local_ids < vocab_rows)
        looked_up = jnp.take(embed_loc, jnp.clip(local_ids, 0, vocab_rows - 1), axis=0)
        x_part = jnp.where(in_range[:, :, None], looked_up, jnp.zeros((), embed_loc.dtype))
        x_loc = lax.psum_scatter(x_part, 'tp', scatter_dimension=1, tiled=True)
        y_loc, grad_x, weight_grads = attention_block(x_loc, grad_y_loc, norm_gain, q_gain, k_gain, wq_loc, wk_loc, wv_loc, wo_loc, tp_size)
        grad_x_full = lax.all_gather(grad_x, 'tp', axis=1, tiled=True)
        seg_ids = jnp.where(in_range, local_ids, vocab_rows).reshape(-1)
        grad_embed = jax.ops.segment_sum(grad_x_full.reshape(-1, d_model).astype(jnp.float32), seg_ids, num_segments=vocab_rows)
        return (y_loc, grad_embed) + weight_grads

    in_specs = (P('dp', None), P('tp', None), P(), P(), P(), P(None, 'tp'), P(None, 'tp'), P(None, 'tp'), P('tp', None), P('dp', 'tp', None))
    out_specs = (P('dp', 'tp', None), P(('dp', 'tp'), None), P('dp'), P('dp'), P('dp'), P('dp', 'tp'), P('dp', 'tp'), P('dp', 'tp'), P(('dp', 'tp'), None))
    return jax.shard_map(local_step, mesh=mesh, in_specs=in_specs, out_specs=out_specs, check_vma=False)
```

profile of v0, /device:TPU:21, one launch (start us, length us, event | category | flops | bytes accessed | tf_op | source)
XLA Modules:
  0.0 961.0 jit_solution(10766656544763931242)
XLA Ops:
  7.3 0.8 compare_and_fusion.1
  8.1 1.3 select_bitcast_fusion
  9.4 14.3 %gather_fusion = bf16[2048,4096]{1,0:T(8,128)(2,1)} fusion(bf16[128,4096]{1,0:T(8,128)(2,1)S(1)} %copy-done, s32[2048]{0:T(1024)S(1)} %broadcast_clamp_fusion), kind=kCustom, calls=%fused_computation | custom fusion | bytes 33562624 | tf_op jit(solution)/shard_map/jit(_take)/gather | solution.py:123
  23.7 14.4 %select_select_fusion = bf16[4,512,4096]{2,1,0:T(8,128)(2,1)} fusion(bf16[4,512,4096]{2,1,0:T(8,128)(2,1)} %bitcast.244, pred[4,512]{1,0:T(4,128)(4,1)S(1)} %get-tuple-element.34, pred[4,512]{1,0:T(4,128)(4,1)S(1)} %get-tuple-element.33), kind=kLoop, calls=%fused_computation.13 | loop fusion | flops 16777216 | bytes 33558528 | tf_op jit(solution)/shard_map/jit(_where)/select_n | solution.py:124
  38.2 0.7 all-gather.12.cloned.1.call-update
  39.0 0.7 all-gather.10.cloned.1.call-update
  39.8 99.8 %reduce-scatter.6.cloned.1.call-done = bf16[4,32,4096]{2,1,0:T(8,128)(2,1)} async-done(((bf16[4,512,4096]{2,1,0:T(8,128)(2,1)}), bf16[4,32,4096]{2,1,0:T(8,128)(2,1)}) %reduce-scatter.6.cloned.1.call-update) | async-done | bytes 1048592 | tf_op jit(solution)/shard_map/reduce_scatter | solution.py:125
  139.6 1.5 fusion.40
  141.2 2.5 fusion.36
  143.8 0.6 all-gather.8.cloned.1.call-update
  144.5 0.1 iota_compare_fusion
  144.6 0.1 iota_multiply_fusion
  144.7 1.0 fusion.93
  145.7 87.3 %all-gather.12.cloned.1.call-done = bf16[4,512,4096]{2,1,0:T(8,128)(2,1)} async-done(((bf16[4,32,4096]{2,1,0:T(8,128)(2,1)}), bf16[4,512,4096]{2,1,0:T(8,128)(2,1)}) %all-gather.12.cloned.1.call-update) | async-done | bytes 16777232 | tf_op jit(solution)/shard_map/all_gather | solution.py:85
  233.0 13.7 %fusion.49 = bf16[4,512,512]{1,2,0:T(8,128)(2,1)S(1)} fusion(bf16[4,512,4096]{2,1,0:T(8,128)(2,1)} %all-gather.12.cloned.1.call-done, bf16[512,4096]{1,0:T(8,128)(2,1)} %param.18), kind=kOutput, calls=%fused_computation.77 | convolution fusion | flops 8590983168 | bytes 23068672 | tf_op jit(solution)/shard_map/bsd,nd->bsn/dot_general | solution.py:87
  246.7 25.2 %all-gather.10.cloned.1.call-done = bf16[4096,512]{0,1:T(8,128)(2,1)} async-done(((bf16[4096,32]{0,1:T(8,128)(2,1)}), bf16[4096,512]{0,1:T(8,128)(2,1)}) %all-gather.10.cloned.1.call-update) | async-done | bytes 4194320 | tf_op jit(solution)/shard_map/all_gather | solution.py:65
  271.9 92.3 %all-gather.6.cloned.1.call-done = bf16[4,512,4096]{2,1,0:T(8,128)(2,1)} async-done(((bf16[4,32,4096]{2,1,0:T(8,128)(2,1)}), bf16[4,512,4096]{2,1,0:T(8,128)(2,1)}) %all-gather.6.cloned.1.call-update) | async-done | bytes 16777232 | tf_op jit(solution)/shard_map/all_gather | solution.py:62
  364.2 11.6 %fusion.75 = (f32[4,512]{1,0:T(4,128)S(1)}, bf16[4,512,128]{1,2,0:T(8,128)(2,1)S(1)}) fusion(bf16[4,512,4096]{2,1,0:T(8,128)(2,1)} %all-gather.6.cloned.1.call-done, bf16[4096,512]{0,1:T(8,128)(2,1)} %all-gather.10.cloned.1.call-done, s32[]{:T(128)S(6)} %select_n.36), kind=kOutput, calls=%fused_computation.103 | convolution fusion | flops 2148530176 | bytes 18358276 | tf_op jit(solution)/shard_map/bsd,dn->bsn/dot_general | solution.py:71
  375.8 14.2 %fusion.21 = (f32[4,512,4]{1,2,0:T(4,128)S(1)}, bf16[4,512,512]{1,2,0:T(8,128)(2,1)S(1)}) fusion(bf16[4,512,4096]{2,1,0:T(8,128)(2,1)} %all-gather.6.cloned.1.call-done, bf16[4096,512]{1,0:T(8,128)(2,1)} %param.15), kind=kOutput, calls=%fused_computation.39 | convolution fusion | flops 8594120704 | bytes 23101440 | tf_op jit(solution)/shard_map/bsd,dn->bsn/dot_general | solution.py:70
  390.1 0.2 fusion.68
  390.3 0.1 fusion.91
  390.4 0.3 fusion.90
  390.8 0.7 fusion.16
  391.5 0.5 slice_negate_fusion.1
  392.0 1.2 fusion.24
  393.3 7.5 fusion.8
  400.8 9.2 fusion.7
  410.0 9.2 fusion.62
  419.2 11.5 %fusion.61 = bf16[4,512,128,1]{2,1,3,0:T(8,128)(2,1)} fusion(bf16[4,512,4096]{2,1,0:T(8,128)(2,1)} %all-gather.6.cloned.1.call-done, bf16[4096,512]{0,1:T(8,128)(2,1)} %all-gather.8.cloned.1.call-done, s32[]{:T(128)S(6)} %select_n.36), kind=kOutput, calls=%fused_computation.91 | convolution fusion | flops 2147745792 | bytes 18350084 | tf_op jit(solution)/shard_map/bsd,dn->bsn/dot_general | solution.py:72
  430.7 10.4 %fusion.2 = (f32[4,4,512]{2,1,0:T(4,128)S(1)}, f32[4,512,512,4]{2,1,3,0:T(8,128)}) fusion(f32[4,4,512]{2,1,0:T(4,128)S(1)} %fusion.7, f32[4,4,512]{2,1,0:T(4,128)S(1)} %get-tuple-element.39, f32[4,512,512,4]{2,1,3,0:T(8,128)S(1)} %copy-done.2, pred[512,512]{0,1:T(8,128)(4,1)S(1)} %iota_compare_fusion, bf16[4,512,128,1]{2,1,3,0:T(8,128)(2,1)} %fusion.61, ...), kind=kOutput, calls=%fused_computation.8 | convolution fusion | flops 1098899456 | bytes 36536320 | tf_op jit(solution)/shard_map/bqkgh,bskh->bkgqs/dot_general | solution.py:43
  441.1 11.9 %fusion.9 = bf16[4,4,512,512]{2,3,1,0:T(8,128)(2,1)} fusion(f32[4,512,512,4]{2,1,3,0:T(8,128)} %get-tuple-element.42, f32[4,4,512]{2,1,0:T(4,128)S(1)} %get-tuple-element.41, f32[4,4,512]{2,1,0:T(4,128)S(1)} %fusion.7, f32[4,4,512]{2,1,0:T(4,128)S(1)} %get-tuple-element.39, f32[4,512,512,4]{2,1,3,0:T(8,128)S(1)} %copy-done.2, ...), kind=kLoop, calls=%fused_computation.18 | loop fusion | flops 33554432 | bytes 42303488 | tf_op jit(solution)/shard_map/reshape.37
  453.0 7.0 broadcast_multiply_fusion
  460.0 1.5 bitcast_multiply_fusion.1
  461.5 0.1 fusion.105
  461.6 1.0 fusion.73
  462.6 0.8 fusion.104
  463.4 0.8 copy-done.5
  464.2 1.8 fusion.19
  466.0 1.6 fusion.20
  467.7 18.3 %fusion.30 = f32[4,512,4096]{2,1,0:T(8,128)} fusion(bf16[4,512,512]{1,2,0:T(8,128)(2,1)S(1)} %bitcast.247, bf16[4096,512]{1,0:T(8,128)(2,1)} %param.15), kind=kOutput, calls=%fused_computation.51 | convolution fusion | flops 8589934592 | bytes 39845888 | tf_op jit(solution)/shard_map/bsn,dn->bsd/dot_general | solution.py:105
  486.0 0.3 fusion.89
  486.3 14.4 %fusion.81 = f32[4,512,4096]{2,1,0:T(8,128)} fusion(bf16[4,512,128]{1,2,0:T(8,128)(2,1)S(1)} %fusion.89, bf16[4096,512]{0,1:T(8,128)(2,1)} %all-gather.10.cloned.1.call-done, s32[]{:T(128)S(6)} %select_n.36), kind=kOutput, calls=%fused_computation.110 | convolution fusion | flops 2147483648 | bytes 35127300 | tf_op jit(solution)/shard_map/bsn,dn->bsd/dot_general | solution.py:105
  500.7 28.4 %add_convert_fusion = bf16[4,512,4096]{2,1,0:T(8,128)(2,1)} fusion(f32[4,512,4096]{2,1,0:T(8,128)} %fusion.30, f32[4,512,4096]{2,1,0:T(8,128)} %fusion.81, bf16[4,512,128]{1,2,0:T(8,128)(2,1)S(1)} %copy-done.13, bf16[4096,512]{0,1:T(8,128)(2,1)} %all-gather.8.cloned.1.call-done, s32[]{:T(128)S(6)} %select_n.36), kind=kOutput, calls=%fused_computation.4 | convolution fusion | flops 2172649472 | bytes 85458944 | tf_op jit(solution)/shard_map/bsn,dn->bsd/dot_general | solution.py:105
  529.3 0.9 copy-done.30
  530.2 9.0 fusion.43
  539.2 1.3 copy-done.27
  540.5 12.5 %convolution_convert_fusion = bf16[4,512,4096]{2,1,0:T(8,128)(2,1)} fusion(bf16[4,512,512]{1,2,0:T(8,128)(2,1)S(1)} %bitcast.251, bf16[512,4096]{1,0:T(8,128)(2,1)S(1)} %copy-done.26), kind=kOutput, calls=%fused_computation.17 | convolution fusion | flops 8598323200 | bytes 23068672 | tf_op jit(solution)/shard_map/bsn,nd->bsd/dot_general | solution.py:82
  553.2 70.9 %reduce-scatter.10.cloned.1.call-done = bf16[4,32,4096]{2,1,0:T(8,128)(2,1)} async-done(((bf16[4,512,4096]{2,1,0:T(8,128)(2,1)}), bf16[4,32,4096]{2,1,0:T(8,128)(2,1)}) %reduce-scatter.10.cloned.1.call-update) | async-done | bytes 1048592 | tf_op jit(solution)/shard_map/reduce_scatter | solution.py:106
  624.2 2.1 fusion.37
  626.3 96.2 %reduce-scatter.8.cloned.1.call-done = bf16[4,32,4096]{2,1,0:T(8,128)(2,1)} async-done(((bf16[4,512,4096]{2,1,0:T(8,128)(2,1)}), bf16[4,32,4096]{2,1,0:T(8,128)(2,1)}) %reduce-scatter.8.cloned.1.call-update) | async-done | bytes 1048592 | tf_op jit(solution)/shard_map/reduce_scatter | solution.py:83
  722.5 3.9 fusion.39
  726.5 4.3 broadcast_in_dim.79.clone.1
  730.8 9.5 fusion.17
  740.4 0.3 reduce-scatter.12.cloned.1.call-start
  740.6 4.3 broadcast_in_dim.79.clone
  744.9 9.4 fusion.18
  754.4 0.6 copy-done.18
  755.1 0.9 copy-done.28
  756.0 14.5 %convolution_bitcast_fusion = f32[512,4096]{1,0:T(8,128)} fusion(bf16[4,512,512]{1,2,0:T(8,128)(2,1)S(1)} %bitcast.252, bf16[4,512,4096]{2,1,0:T(8,128)(2,1)} %all-gather.12.cloned.1.call-done), kind=kOutput, calls=%fused_computation.27 | convolution fusion | flops 8589934592 | bytes 27262976 | tf_op jit(solution)/shard_map/bsn,bsd->nd/dot_general | solution.py:86
  770.5 14.7 %convolution_bitcast_fusion.1 = f32[4096,512]{1,0:T(8,128)} fusion(bf16[4,512,4096]{2,1,0:T(8,128)(2,1)} %all-gather.6.cloned.1.call-done, bf16[4,512,512]{1,2,0:T(8,128)(2,1)S(1)} %bitcast.248), kind=kOutput, calls=%fused_computation.28 | convolution fusion | flops 8589934592 | bytes 27262976 | tf_op jit(solution)/shard_map/bsd,bsn->dn/dot_general | solution.py:95
  785.2 46.4 %all-reduce.4 = (f32[4096]{0:T(1024)}, f32[128]{0:T(128)}, f32[128]{0:T(128)}) all-reduce(f32[4096]{0:T(1024)S(1)} %get-tuple-element.11, f32[128]{0:T(128)S(1)} %get-tuple-element.9, f32[128]{0:T(128)S(1)} %copy-done.25), channel_id=1, replica_groups=mesh['dp'=4,'tp'=16] {'tp'}, use_global_device_ids=true, to_apply=%region_14.15 | all-reduce | flops 4352 | bytes 34816 | tf_op jit(solution)/shard_map/psum | solution.py:109
  831.6 48.0 %scatter_custom_fusion = f32[128,4096]{1,0:T(8,128)} fusion(s32[2048]{0:T(1024)S(1)} %bitcast.250, bf16[2048,4096]{1,0:T(8,128)(2,1)} %bitcast.246, f32[]{:T(128)} %constant.29.clone.1), kind=kCustom, calls=%fused_computation.2 | custom fusion | flops 16777216 | bytes 18874372 | tf_op jit(solution)/shard_map/scatter-add | solution.py:129
  879.6 4.9 reduce-scatter.14.cloned.1.call-done
  884.5 69.2 %reduce-scatter.12.cloned.1.call-done = f32[4096,32]{0,1:T(8,128)} async-done(((f32[4096,512]{0,1:T(8,128)}), f32[4096,32]{0,1:T(8,128)}) %reduce-scatter.12.cloned.1.call-update) | async-done | bytes 524304 | tf_op jit(solution)/shard_map/reduce_scatter | solution.py:100
  (85 shorter events, 1.2 us)
Async XLA Ops:
  7.2 2.2 copy-start
  7.2 132.4 %reduce-scatter.6.cloned.1.call-start = ((), (), s32[]{:S(2)}) async-start(), calls=%async_computation.5 | async-start | bytes 17825792 | tf_op jit(solution)/shard_map/reduce_scatter | solution.py:125
  38.1 103.1 %copy-start.16 = (f32[4096]{0:T(1024)S(1)}, f32[4096]{0:T(1024)}, u32[]{:S(2)}) copy-start(f32[4096]{0:T(1024)} %param.12) | copy-start | bytes 49156
  38.2 194.8 %all-gather.12.cloned.1.call-start = ((), (), s32[]{:S(2)}) async-start(), calls=%async_computation.10 | async-start | bytes 17825792 | tf_op jit(solution)/shard_map/all_gather | solution.py:85
  39.0 232.9 %all-gather.10.cloned.1.call-start = ((), (), s32[]{:S(2)}) async-start(), calls=%async_computation.8 | async-start | bytes 4456448 | tf_op jit(solution)/shard_map/all_gather | solution.py:65
  39.8 324.4 %all-gather.6.cloned.1.call-start = ((), (), s32[]{:S(2)}) async-start(), calls=%async_computation.6 | async-start | bytes 17825792 | tf_op jit(solution)/shard_map/all_gather | solution.py:62
  141.1 3.5 copy-start.21
  141.2 3.5 copy-start.19
  143.7 275.5 %all-gather.8.cloned.1.call-start = ((), (), s32[]{:S(2)}) async-start(), calls=%async_computation.7 | async-start | bytes 4456448 | tf_op jit(solution)/shard_map/all_gather | solution.py:66
  144.4 479.8 %reduce-scatter.10.cloned.1.call-start = ((), (), s32[]{:S(2)}) async-start(), calls=%async_computation.11 | async-start | bytes 17825792 | tf_op jit(solution)/shard_map/reduce_scatter | solution.py:106
  246.7 163.3 %copy-start.29 = (bf16[4,512,512]{1,2,0:T(8,128)(2,1)}, bf16[4,512,512]{1,2,0:T(8,128)(2,1)S(1)}, u32[]{:S(2)}) copy-start(bf16[4,512,512]{1,2,0:T(8,128)(2,1)S(1)} %fusion.49) | copy-start | bytes 6291460
  375.8 14.6 %copy-start.8 = (bf16[4,512,128]{1,2,0:T(8,128)(2,1)}, bf16[4,512,128]{1,2,0:T(8,128)(2,1)S(1)}, u32[]{:S(2)}) copy-start(bf16[4,512,128]{1,2,0:T(8,128)(2,1)S(1)} %get-tuple-element.38) | copy-start | bytes 1572868
  375.8 14.3 %copy-start.24 = (f32[128]{0:T(128)S(1)}, f32[128]{0:T(128)}, u32[]{:S(2)}) copy-start(f32[128]{0:T(128)} %param.14) | copy-start | bytes 1540
  390.1 2.0 copy-start.4
  390.1 0.7 copy-start.23
  390.8 2.5 copy-start.10
  393.2 7.6 copy-start.6
  419.2 11.5 %copy-start.2 = (f32[4,512,512,4]{2,1,3,0:T(8,128)S(1)}, f32[4,512,512,4]{2,1,3,0:T(8,128)}, u32[]{:S(2)}) copy-start(f32[4,512,512,4]{2,1,3,0:T(8,128)} %get-tuple-element.40) | copy-start | bytes 50331652
  453.0 7.0 copy-start.3
  453.0 7.0 copy-start.11
  460.0 1.6 copy-start.9
  462.6 1.6 copy-start.5
  467.6 18.3 %copy-start.14 = (bf16[4,512,4,128]{1,3,2,0:T(8,128)(2,1)}, bf16[4,512,4,128]{1,3,2,0:T(8,128)(2,1)S(1)}, u32[]{:S(2)}) copy-start(bf16[4,512,4,128]{1,3,2,0:T(8,128)(2,1)S(1)} %fusion.20) | copy-start | bytes 6291460
  486.3 14.4 %copy-start.13 = (bf16[4,512,128]{1,2,0:T(8,128)(2,1)S(1)}, bf16[4,512,128]{1,2,0:T(8,128)(2,1)}, u32[]{:S(2)}) copy-start(bf16[4,512,128]{1,2,0:T(8,128)(2,1)} %fusion.62) | copy-start | bytes 1572868
  529.1 1.0 copy-start.30
  529.2 193.3 %reduce-scatter.8.cloned.1.call-start = ((), (), s32[]{:S(2)}) async-start(), calls=%async_computation.9 | async-start | bytes 17825792 | tf_op jit(solution)/shard_map/reduce_scatter | solution.py:83
  530.2 10.4 %copy-start.26 = (bf16[512,4096]{1,0:T(8,128)(2,1)S(1)}, bf16[512,4096]{1,0:T(8,128)(2,1)}, u32[]{:S(2)}) copy-start(bf16[512,4096]{1,0:T(8,128)(2,1)} %param.18) | copy-start | bytes 12582916
  539.2 1.3 copy-start.27
  553.1 71.1 %copy-start.7 = (bf16[4,32,4096]{2,1,0:T(8,128)(2,1)S(1)}, bf16[4,32,4096]{2,1,0:T(8,128)(2,1)}, u32[]{:S(2)}) copy-start(bf16[4,32,4096]{2,1,0:T(8,128)(2,1)} %reduce-scatter.6.cloned.1.call-done) | copy-start | bytes 3145732
  553.1 71.1 %copy-start.17 = (f32[4096]{0:T(1024)S(1)}, f32[4096]{0:T(1024)}, u32[]{:S(2)}) copy-start(f32[4096]{0:T(1024)} %param.12) | copy-start | bytes 49156
  553.1 71.1 %copy-start.20 = (f32[4,32]{1,0:T(4,128)S(1)}, f32[4,32]{1,0:T(4,128)}, u32[]{:S(2)}) copy-start(f32[4,32]{1,0:T(4,128)} %copy-done.19) | copy-start | bytes 1540
  553.1 73.2 %copy-start.22 = (f32[4,32]{1,0:T(4,128)S(1)}, f32[4,32]{1,0:T(4,128)}, u32[]{:S(2)}) copy-start(f32[4,32]{1,0:T(4,128)} %copy-done.21) | copy-start | bytes 1540
  553.1 169.4 %copy-start.12 = (bf16[4,32,4096]{2,1,0:T(8,128)(2,1)S(1)}, bf16[4,32,4096]{2,1,0:T(8,128)(2,1)}, u32[]{:S(2)}) copy-start(bf16[4,32,4096]{2,1,0:T(8,128)(2,1)} %param.19) | copy-start | bytes 3145732
  553.2 278.5 %all-gather.14.cloned.1.call-start = ((), (), s32[]{:S(2)}) async-start(), calls=%async_computation.12 | async-start | bytes 17825792 | tf_op jit(solution)/shard_map/all_gather | solution.py:127
  726.5 158.0 %reduce-scatter.14.cloned.1.call-start = ((), (), s32[]{:S(2)}) async-start(), calls=%async_computation.14 | async-start | bytes 8912896 | tf_op jit(solution)/shard_map/reduce_scatter | solution.py:101
  740.4 213.3 %reduce-scatter.12.cloned.1.call-start = ((), (), s32[]{:S(2)}) async-start(), calls=%async_computation.13 | async-start | bytes 8912896 | tf_op jit(solution)/shard_map/reduce_scatter | solution.py:100
  754.4 0.7 copy-start.18
  754.4 1.6 copy-start.28
  756.0 14.5 %copy-start.15 = (bf16[4,512,4,128]{1,3,2,0:T(8,128)(2,1)S(1)}, bf16[4,512,4,128]{1,3,2,0:T(8,128)(2,1)}, u32[]{:S(2)}) copy-start(bf16[4,512,4,128]{1,3,2,0:T(8,128)(2,1)} %copy-done.14) | copy-start | bytes 6291460
  770.5 14.7 %copy-start.25 = (f32[128]{0:T(128)S(1)}, f32[128]{0:T(128)}, u32[]{:S(2)}) copy-start(f32[128]{0:T(128)} %get-tuple-element.13) | copy-start | bytes 1540
  831.6 122.1 %copy-start.1 = (bf16[128,4096]{1,0:T(8,128)(2,1)S(1)}, bf16[128,4096]{1,0:T(8,128)(2,1)}, u32[]{:S(2)}) copy-start(bf16[128,4096]{1,0:T(8,128)(2,1)} %param.11) | copy-start | bytes 3145732
Sparse Core Ops, SparseCore 0:
  38.3 101.3 reduce-scatter.5
  141.3 91.6 all-gather.11
  234.6 37.1 all-gather.9
  273.9 90.1 all-gather.5
  365.6 37.1 all-gather.7
  529.3 94.8 reduce-scatter.9
  626.5 95.9 reduce-scatter.7
  726.6 92.0 all-gather.13
  821.6 62.8 reduce-scatter.13
  887.3 66.3 reduce-scatter.11
where the time goes:
time: 971 us; the launch traced here: 961 us
  waiting for transfers between devices  548 us (56%)
  matrix products  218 us (22%)
  other arithmetic  105 us (11%)
  blocking collectives  46.4 us (5%)
  local copies, waits for them, and re-layouts  27.5 us (3%)
  between operations  15.1 us (2%)
    reduce_scatter x1, waiting for transfers between devices, local_step(): x_loc = lax.psum_scatter(x_part, 'tp', scatter_dimension=1, tiled=True)  99.8 us
    reduce_scatter x1, waiting for transfers between devices, attention_block(): attn_sum = lax.psum_scatter(out_part, 'tp', scatter_dimension=1, tiled=True)  96.2 us
    all_gather x1, waiting for transfers between devices, attention_block(): lax.all_gather(h_wide.astype(jnp.bfloat16), 'tp', axis=1, tiled=True)  92.3 us
    all_gather x1, waiting for transfers between devices, attention_block(): grad_y_full = lax.all_gather(grad_y_loc, 'tp', axis=1, tiled=True)  87.3 us
    reduce_scatter x1, waiting for transfers between devices, attention_block(): lax.psum_scatter(grad_hidden_part, 'tp', scatter_dimension=1, tiled=True)  70.9 us
    reduce_scatter x1, waiting for transfers between devices, attention_block(): lax.psum_scatter(lax.dynamic_update_slice_in_dim(zero_cols, grad_wk_head,...  69.2 us
    scatter-add x1, other arithmetic, local_step(): jax.ops.segment_sum(grad_x_full.reshape(-1, d_model).astype(jnp.float32),...  48 us
    psum x1, blocking collectives, attention_block(): grad_norm_gain = lax.psum(grad_gain_part, 'tp')  46.4 us
  transfers between devices with their start and end apart: 10, of which 8 were waited for; matrix products, arithmetic and copies ran while one was open for 21% of the time, Pallas kernels for 0%

commit v1 on v0

v1 whole, which is shorter than its diff:
```python
import functools
import jax
import jax.numpy as jnp
from jax import lax
from jax.sharding import PartitionSpec as P

EPS = 1.0e-6
ROPE_BASE = 1.0e6
NEG_BIG = -1.0e30
BF = jnp.bfloat16
F32 = jnp.float32


def rope_tables(seq_len, head_dim):
    half_dim = head_dim // 2
    inv_freq = ROPE_BASE ** (-2.0 * jnp.arange(half_dim, dtype=F32) / head_dim)
    angles = jnp.arange(seq_len, dtype=F32)[:, None] * inv_freq[None, :]
    angles = jnp.concatenate([angles, angles], axis=-1)
    return jnp.cos(angles), jnp.sin(angles)


def rms_scale(wide_in, gain_vec):
    return wide_in * lax.rsqrt(jnp.mean(wide_in * wide_in, axis=-1, keepdims=True) + EPS) * gain_vec


def norm_rope(raw_heads, gain_vec, cos_tab, sin_tab):
    normed = rms_scale(raw_heads.astype(F32), gain_vec)
    half_dim = normed.shape[-1] // 2
    rotated = jnp.concatenate([-normed[..., half_dim:], normed[..., :half_dim]], axis=-1)
    return normed * cos_tab[:, None, :] + rotated * sin_tab[:, None, :]


def mm(spec, a, b):
    return jnp.einsum(spec, a, b, preferred_element_type=F32)


def attention_core(q_four, k_rot, v_three):
    seq_len = q_four.shape[1]
    scores = mm('bqgh,bsh->bgqs', q_four, k_rot) * q_four.shape[-1] ** -0.5
    causal = jnp.arange(seq_len)[:, None] >= jnp.arange(seq_len)[None, :]
    attn_prob = jax.nn.softmax(jnp.where(causal, scores, NEG_BIG), axis=-1)
    prob_bf = attn_prob.astype(BF)
    attn_out = mm('bgqs,bsh->bqgh', prob_bf, v_three).astype(BF)
    return attn_prob, prob_bf, attn_out


def attention_grad(attn_prob, prob_bf, q_four, k_rot, v_three, grad_four):
    attn_scale = q_four.shape[-1] ** -0.5
    grad_prob = mm('bqgh,bsh->bgqs', grad_four, v_three)
    grad_values = mm('bgqs,bqgh->bsh', prob_bf, grad_four).astype(BF)
    grad_scores = (attn_prob * (grad_prob - jnp.sum(attn_prob * grad_prob, axis=-1, keepdims=True)) * attn_scale).astype(BF)
    grad_q_rot = mm('bgqs,bsh->bqgh', grad_scores, k_rot)
    grad_k_rot = mm('bgqs,bqgh->bsh', grad_scores, q_four)
    return grad_q_rot, grad_k_rot, grad_values


def solution(mesh):
    tp = mesh.shape['tp']

    def local_step(tok_ids, embed_loc, norm_gain, q_gain, k_gain, wq, wk, wv, wo, gy_loc):
        rank = lax.axis_index('tp')
        vrows, d_model = embed_loc.shape
        batch, seq = tok_ids.shape
        seq_dev = seq // tp
        vocab = vrows * tp
        hd = q_gain.shape[0]
        qn = wq.shape[1]
        heads = qn // hd
        kn = wk.shape[1]
        share = hd // kn
        toks = batch * seq
        tok_flat = tok_ids.reshape(toks)

        table = lax.all_gather(embed_loc, 'tp', axis=0, tiled=True)
        gy_in = gy_loc
        gy_all = lax.all_gather(gy_in, 'tp', axis=0, tiled=False).reshape(toks, d_model)
        used = jnp.any(tok_flat[None, :] == jnp.arange(vocab, dtype=tok_ids.dtype)[:, None], axis=1)
        hidden = jnp.where(used[:, None], rms_scale(table.astype(F32), norm_gain), 0.0).astype(BF)
        w_all = jnp.concatenate([wq, wk, wv], axis=1)
        rows_all = mm('rd,dn->rn', hidden, w_all).astype(BF)
        onehot = (tok_flat[:, None] == jnp.arange(vocab, dtype=tok_ids.dtype)[None, :]).astype(BF)
        q_tok = mm('tr,rn->tn', onehot, rows_all[:, :qn]).astype(BF)
        kv_t = rows_all[:, qn:].T
        swap1 = [(i, i ^ 1) for i in range(tp)]
        swap2 = [(i, i ^ 2) for i in range(tp)]
        odd = (rank & 1) == 1
        far = (rank & 2) == 2
        kv_s = lax.ppermute(kv_t, 'tp', swap1)
        pair = jnp.where(odd, jnp.stack([kv_s, kv_t]), jnp.stack([kv_t, kv_s]))
        pair_o = lax.ppermute(pair, 'tp', swap2)
        quad = jnp.where(far, jnp.stack([pair_o, pair]), jnp.stack([pair, pair_o]))
        quad = quad.reshape(share, 2, kn, vocab).transpose(1, 0, 2, 3).reshape(2 * hd, vocab)
        kv_tok = mm('tr,nr->tn', onehot, quad).astype(BF)

        cos_tab, sin_tab = rope_tables(seq, hd)
        rope_fn = functools.partial(norm_rope, cos_tab=cos_tab, sin_tab=sin_tab)
        q_wide, q_pull = jax.vjp(rope_fn, q_tok.reshape(batch, seq, heads, hd), q_gain)
        k_wide, k_pull = jax.vjp(rope_fn, kv_tok[:, :hd].reshape(batch, seq, 1, hd), k_gain)
        q_four = q_wide.astype(BF)
        k_rot = k_wide.astype(BF)[:, :, 0]
        v_three = kv_tok[:, hd:].reshape(batch, seq, hd)
        attn_prob, prob_bf, attn_out = attention_core(q_four, k_rot, v_three)
        attn_dev = attn_out.reshape(batch, tp, seq_dev, qn).transpose(1, 0, 2, 3).reshape(toks, qn)

        out_part = mm('tn,nd->td', attn_dev, wo).astype(BF)
        attn_sum = lax.psum_scatter(out_part, 'tp', scatter_dimension=0, tiled=True)
        my_ids = lax.dynamic_slice_in_dim(tok_ids, rank * seq_dev, seq_dev, axis=1)
        x_mine = jnp.take(table, my_ids.reshape(-1), axis=0)
        y_loc = (x_mine.astype(F32) + attn_sum.astype(F32)).astype(BF).reshape(batch, seq_dev, d_model)

        gw_out = mm('tn,td->nd', attn_dev, gy_all)
        grad_attn = mm('td,nd->tn', gy_all, wo).astype(BF)
        grad_four = grad_attn.reshape(tp, batch, seq_dev, qn).transpose(1, 0, 2, 3).reshape(batch, seq, heads, hd)
        gq_rot, gk_rot, g_val = attention_grad(attn_prob, prob_bf, q_four, k_rot, v_three, grad_four)
        gq_raw, gq_gain = q_pull(gq_rot.astype(BF).astype(F32))
        gk_raw, gk_gain = k_pull(gk_rot.astype(BF).astype(F32)[:, :, None])
        gkv_tok = jnp.concatenate([gk_raw.reshape(toks, hd), g_val.reshape(toks, hd)], axis=1)
        gq_rows = mm('tr,tn->rn', onehot, gq_raw.reshape(toks, qn)).astype(BF)
        gkv_t = mm('tn,tr->nr', gkv_tok, onehot).reshape(2, share, kn, vocab).transpose(1, 0, 2, 3)
        gkv_t = gkv_t.reshape(2, 2, 2 * kn, vocab)
        mine1 = jnp.where(odd, gkv_t[:, 1], gkv_t[:, 0])
        send1 = jnp.where(odd, gkv_t[:, 0], gkv_t[:, 1]).astype(BF)
        half = mine1 + lax.ppermute(send1, 'tp', swap1).astype(F32)
        mine2 = jnp.where(far, half[1], half[0])
        send2 = jnp.where(far, half[0], half[1]).astype(BF)
        gkv_rows = (mine2 + lax.ppermute(send2, 'tp', swap2).astype(F32)).astype(BF).T
        g_rows = jnp.concatenate([gq_rows, gkv_rows], axis=1)
        gh_part = mm('rn,dn->rd', g_rows, w_all).astype(BF)
        gh = lax.psum_scatter(gh_part, 'tp', scatter_dimension=0, tiled=True)
        gw_query = mm('rd,rn->dn', hidden, gq_rows)
        gw_kv = mm('rd,rn->dn', hidden, gkv_rows)
        dev_ids = tok_ids.reshape(batch, tp, seq_dev).transpose(1, 0, 2).reshape(toks)
        my_rows = rank * vrows + jnp.arange(vrows, dtype=tok_ids.dtype)
        mine_hot = (my_rows[:, None] == dev_ids[None, :]).astype(BF)
        gy_rows = lax.optimization_barrier(mm('rt,td->rd', mine_hot, gy_all))
        _, norm_pull = jax.vjp(rms_scale, embed_loc.astype(F32), norm_gain)
        gx_norm, gn_gain = norm_pull(gh.astype(F32))
        g_embed = lax.optimization_barrier(gy_rows) + gx_norm
        gains = jnp.concatenate([gn_gain, gq_gain, gk_gain])
        gains = jnp.sum(lax.all_gather(gains, 'tp', axis=0, tiled=False), axis=0)
        return (y_loc, g_embed, gains[:d_model], gains[d_model:d_model + hd], gains[d_model + hd:], gw_query, gw_kv[:, :kn], gw_kv[:, kn:], gw_out)

    in_specs = (P('dp', None), P('tp', None), P(), P(), P(), P(None, 'tp'), P(None, 'tp'), P(None, 'tp'), P('tp', None), P('dp', 'tp', None))
    out_specs = (P('dp', 'tp', None), P(('dp', 'tp'), None), P('dp'), P('dp'), P('dp'), P('dp', 'tp'), P('dp', 'tp'), P('dp', 'tp'), P(('dp', 'tp'), None))
    return jax.shard_map(local_step, mesh=mesh, in_specs=in_specs, out_specs=out_specs, check_vma=False)
```

time: 971 us -> 523 us (0.54)
  waiting for transfers between devices: 548 us -> 152 us
  other arithmetic: 105 us -> 54.6 us
  local copies, waits for them, and re-layouts: 27.5 us -> 58.1 us
  blocking collectives: 46.4 us -> 17.5 us
    reduce_scatter x5 -> x2, waiting for transfers between devices: 341 us -> 37.2 us  [the longest x1 37.2 us: local_step(): gh = lax.psum_scatter(gh_part, 'tp', scatter_dimension=0, tiled=True)]
    all_gather x5 -> x2, waiting for transfers between devices: 205 us -> 90 us  [the longest x1 90 us: local_step(): table = lax.all_gather(embed_loc, 'tp', axis=0, tiled=True)]
    scatter-add x1 -> x0, other arithmetic: 48 us -> none  [local_step(): jax.ops.segment_sum(grad_x_full.reshape(-1, d_model).astype(jnp.float32),...]
    psum x1 -> x0, blocking collectives: 46.4 us -> none  [attention_block(): grad_norm_gain = lax.psum(grad_gain_part, 'tp')]
    ppermute x0 -> x4, waiting for transfers between devices: none -> 23.4 us  [the longest x1 21.1 us: local_step(): pair_o = lax.ppermute(pair, 'tp', swap2)]
    convert_element_type x0 -> x7, local copies, waits for them, and re-layouts: none -> 19.9 us  [the longest x6 15.6 us: norm_rope(): normed = rms_scale(raw_heads.astype(F32), gain_vec)]
    all_gather x0 -> x1, blocking collectives: none -> 17.5 us  [local_step(): gains = jnp.sum(lax.all_gather(gains, 'tp', axis=0, tiled=False), axis=0)]
    dot_general x18 -> x17, matrix products: 218 us -> 203 us  [mm(): return jnp.einsum(spec, a, b, preferred_element_type=F32)]
  transfers between devices with their start and end apart: 10 -> 8, of which waited for: 8 -> 4; matrix products, arithmetic and copies ran while one was open for 21% -> 61% of each run, Pallas kernels for 0% -> 0%
where the time goes in v1:
time: 523 us; the launch traced here: 514 us
  matrix products  214 us (41%)
  waiting for transfers between devices  152 us (29%)
  local copies, waits for them, and re-layouts  58.1 us (11%)
  other arithmetic  54.6 us (10%)
  blocking collectives  17.5 us (3%)
  between operations  14.9 us (3%)
    dot_general x17, matrix products, mm(): return jnp.einsum(spec, a, b, preferred_element_type=F32)  203 us
    all_gather x1, waiting for transfers between devices, local_step(): table = lax.all_gather(embed_loc, 'tp', axis=0, tiled=True)  90 us
    reduce_scatter x1, waiting for transfers between devices, local_step(): gh = lax.psum_scatter(gh_part, 'tp', scatter_dimension=0, tiled=True)  37.2 us
    ppermute x1, waiting for transfers between devices, local_step(): pair_o = lax.ppermute(pair, 'tp', swap2)  21.1 us
    all_gather x1, blocking collectives, local_step(): gains = jnp.sum(lax.all_gather(gains, 'tp', axis=0, tiled=False), axis=0)  17.5 us
    convert_element_type x6, local copies, waits for them, and re-layouts, norm_rope(): normed = rms_scale(raw_heads.astype(F32), gain_vec)  15.6 us
    reduce_sum x4, other arithmetic, rms_scale(): jnp.mean(wide_in * wide_in, axis=-1, keepdims=True) + EPS  12.6 us
    unnamed x68, local copies, waits for them, and re-layouts  11.4 us
  transfers between devices with their start and end apart: 8, of which 4 were waited for; matrix products, arithmetic and copies ran while one was open for 61% of the time, Pallas kernels for 0%

profile of v1, /device:TPU:21, one launch (start us, length us, event | category | flops | bytes accessed | tf_op | source)
XLA Modules:
  0.0 513.6 jit_solution(8221855831281760042)
XLA Ops:
  7.3 0.7 all-gather.6.cloned.1.call-update
  8.1 0.7 all-gather.8.cloned.1.call-update
  8.9 0.7 copy.230
  9.6 1.4 copy.184
  11.0 1.6 copy.185
  12.6 0.9 iota_compare_fusion.14
  13.6 1.0 fusion.89
  14.6 2.1 fusion.13
  16.7 90.0 %all-gather.6.cloned.1.call-done = bf16[2048,4096]{1,0:T(8,128)(2,1)} async-done(((bf16[128,4096]{1,0:T(8,128)(2,1)}), bf16[2048,4096]{1,0:T(8,128)(2,1)}) %all-gather.6.cloned.1.call-update) | async-done | bytes 16777232 | tf_op jit(solution)/shard_map/all_gather | solution.py:74
  106.7 7.5 %fusion.2 = f32[2048]{0:T(1024)S(1)} fusion(bf16[2048,4096]{1,0:T(8,128)(2,1)} %all-gather.6.cloned.1.call-done), kind=kLoop, calls=%fused_computation.5 | loop fusion | flops 25163776 | bytes 16785408 | tf_op jit(solution)/shard_map/reduce_sum | solution.py:23
  114.2 3.2 copy-done
  117.4 10.6 %fusion.5 = bf16[2048,4096]{1,0:T(8,128)(2,1)} fusion(bf16[2048,4096]{1,0:T(8,128)(2,1)S(1)} %copy-done, f32[4096]{0:T(1024)S(1)} %copy-done.19, f32[2048]{0:T(1024)S(1)} %add_rsqrt_fusion, pred[2048]{0:T(1024)(128)(4,1)S(1)} %fusion.13), kind=kLoop, calls=%fused_computation.8 | loop fusion | flops 41943040 | bytes 33581056 | tf_op jit(solution)/shard_map/convert_element_type | solution.py:78
  128.0 17.8 %convolution_convert_fusion.2 = bf16[2048,576]{0,1:T(8,128)(2,1)} fusion(bf16[2048,4096]{1,0:T(8,128)(2,1)} %fusion.5, bf16[4096,32]{1,0:T(8,128)(2,1)S(1)} %copy.185, bf16[4096,32]{1,0:T(8,128)(2,1)S(1)} %copy.184, bf16[4096,512]{1,0:T(8,128)(2,1)} %param.15), kind=kOutput, calls=%fused_computation.61 | convolution fusion | flops 9679011840 | bytes 23855104 | tf_op jit(solution)/shard_map/rd,dn->rn/dot_general | solution.py:34
  145.8 1.0 slice_bitcast_fusion.4
  147.4 7.7 %fusion.35 = f32[2048,512]{1,0:T(8,128)} fusion(s32[2048]{0:T(1024)S(1)} %bitcast.233, bf16[2048,576]{0,1:T(8,128)(2,1)} %convolution_convert_fusion.2), kind=kOutput, calls=%fused_computation.63 | convolution fusion | flops 4301258752 | bytes 6299648 | tf_op jit(solution)/shard_map/tr,rn->tn/dot_general | solution.py:34
  155.1 5.2 %reshape.380 = f32[4,512,4,128]{3,2,1,0:T(4,128)} reshape(f32[2048,512]{1,0:T(8,128)} %fusion.35) | data formatting | bytes 8388608 | tf_op jit(solution)/shard_map/jvp()/convert_element_type | solution.py:27
  160.3 5.2 %copy.190 = f32[4,512,4,128]{1,3,2,0:T(8,128)} copy(f32[4,512,4,128]{3,2,1,0:T(4,128)} %reshape.380) | data formatting | bytes 8388608 | tf_op jit(solution)/shard_map/jvp()/convert_element_type | solution.py:27
  165.5 4.5 multiply_reduce_fusion.2
  170.4 3.2 multiply_multiply_fusion
  173.6 0.8 slice_negate_fusion.1
  174.7 1.2 copy-done.1
  175.8 2.6 fusion.27
  178.5 21.1 %collective-permute-done.1 = bf16[2,64,2048]{2,1,0:T(8,128)(2,1)S(1)} collective-permute-done((bf16[2,64,2048]{2,1,0:T(8,128)(2,1)S(1)}, bf16[2,64,2048]{2,1,0:T(8,128)(2,1)S(1)}, u32[]{:S(2)}, u32[]{:S(2)}) %collective-permute-start.1) | collective-permute-done | bytes 524320 | tf_op jit(solution)/shard_map/ppermute | solution.py:90
  199.9 3.6 fusion.37
  203.9 0.9 slice_convert_fusion
  205.9 0.6 copy-done.6
  206.9 10.6 %fusion.107 = (f32[4,4,512]{2,1,0:T(4,128)S(1)}, f32[4,4,512,512]{2,3,1,0:T(8,128)}) fusion(pred[512,512]{0,1:T(8,128)(4,1)} %iota_compare_fusion.14, bf16[4,512,128,1]{1,2,3,0:T(8,128)(2,1)S(1)} %fusion.82, bf16[4,512,4,128]{1,3,2,0:T(8,128)(2,1)} %fusion.27), kind=kOutput, calls=%fused_computation.175 | convolution fusion | flops 1090519552 | bytes 19693568 | tf_op jit(solution)/shard_map/sub | solution.py:41
  217.6 8.6 %convert_bitcast_fusion = bf16[4,512,4,128]{1,3,2,0:T(8,128)(2,1)} fusion(bf16[4,512,128,1]{2,1,3,0:T(8,128)(2,1)S(1)} %bitcast.217, f32[4,4,512,512]{2,3,1,0:T(8,128)} %get-tuple-element.35, f32[4,4,512]{2,1,0:T(4,128)S(1)} %get-tuple-element.34), kind=kOutput, calls=%fused_computation.84 | convolution fusion | flops 1083179008 | bytes 19431424 | tf_op jit(solution)/shard_map/bgqs,bsh->bqgh/dot_general | solution.py:34
  226.1 4.2 copy.195
  230.4 4.1 reshape.366
  234.5 1.9 copy.196
  236.4 0.9 copy-done.25
  237.3 11.6 %convolution_convert_fusion.1 = bf16[2048,4096]{1,0:T(8,128)(2,1)} fusion(bf16[2048,512]{1,0:T(8,128)(2,1)S(1)} %bitcast.221, bf16[512,4096]{1,0:T(8,128)(2,1)S(1)} %copy-done.25), kind=kOutput, calls=%fused_computation.24 | convolution fusion | flops 8598323200 | bytes 23068672 | tf_op jit(solution)/shard_map/tn,nd->td/dot_general | solution.py:34
  249.1 13.8 %convolution_convert_fusion.3 = bf16[2048,512]{1,0:T(8,128)(2,1)S(1)} fusion(bf16[2048,4096]{1,0:T(8,128)(2,1)} %bitcast.207, bf16[512,4096]{1,0:T(8,128)(2,1)} %param.18), kind=kOutput, calls=%fused_computation.65 | convolution fusion | flops 8590983168 | bytes 23068672 | tf_op jit(solution)/shard_map/td,nd->tn/dot_general | solution.py:34
  262.9 1.6 copy.248
  264.5 4.0 reshape.372
  268.5 9.8 %fusion.53 = f32[4,512,512,4]{2,1,3,0:T(8,128)} fusion(bf16[4,512,128,1]{2,1,3,0:T(8,128)(2,1)S(1)} %bitcast.218, bf16[4,512,4,128]{3,2,1,0:T(4,128)(2,1)} %reshape.372), kind=kOutput, calls=%fused_computation.87 | convolution fusion | flops 1073741824 | bytes 19398656 | tf_op jit(solution)/shard_map/bqgh,bsh->bgqs/dot_general | solution.py:34
  278.2 23.1 %fusion.68 = bf16[4,512,128]{1,2,0:T(8,128)(2,1)S(1)} fusion(bf16[4,512,4,128]{1,3,2,0:T(8,128)(2,1)} %fusion.27, f32[4,512,512,4]{2,1,3,0:T(8,128)} %fusion.53, f32[4,4,512,512]{2,3,1,0:T(8,128)} %get-tuple-element.35, f32[4,4,512]{2,1,0:T(4,128)S(1)} %get-tuple-element.34), kind=kOutput, calls=%fused_computation.96 | convolution fusion | flops 1103372800 | bytes 36208640 | tf_op jit(solution)/shard_map/bgqs,bqgh->bsh/dot_general | solution.py:34
  302.7 8.7 %fusion.63 = bf16[4,512,128]{2,1,0:T(8,128)(2,1)S(1)} fusion(bf16[4,512,4,128]{3,2,1,0:T(4,128)(2,1)} %reshape.372, f32[4,4,512,512]{2,3,1,0:T(8,128)} %get-tuple-element.35, f32[4,4,512]{2,1,0:T(4,128)S(1)} %get-tuple-element.34), kind=kOutput, calls=%fused_computation.95 | convolution fusion | flops 1082392576 | bytes 19431424 | tf_op jit(solution)/shard_map/bgqs,bqgh->bsh/dot_general | solution.py:34
  311.4 3.7 fusion.9
  315.4 1.1 collective-permute-start.2
  316.5 25.1 %bitcast_multiply_fusion.6 = (f32[4,512,4,128]{1,3,2,0:T(8,128)}, bf16[4,128,4,512]{3,1,2,0:T(8,128)(2,1)}) fusion(f32[512,128]{0,1:T(8,128)S(1)} %copy-done.7, bf16[4,512,128,1]{1,2,3,0:T(8,128)(2,1)} %copy-done.16, f32[4,512,512,4]{2,1,3,0:T(8,128)} %fusion.53, f32[4,4,512,512]{2,3,1,0:T(8,128)} %get-tuple-element.35, f32[4,4,512]{2,1,0:T(4,128)S(1)} %get-tuple-element.34), kind=kOutput, calls=%fused_computation.44 | convolution fusion | flops 1106256384 | bytes 40665088 | tf_op jit(solution)/shard_map/bgqs,bsh->bqgh/dot_general | solution.py:34
  341.6 3.2 fusion.103
  345.1 0.7 copy-done.4
  345.7 1.9 multiply_reduce_fusion
  347.6 2.7 fusion.25
  350.3 4.2 copy.203
  354.6 1.4 bitcast_add_fusion
  356.3 5.5 %fusion.36 = bf16[2048,512]{0,1:T(8,128)(2,1)S(1)} fusion(s32[2048]{0:T(1024)S(1)} %bitcast.236, bf16[256,8,4,128]{3,2,1,0:T(4,128)(2,1)S(1)} %bitcast.219), kind=kOutput, calls=%fused_computation.64 | convolution fusion | flops 4300210176 | bytes 4202496 | tf_op jit(solution)/shard_map/tr,tn->rn/dot_general | solution.py:34
  361.8 2.3 collective-permute-done.3
  364.2 22.6 %convolution_convert_fusion = bf16[2048,4096]{1,0:T(8,128)(2,1)} fusion(bf16[2048,64]{0,1:T(8,128)(2,1)S(1)} %bitcast.223, bf16[2048,512]{0,1:T(8,128)(2,1)S(1)} %fusion.36, bf16[4096,32]{1,0:T(8,128)(2,1)S(1)} %copy-done.13, bf16[4096,32]{1,0:T(8,128)(2,1)S(1)} %copy-done.11, bf16[4096,512]{1,0:T(8,128)(2,1)} %param.15), kind=kOutput, calls=%fused_computation.23 | convolution fusion | flops 9690939392 | bytes 23855104 | tf_op jit(solution)/shard_map/rn,dn->rd/dot_general | solution.py:34
  386.9 0.6 copy-done.21
  388.4 8.1 %fusion.79 = f32[128,4096]{1,0:T(8,128)S(1)} fusion(bf16[2048,4096]{1,0:T(8,128)(2,1)} %bitcast.208, s32[2048]{0:T(1024)S(1)} %eq.59, s32[128]{0:T(128)S(1)} %iota_add_fusion), kind=kOutput, calls=%fused_computation.117 | convolution fusion | flops 2147745792 | bytes 18883072 | tf_op jit(solution)/shard_map/rt,td->rd/dot_general | solution.py:34
  396.5 11.1 %gather_fusion = bf16[128,4096]{1,0:T(8,128)(2,1)} fusion(bf16[2048,4096]{1,0:T(8,128)(2,1)} %all-gather.6.cloned.1.call-done, s32[1024]{0:T(1024)S(1)} %pad_clamp_fusion), kind=kCustom, calls=%fused_computation | custom fusion | bytes 2097664 | tf_op jit(solution)/shard_map/jit(_take)/gather | solution.py:108
  407.6 15.5 %convolution_bitcast_fusion = f32[512,4096]{1,0:T(8,128)} fusion(bf16[16,4,32,4096]{3,2,1,0:T(8,128)(2,1)} %bitcast.209, bf16[4,16,32,512]{3,2,1,0:T(8,128)(2,1)} %reshape.366), kind=kOutput, calls=%fused_computation.37 | convolution fusion | flops 8589934592 | bytes 27262976 | tf_op jit(solution)/shard_map/tn,td->nd/dot_general | solution.py:34
  423.2 15.0 %fusion.108 = f32[4096,512]{1,0:T(8,128)} fusion(bf16[2048,4096]{1,0:T(8,128)(2,1)} %fusion.5, bf16[2048,512]{0,1:T(8,128)(2,1)S(1)} %copy-done.27), kind=kOutput, calls=%fused_computation.176 | convolution fusion | flops 8589934592 | bytes 27262976 | tf_op jit(solution)/shard_map/rd,rn->dn/dot_general | solution.py:34
  438.3 3.1 fusion.109
  441.3 1.0 fusion.104
  442.4 2.9 add_convert_fusion
  445.3 37.2 %reduce-scatter.5.cloned.1.call-done = bf16[128,4096]{1,0:T(8,128)(2,1)} async-done(((bf16[2048,4096]{1,0:T(8,128)(2,1)}), bf16[128,4096]{1,0:T(8,128)(2,1)}) %reduce-scatter.5.cloned.1.call-update) | async-done | bytes 1048592 | tf_op jit(solution)/shard_map/reduce_scatter | solution.py:129
  482.5 2.1 fusion.42
  484.7 17.5 %all-gather.2 = f32[16,1,4352]{2,1,0:T(1,128)S(1)} all-gather(f32[1,1,4352]{2,1,0:T(1,128)S(1)} %reshape.392), channel_id=3, replica_groups=mesh['dp'=4,'tp'=16] {'tp'}, dimensions={0}, use_global_device_ids=true | all-gather | bytes 295936 | tf_op jit(solution)/shard_map/all_gather | solution.py:140
  502.9 0.6 slice.86
  503.5 3.1 fusion.43
  (118 shorter events, 7.7 us)
Async XLA Ops:
  7.2 99.5 %all-gather.6.cloned.1.call-start = ((), (), s32[]{:S(2)}) async-start(), calls=%async_computation.2 | async-start | bytes 17825792 | tf_op jit(solution)/shard_map/all_gather | solution.py:74
  8.0 241.1 %all-gather.8.cloned.1.call-start = ((), (), s32[]{:S(2)}) async-start(), calls=%async_computation.5 | async-start | bytes 17825792 | tf_op jit(solution)/shard_map/all_gather | solution.py:76
  8.8 433.6 %reduce-scatter.3.cloned.1.call-start = ((), (), s32[]{:S(2)}) async-start(), calls=%async_computation.3 | async-start | bytes 17825792 | tf_op jit(solution)/shard_map/reduce_scatter | solution.py:106
  11.0 117.0 %copy-start.10 = (bf16[4096,32]{1,0:T(8,128)(2,1)}, bf16[4096,32]{1,0:T(8,128)(2,1)S(1)}, u32[]{:S(2)}) copy-start(bf16[4096,32]{1,0:T(8,128)(2,1)S(1)} %copy.184) | copy-start | bytes 786436
  12.6 115.4 %copy-start.12 = (bf16[4096,32]{1,0:T(8,128)(2,1)}, bf16[4096,32]{1,0:T(8,128)(2,1)S(1)}, u32[]{:S(2)}) copy-start(bf16[4096,32]{1,0:T(8,128)(2,1)S(1)} %copy.185) | copy-start | bytes 786436
  14.6 160.0 %copy-start.5 = (f32[512,128]{0,1:T(8,128)}, f32[512,128]{0,1:T(8,128)S(1)}, u32[]{:S(2)}) copy-start(f32[512,128]{0,1:T(8,128)S(1)} %get-tuple-element.31) | copy-start | bytes 786436
  16.7 97.5 %copy-start.19 = (f32[4096]{0:T(1024)S(1)}, f32[4096]{0:T(1024)}, u32[]{:S(2)}) copy-start(f32[4096]{0:T(1024)} %param.12) | copy-start | bytes 49156
  106.7 10.7 %copy-start = (bf16[2048,4096]{1,0:T(8,128)(2,1)S(1)}, bf16[2048,4096]{1,0:T(8,128)(2,1)}, u32[]{:S(2)}) copy-start(bf16[2048,4096]{1,0:T(8,128)(2,1)} %all-gather.6.cloned.1.call-done) | copy-start | bytes 50331652
  146.8 27.6 %collective-permute-start = (bf16[64,2048]{1,0:T(8,128)(2,1)S(1)}, bf16[64,2048]{1,0:T(8,128)(2,1)S(1)}, u32[]{:S(2)}, u32[]{:S(2)}) collective-permute-start(bf16[64,2048]{1,0:T(8,128)(2,1)S(1)} %get-tuple-element.21), channel_id=1, source_target_pairs={{0,1},{1,0},{2,3},{3,2},{4,5},{5,4},{6,7},{7,6},{8,9},{9,8},{10,11... | collective-permute-start | bytes 786440 | tf_op jit(solution)/shard_map/ppermute | solution.py:88
  165.5 4.9 copy-start.22
  170.3 3.3 copy-start.17
  170.4 4.3 copy-start.14
  173.6 2.2 copy-start.1
  174.5 25.2 %collective-permute-start.1 = (bf16[2,64,2048]{2,1,0:T(8,128)(2,1)S(1)}, bf16[2,64,2048]{2,1,0:T(8,128)(2,1)S(1)}, u32[]{:S(2)}, u32[]{:S(2)}) collective-permute-start(bf16[2,64,2048]{2,1,0:T(8,128)(2,1)S(1)} %maximum_select_fusion.1), channel_id=1, source_target_pairs={{0,2},{1,3},{2,0},{3,1},{4,6},{5,7},{6,4},{7,5},{8,10},{9,11},{10,... | collective-permute-start | bytes 1572872 | tf_op jit(solution)/shard_map/ppermute | solution.py:90
  203.5 2.0 copy-start.24
  205.5 1.0 copy-start.6
  206.9 10.6 %copy-start.16 = (bf16[4,512,128,1]{1,2,3,0:T(8,128)(2,1)}, bf16[4,512,128,1]{1,2,3,0:T(8,128)(2,1)S(1)}, u32[]{:S(2)}) copy-start(bf16[4,512,128,1]{1,2,3,0:T(8,128)(2,1)S(1)} %fusion.82) | copy-start | bytes 1572868
  206.9 10.6 %copy-start.8 = (bf16[2048,128]{1,0:T(8,128)(2,1)S(1)}, bf16[2048,128]{1,0:T(8,128)(2,1)}, u32[]{:S(2)}) copy-start(bf16[2048,128]{1,0:T(8,128)(2,1)} %get-tuple-element.29) | copy-start | bytes 1572868
  234.5 2.8 copy-start.25
  249.0 233.6 %reduce-scatter.5.cloned.1.call-start = ((), (), s32[]{:S(2)}) async-start(), calls=%async_computation.4 | async-start | bytes 17825792 | tf_op jit(solution)/shard_map/reduce_scatter | solution.py:129
  278.2 23.1 %copy-start.7 = (f32[512,128]{0,1:T(8,128)S(1)}, f32[512,128]{0,1:T(8,128)}, u32[]{:S(2)}) copy-start(f32[512,128]{0,1:T(8,128)} %copy-done.5) | copy-start | bytes 786436
  315.4 39.2 %collective-permute-start.2 = (bf16[2,64,2048]{2,1,0:T(8,128)(2,1)S(1)}, bf16[2,64,2048]{2,1,0:T(8,128)(2,1)}, u32[]{:S(2)}, u32[]{:S(2)}) collective-permute-start(bf16[2,64,2048]{2,1,0:T(8,128)(2,1)S(1)} %fusion.81), channel_id=1, source_target_pairs={{0,1},{1,0},{2,3},{3,2},{4,5},{5,4},{6,7},{7,6},{8,9},{9,8},{10,11... | collective-permute-start | bytes 1572872 | tf_op jit(solution)/shard_map/ppermute | solution.py:123
  341.6 3.5 copy-start.2
  341.6 4.1 copy-start.4
  341.6 4.1 copy-start.15
  341.6 4.1 copy-start.23
  345.7 1.9 copy-start.18
  354.5 1.7 copy-start.9
  356.0 8.1 %collective-permute-start.3 = (bf16[64,2048]{1,0:T(8,128)(2,1)S(1)}, bf16[64,2048]{1,0:T(8,128)(2,1)S(1)}, u32[]{:S(2)}, u32[]{:S(2)}) collective-permute-start(bf16[64,2048]{1,0:T(8,128)(2,1)S(1)} %fusion.87), channel_id=1, source_target_pairs={{0,2},{1,3},{2,0},{3,1},{4,6},{5,7},{6,4},{7,5},{8,10},{9,11},{10,... | collective-permute-start | bytes 786440 | tf_op jit(solution)/shard_map/ppermute | solution.py:126
  356.3 7.9 %copy-start.11 = (bf16[4096,32]{1,0:T(8,128)(2,1)S(1)}, bf16[4096,32]{1,0:T(8,128)(2,1)}, u32[]{:S(2)}) copy-start(bf16[4096,32]{1,0:T(8,128)(2,1)} %copy-done.10) | copy-start | bytes 786436
  356.3 7.9 %copy-start.13 = (bf16[4096,32]{1,0:T(8,128)(2,1)S(1)}, bf16[4096,32]{1,0:T(8,128)(2,1)}, u32[]{:S(2)}) copy-start(bf16[4096,32]{1,0:T(8,128)(2,1)} %copy-done.12) | copy-start | bytes 786436
  361.8 25.0 %copy-start.26 = (bf16[2048,512]{0,1:T(8,128)(2,1)}, bf16[2048,512]{0,1:T(8,128)(2,1)S(1)}, u32[]{:S(2)}) copy-start(bf16[2048,512]{0,1:T(8,128)(2,1)S(1)} %fusion.36) | copy-start | bytes 6291460
  386.8 0.7 copy-start.21
  386.8 1.2 copy-start.3
  407.6 15.5 %copy-start.27 = (bf16[2048,512]{0,1:T(8,128)(2,1)S(1)}, bf16[2048,512]{0,1:T(8,128)(2,1)}, u32[]{:S(2)}) copy-start(bf16[2048,512]{0,1:T(8,128)(2,1)} %copy-done.26) | copy-start | bytes 6291460
  407.6 30.6 %slice-start = ((s8[16777216]{0:T(1024)(128)(4,1)}), s8[4194304]{0:T(1024)(128)(4,1)S(1)}, s32[]{:S(2)}) async-start(s8[16777216]{0:T(1024)(128)(4,1)} %bitcast.205), calls=%async_computation.6 | async-start | bytes 8388608
  407.6 30.6 %slice-start.1 = ((s8[16777216]{0:T(1024)(128)(4,1)}), s8[4194304]{0:T(1024)(128)(4,1)S(1)}, s32[]{:S(2)}) async-start(s8[16777216]{0:T(1024)(128)(4,1)} %bitcast.205), calls=%async_computation.7 | async-start | bytes 8388608
  423.2 15.1 %slice-start.2 = ((s8[16777216]{0:T(1024)(128)(4,1)}), s8[4194304]{0:T(1024)(128)(4,1)S(1)}, s32[]{:S(2)}) async-start(s8[16777216]{0:T(1024)(128)(4,1)} %bitcast.205), calls=%async_computation.8 | async-start | bytes 8388608
  423.2 15.1 %slice-start.3 = ((s8[16777216]{0:T(1024)(128)(4,1)}), s8[4194304]{0:T(1024)(128)(4,1)S(1)}, s32[]{:S(2)}) async-start(s8[16777216]{0:T(1024)(128)(4,1)} %bitcast.205), calls=%async_computation.9 | async-start | bytes 8388608
  441.3 41.2 %copy-start.20 = (f32[4096]{0:T(1024)S(1)}, f32[4096]{0:T(1024)}, u32[]{:S(2)}) copy-start(f32[4096]{0:T(1024)} %param.12) | copy-start | bytes 49156
Sparse Core Ops, SparseCore 0:
  9.6 97.0 all-gather.5
  108.3 100.1 all-gather.7
  249.1 95.5 reduce-scatter.2
  387.0 95.4 reduce-scatter.4

commit v2 on v1

--- a/solution.py
+++ b/solution.py
@@ -2,13 +2,232 @@
 import jax
 import jax.numpy as jnp
 from jax import lax
+from jax.experimental import pallas as pl
+from jax.experimental.pallas import tpu as pltpu
 from jax.sharding import PartitionSpec as P
 
-EPS = 1.0e-6
 ROPE_BASE = 1.0e6
 NEG_BIG = -1.0e30
+
+
 BF = jnp.bfloat16
 F32 = jnp.float32
+EPS = 1.0e-6
+MESH = pl.DeviceIdType.MESH
+NT = (((1,), (1,)), ((), ()))
+NN = (((1,), (0,)), ((), ()))
+TN = (((0,), (0,)), ((), ()))
+
+
+def dotf(a, b, dims=NN):
+    return lax.dot_general(a, b, dims, preferred_element_type=F32)
+
+
+def seat():
+    rank = lax.axis_index('tp')
+    core = lax.rem(rank, 2)
+    return rank, rank // 2, core
+
+
+def rdma(src, dst, ssem, rsem, dev):
+    return pltpu.make_async_remote_copy(src_ref=src, dst_ref=dst, send_sem=ssem, recv_sem=rsem, device_id={'tp': dev}, device_id_type=MESH)
+
+
+def enter(devs):
+    barrier = pltpu.get_barrier_semaphore()
+    for dev in devs:
+        pl.semaphore_signal(barrier, inc=1, device_id={'tp': dev}, device_id_type=MESH)
+    pl.semaphore_wait(barrier, len(devs))
+
+
+def rms_f32(x, gain):
+    return x * lax.rsqrt(jnp.mean(x * x, axis=-1, keepdims=True) + EPS) * gain
+
+
+def k1_body(nz, embed, wq, wk_t, wv_t, gain, tok_dev, h_out, q_out, kv_out, x_out, table, hbuf, wq_v, wkv_v, kvx, in_sem, h_sem, rs, rr, ss, sr, xs, xr):
+    rank, z, core = seat()
+    right = 2 * lax.rem(z + 1, nz) + core
+    left = 2 * lax.rem(z + nz - 1, nz) + core
+    sib = rank + 1 - 2 * core
+    par = lax.rem(z, 2)
+    far = rank + 2 - 4 * par
+    vrows = embed.shape[0]
+    kn = wk_t.shape[0]
+    half, sub_rows = vrows // 2, vrows // 4
+    vocab = vrows * 2 * nz
+    events = 2 * nz
+
+    ld = [pltpu.make_async_copy(embed, table.at[pl.ds(pl.multiple_of(rank * vrows, vrows), vrows)], in_sem.at[0]),
+          pltpu.make_async_copy(wq, wq_v, in_sem.at[1])]
+    for i, w in enumerate((wk_t, wv_t, wk_t, wv_t)):
+        ld.append(pltpu.make_async_copy(w, wkv_v.at[pl.ds(i * kn, kn)], in_sem.at[2 + i]))
+    for c in ld:
+        c.start()
+    enter((right, left, sib))
+    ld[0].wait()
+
+    def row_of(d, e, c):
+        s = e // 2
+        zd = lax.rem(z + (nz - s if d == 0 else s), nz)
+        return pl.multiple_of(vrows * (2 * zd + c) + half * d + sub_rows * lax.rem(e, 2), sub_rows)
+
+    def chunk(d, e, c):
+        return table.at[pl.ds(row_of(d, e, c), sub_rows)]
+
+    def ring(d, e):
+        a = chunk(d, e, core)
+        return rdma(a, a, rs.at[d, e], rr.at[d, e + 2], right if d == 0 else left)
+
+    def ring_in(d, e):
+        a = chunk(d, e, core)
+        return rdma(a, a, rs.at[d, e], rr.at[d, e], right if d == 0 else left)
+
+    def side(d, e):
+        a = chunk(d, e, core)
+        return rdma(a, a, ss.at[d, e], sr.at[d, e], sib)
+
+    def h_copy(slot, i, row):
+        return pltpu.make_async_copy(hbuf.at[slot, pl.ds(i * sub_rows, sub_rows)], h_out.at[pl.ds(row, sub_rows)], h_sem.at[slot, i])
+
+    own = 2 * par + core
+    lane = lax.broadcasted_iota(jnp.int32, (sub_rows, 4 * kn), 1)
+
+    def work(e):
+        slot = lax.rem(e, 2)
+
+        @pl.when(e >= 2)
+        def _():
+            for i in range(4):
+                h_copy(slot, i, row_of(0, e, core)).wait()
+
+        rows = [row_of(d, e, c) for d in (0, 1) for c in (0, 1)]
+        for i, row in enumerate(rows):
+            x = table[pl.ds(row, sub_rows), :].astype(F32)
+            ids = row + lax.broadcasted_iota(jnp.int32, (sub_rows, tok_dev.shape[1]), 0)
+            hit = jnp.zeros((sub_rows, tok_dev.shape[1]), F32)
+            for j in range(tok_dev.shape[0]):
+                hit = jnp.maximum(hit, jnp.where(tok_dev[j:j + 1, :] == ids, 1.0, 0.0))
+            used = jnp.max(hit, axis=1, keepdims=True)
+            h = jnp.where(used > 0.5, rms_f32(x, gain[...]), 0.0)
+            hbuf[slot, pl.ds(i * sub_rows, sub_rows), :] = h.astype(BF)
+            h_copy(slot, i, row).start()
+        hb = hbuf[slot]
+        q = dotf(hb, wq_v[...]).astype(BF)
+        kv = dotf(hb, wkv_v[...], NT).astype(BF)
+        for i, row in enumerate(rows):
+            q_out[pl.ds(row, sub_rows), :] = q[i * sub_rows:(i + 1) * sub_rows]
+            upper = row // (vocab // 2)
+            r2 = pl.multiple_of(lax.rem(row, vocab // 2), sub_rows)
+            new = kv[i * sub_rows:(i + 1) * sub_rows]
+            old = kvx[own, pl.ds(r2, sub_rows), :]
+            mine = (lane // (2 * kn)) == upper
+            kvx[own, pl.ds(r2, sub_rows), :] = jnp.where(mine, new.astype(F32), old.astype(F32)).astype(BF)
+
+    kvx[...] = jnp.zeros_like(kvx)
+
+    def step(e, _):
+        @pl.when(e >= 2)
+        def _():
+            for d in (0, 1):
+                ring_in(d, e).wait_recv()
+
+        @pl.when(e < events - 2)
+        def _():
+            for d in (0, 1):
+                ring(d, e).start()
+        for d in (0, 1):
+            side(d, e).start()
+
+        @pl.when(e == 1)
+        def _():
+            for c in ld[1:]:
+                c.wait()
+
+        @pl.when(e >= 1)
+        def _():
+            for d in (0, 1):
+                side(d, e - 1).wait_recv()
+            work(e - 1)
+        return 0
+
+    lax.fori_loop(0, events, step, 0)
+    for d in (0, 1):
+        side(d, events - 1).wait_recv()
+    work(events - 1)
+
+    opp = 2 * (1 - par) + core
+    to_far = rdma(kvx.at[own], kvx.at[own], xs.at[0], xr.at[0], far)
+    to_sib = rdma(kvx.at[own], kvx.at[own], xs.at[1], xr.at[1], sib)
+    relay = rdma(kvx.at[opp], kvx.at[opp], xs.at[2], xr.at[2], sib)
+    to_far.start()
+    to_sib.start()
+    mine = jnp.broadcast_to(tok_dev[pl.ds(rank, 1), :].astype(F32), (tok_dev.shape[1], tok_dev.shape[1]))
+    col = mine.T.astype(jnp.int32)
+    lanes = lax.broadcasted_iota(jnp.int32, col.shape, 1)
+    hot = jnp.concatenate([jnp.where(col == lanes + j * col.shape[1], 1.0, 0.0).astype(BF) for j in range(vocab // col.shape[1])], axis=1)
+    width = 512 if embed.shape[1] % 512 == 0 else embed.shape[1]
+
+    def pick(j, _):
+        cols = pl.ds(pl.multiple_of(j * width, width), width)
+        x_out[:, cols] = dotf(hot, table[:, cols]).astype(BF)
+        return 0
+
+    lax.fori_loop(0, embed.shape[1] // width, pick, 0)
+    to_far.wait_recv()
+    relay.start()
+    to_sib.wait_recv()
+    relay.wait_recv()
+    hd = kv_out.shape[1] // 2
+    for up in (0, 1):
+        acc = None
+        for r in range(4):
+            l_i = lax.broadcasted_iota(jnp.int32, (4 * kn, 2 * hd), 0) - 2 * kn * up
+            m_i = lax.broadcasted_iota(jnp.int32, (4 * kn, 2 * hd), 1)
+            is_k = (l_i >= 0) & (l_i < kn) & (m_i == l_i + kn * r)
+            is_v = (l_i >= kn) & (l_i < 2 * kn) & (m_i == hd + kn * r + l_i - kn)
+            place = jnp.where(is_k | is_v, 1.0, 0.0).astype(BF)
+            t = dotf(kvx[r], place)
+            acc = t if acc is None else acc + t
+        kv_out[up * (vocab // 2):(up + 1) * (vocab // 2), :] = acc.astype(BF)
+    for c in (to_far, to_sib, relay):
+        c.wait_send()
+
+    def drain(e, _):
+        @pl.when(e < events - 2)
+        def _():
+            for d in (0, 1):
+                ring(d, e).wait_send()
+        for d in (0, 1):
+            side(d, e).wait_send()
+        return 0
+
+    lax.fori_loop(0, events, drain, 0)
+    for slot in (0, 1):
+        for i in range(4):
+            h_copy(slot, i, row_of(0, 0, core)).wait()
+
+
+def gather_project(nz, embed, wq, wk_t, wv_t, gain, tok_dev):
+    vrows, d = embed.shape
+    vocab = vrows * 2 * nz
+    qn = wq.shape[1]
+    kn = wk_t.shape[0]
+    hd = 4 * kn
+    ev = 2 * nz
+    dma = pltpu.SemaphoreType.DMA
+    anym = pl.BlockSpec(memory_space=pl.ANY)
+    vm = pl.BlockSpec(memory_space=pltpu.VMEM)
+    return pl.pallas_call(
+        functools.partial(k1_body, nz),
+        name='gather_project',
+        out_shape=(jax.ShapeDtypeStruct((vocab, d), BF), jax.ShapeDtypeStruct((vocab, qn), BF), jax.ShapeDtypeStruct((vocab, 2 * hd), BF), jax.ShapeDtypeStruct((vrows, d), BF)),
+        in_specs=[anym, anym, anym, anym, vm, vm],
+        out_specs=(anym, vm, vm, vm),
+        scratch_shapes=[pltpu.VMEM((vocab, d), BF), pltpu.VMEM((2, vrows, d), BF), pltpu.VMEM((d, qn), BF), pltpu.VMEM((4 * kn, d), BF), pltpu.VMEM((4, vocab // 2, 4 * kn), BF),
+                        dma((6,)), dma((2, 4)), dma((2, ev)), dma((2, ev)), dma((2, ev)), dma((2, ev)), dma((3,)), dma((3,))],
+        compiler_params=pltpu.CompilerParams(collective_id=0, has_side_effects=True, vmem_limit_bytes=56 * 1024 * 1024),
+        cost_estimate=pl.CostEstimate(flops=2 * vocab * d * (qn + 4 * kn), bytes_accessed=4 * vocab * d, transcendentals=0),
+    )(embed, wq, wk_t, wv_t, gain, tok_dev)
 
 
 def rope_tables(seq_len, head_dim):
@@ -71,27 +290,18 @@
         toks = batch * seq
         tok_flat = tok_ids.reshape(toks)
 
-        table = lax.all_gather(embed_loc, 'tp', axis=0, tiled=True)
-        gy_in = gy_loc
+        dev_ids = tok_ids.reshape(batch, tp, seq_dev).transpose(1, 0, 2)
+        hidden, q_rows, kv_rows, x_mine = gather_project(tp // 2, embed_loc, wq, wk.T, wv.T, norm_gain[None, :], dev_ids.reshape(tp, batch * seq_dev))
+        gy_in, q_rows = lax.optimization_barrier((gy_loc, q_rows))
         gy_all = lax.all_gather(gy_in, 'tp', axis=0, tiled=False).reshape(toks, d_model)
-        used = jnp.any(tok_flat[None, :] == jnp.arange(vocab, dtype=tok_ids.dtype)[:, None], axis=1)
-        hidden = jnp.where(used[:, None], rms_scale(table.astype(F32), norm_gain), 0.0).astype(BF)
+        onehot = (tok_flat[:, None] == jnp.arange(vocab, dtype=tok_ids.dtype)[None, :]).astype(BF)
+        q_tok = mm('tr,rn->tn', onehot, q_rows).astype(BF)
+        kv_tok = mm('tr,rn->tn', onehot, kv_rows).astype(BF)
         w_all = jnp.concatenate([wq, wk, wv], axis=1)
-        rows_all = mm('rd,dn->rn', hidden, w_all).astype(BF)
-        onehot = (tok_flat[:, None] == jnp.arange(vocab, dtype=tok_ids.dtype)[None, :]).astype(BF)
-        q_tok = mm('tr,rn->tn', onehot, rows_all[:, :qn]).astype(BF)
-        kv_t = rows_all[:, qn:].T
         swap1 = [(i, i ^ 1) for i in range(tp)]
         swap2 = [(i, i ^ 2) for i in range(tp)]
         odd = (rank & 1) == 1
         far = (rank & 2) == 2
-        kv_s = lax.ppermute(kv_t, 'tp', swap1)
-        pair = jnp.where(odd, jnp.stack([kv_s, kv_t]), jnp.stack([kv_t, kv_s]))
-        pair_o = lax.ppermute(pair, 'tp', swap2)
-        quad = jnp.where(far, jnp.stack([pair_o, pair]), jnp.stack([pair, pair_o]))
-        quad = quad.reshape(share, 2, kn, vocab).transpose(1, 0, 2, 3).reshape(2 * hd, vocab)
-        kv_tok = mm('tr,nr->tn', onehot, quad).astype(BF)
-
         cos_tab, sin_tab = rope_tables(seq, hd)
         rope_fn = functools.partial(norm_rope, cos_tab=cos_tab, sin_tab=sin_tab)
         q_wide, q_pull = jax.vjp(rope_fn, q_tok.reshape(batch, seq, heads, hd), q_gain)
@@ -104,8 +314,6 @@
 
         out_part = mm('tn,nd->td', attn_dev, wo).astype(BF)
         attn_sum = lax.psum_scatter(out_part, 'tp', scatter_dimension=0, tiled=True)
-        my_ids = lax.dynamic_slice_in_dim(tok_ids, rank * seq_dev, seq_dev, axis=1)
-        x_mine = jnp.take(table, my_ids.reshape(-1), axis=0)
         y_loc = (x_mine.astype(F32) + attn_sum.astype(F32)).astype(BF).reshape(batch, seq_dev, d_model)
 
         gw_out = mm('tn,td->nd', attn_dev, gy_all)
@@ -129,7 +337,7 @@
         gh = lax.psum_scatter(gh_part, 'tp', scatter_dimension=0, tiled=True)
         gw_query = mm('rd,rn->dn', hidden, gq_rows)
         gw_kv = mm('rd,rn->dn', hidden, gkv_rows)
-        dev_ids = tok_ids.reshape(batch, tp, seq_dev).transpose(1, 0, 2).reshape(toks)
+        dev_ids = dev_ids.reshape(toks)
         my_rows = rank * vrows + jnp.arange(vrows, dtype=tok_ids.dtype)
         mine_hot = (my_rows[:, None] == dev_ids[None, :]).astype(BF)
         gy_rows = lax.optimization_barrier(mm('rt,td->rd', mine_hot, gy_all))

time: 523 us -> 477 us (0.912)
  Pallas kernels: 0 us -> 106 us
  waiting for transfers between devices: 152 us -> 60.7 us
  other arithmetic: 54.6 us -> 34.1 us
  matrix products: 214 us -> 196 us
  local copies, waits for them, and re-layouts: 58.1 us -> 40.9 us
    pallas_call x0 -> x1, Pallas kernels: none -> 106 us  [gather_project(): pl.pallas_call(functools.partial(k1_body, nz), name='gather_project', out...]
    all_gather x1 -> x0, waiting for transfers between devices: 90 us -> none  [local_step(): table = lax.all_gather(embed_loc, 'tp', axis=0, tiled=True)]
    ppermute x2 -> x0, waiting for transfers between devices: 21.1 us -> none  [the longest x1 21.1 us: local_step(): pair_o = lax.ppermute(pair, 'tp', swap2)]
    dot_general x17 -> x16, matrix products: 203 us -> 185 us  [mm(): return jnp.einsum(spec, a, b, preferred_element_type=F32)]
    reduce_scatter x1, waiting for transfers between devices: 37.2 us -> 49.8 us  [local_step(): gh = lax.psum_scatter(gh_part, 'tp', scatter_dimension=0, tiled=True)]
    gather x1 -> x0, local copies, waits for them, and re-layouts: 11.1 us -> none  [local_step(): x_mine = jnp.take(table, my_ids.reshape(-1), axis=0)]
    convert_element_type x1 -> x0, other arithmetic: 10.6 us -> none  [local_step(): jnp.where(used[:, None], rms_scale(table.astype(F32), norm_gain), 0.0)]
    all_gather x1, waiting for transfers between devices: 0.02 us -> 8.66 us  [local_step(): lax.all_gather(gy_in, 'tp', axis=0, tiled=False).reshape(toks, d_model)]
  transfers between devices with their start and end apart: 8 -> 5, of which waited for: 4 -> 3; matrix products, arithmetic and copies ran while one was open for 61% -> 54% of each run, Pallas kernels for 0% -> 0%
where the time goes in v2:
time: 477 us; the launch traced here: 471 us
  matrix products  196 us (41%)
  Pallas kernels  106 us (22%)
  waiting for transfers between devices  60.7 us (13%)
  local copies, waits for them, and re-layouts  40.9 us (9%)
  other arithmetic  34.1 us (7%)
  blocking collectives  17.5 us (4%)
  between operations  14.6 us (3%)
    dot_general x16, matrix products, mm(): return jnp.einsum(spec, a, b, preferred_element_type=F32)  185 us
    pallas_call x1, Pallas kernels, gather_project(): pl.pallas_call(functools.partial(k1_body, nz), name='gather_project', out...  106 us
    reduce_scatter x1, waiting for transfers between devices, local_step(): gh = lax.psum_scatter(gh_part, 'tp', scatter_dimension=0, tiled=True)  49.8 us
    all_gather x1, blocking collectives, local_step(): gains = jnp.sum(lax.all_gather(gains, 'tp', axis=0, tiled=False), axis=0)  17.5 us
    convert_element_type x6, local copies, waits for them, and re-layouts, norm_rope(): normed = rms_scale(raw_heads.astype(F32), gain_vec)  16.7 us
    sub x1, matrix products, attention_core(): attn_prob = jax.nn.softmax(jnp.where(causal, scores, NEG_BIG), axis=-1)  11 us
  transfers between devices with their start and end apart: 5, of which 3 were waited for; matrix products, arithmetic and copies ran while one was open for 54% of the time, Pallas kernels for 0%

profile of v2, /device:TPU:21, one launch (start us, length us, event | category | flops | bytes accessed | tf_op | source)
XLA Modules:
  0.0 471.1 jit_solution(9721784024961446030)
XLA Ops:
  7.3 0.8 reshape.249
  8.1 0.7 reshape.250.tok_dev
  8.7 106.4 %gather_project.1 = (bf16[2048,4096]{1,0:T(8,128)(2,1)}, bf16[2048,512]{1,0:T(8,128)(2,1)}, bf16[2048,256]{1,0:T(8,128)(2,1)}, bf16[128,4096]{1,0:T(8,128)(2,1)}) custom-call(bf16[128,4096]{1,0:T(8,128)(2,1)} %embed.1, bf16[4096,512]{1,0:T(8,128)(2,1)} %wq.1, bf16[32,4096]{1,0:T(8,128)(2,1)} %bitcast.213, bf16[32,4096]{1,0:T(8,128)(2,1)} %bitcast.214, ...), custom_call_target="tpu_custom_call" | custom-call | flops 10737418240 | bytes 33554432 | tf_op jit(solution)/shard_map/gather_project/pallas_call | solution.py:220
  115.6 4.2 fusion.37
  119.8 0.3 multiply_reduce_fusion.5
  120.2 0.9 slice_convert_fusion
  121.5 0.3 copy.150
  121.8 7.7 %fusion.35 = f32[2048,512]{1,0:T(8,128)} fusion(bf16[2048,512]{1,0:T(8,128)(2,1)} %get-tuple-element.18, s32[2048]{0:T(1024)S(1)} %bitcast.218), kind=kOutput, calls=%fused_computation.57 | convolution fusion | flops 4301258752 | bytes 6299648 | tf_op jit(solution)/shard_map/tr,rn->tn/dot_general | solution.py:253
  129.5 5.2 %reshape.265 = f32[4,512,4,128]{3,2,1,0:T(4,128)} reshape(f32[2048,512]{1,0:T(8,128)} %fusion.35) | data formatting | bytes 8388608 | tf_op jit(solution)/shard_map/jvp()/convert_element_type | solution.py:246
  134.7 5.2 %copy.153 = f32[4,512,4,128]{1,3,2,0:T(8,128)} copy(f32[4,512,4,128]{3,2,1,0:T(4,128)} %reshape.265) | data formatting | bytes 8388608 | tf_op jit(solution)/shard_map/jvp()/convert_element_type | solution.py:246
  140.0 4.5 multiply_reduce_fusion.2
  144.8 0.8 iota_compare_fusion.13
  145.7 1.0 fusion.88
  147.0 1.2 fusion.81
  148.2 0.7 multiply_multiply_fusion
  149.0 0.8 slice_negate_fusion.1
  149.8 2.7 fusion.27
  152.5 11.0 %fusion.104 = (f32[4,4,512]{2,1,0:T(4,128)S(1)}, f32[4,4,512,512]{2,3,1,0:T(8,128)}) fusion(pred[512,512]{0,1:T(8,128)(4,1)S(1)} %copy-done.22, bf16[4,512,128,1]{1,2,3,0:T(8,128)(2,1)S(1)} %copy-done.15, bf16[4,512,4,128]{1,3,2,0:T(8,128)(2,1)} %fusion.27), kind=kOutput, calls=%fused_computation.154 | convolution fusion | flops 1090519552 | bytes 19693568 | tf_op jit(solution)/shard_map/sub | solution.py:260
  163.5 8.6 %convert_bitcast_fusion = bf16[4,512,4,128]{1,3,2,0:T(8,128)(2,1)} fusion(bf16[4,512,128,1]{2,1,3,0:T(8,128)(2,1)S(1)} %bitcast.203, f32[4,4,512,512]{2,3,1,0:T(8,128)} %get-tuple-element.44, f32[4,4,512]{2,1,0:T(4,128)S(1)} %get-tuple-element.43), kind=kOutput, calls=%fused_computation.77 | convolution fusion | flops 1083179008 | bytes 19431424 | tf_op jit(solution)/shard_map/bgqs,bsh->bqgh/dot_general | solution.py:253
  172.1 4.2 copy.158
  176.3 2.7 reshape.252
  179.2 2.8 copy-done.30
  182.0 11.6 %convolution_convert_fusion.1 = bf16[2048,4096]{1,0:T(8,128)(2,1)} fusion(bf16[2048,512]{1,0:T(8,128)(2,1)S(1)} %bitcast.206, bf16[512,4096]{1,0:T(8,128)(2,1)S(1)} %copy-done.30), kind=kOutput, calls=%fused_computation.15 | convolution fusion | flops 8598323200 | bytes 23068672 | tf_op jit(solution)/shard_map/tn,nd->td/dot_general | solution.py:253
  193.8 0.8 copy-done.20
  194.6 1.3 copy.174
  195.9 1.3 copy.175
  197.2 8.7 %all-gather.5.cloned.1.call-done = bf16[64,32,4096]{2,1,0:T(8,128)(2,1)} async-done(((bf16[4,32,4096]{2,1,0:T(8,128)(2,1)}), bf16[64,32,4096]{2,1,0:T(8,128)(2,1)}) %all-gather.5.cloned.1.call-update) | async-done | bytes 16777232 | tf_op jit(solution)/shard_map/all_gather | solution.py:296
  205.9 14.0 %convolution_convert_fusion.2 = bf16[2048,512]{1,0:T(8,128)(2,1)S(1)} fusion(bf16[2048,4096]{1,0:T(8,128)(2,1)} %bitcast.193, bf16[512,4096]{1,0:T(8,128)(2,1)} %param.18), kind=kOutput, calls=%fused_computation.59 | convolution fusion | flops 8590983168 | bytes 23068672 | tf_op jit(solution)/shard_map/td,nd->tn/dot_general | solution.py:253
  219.9 1.6 copy.212
  221.5 2.5 reshape.257
  224.1 9.2 %fusion.52 = f32[4,512,512,4]{2,1,3,0:T(8,128)} fusion(bf16[4,512,128,1]{2,1,3,0:T(8,128)(2,1)} %bitcast.202, bf16[4,512,4,128]{3,2,1,0:T(4,128)(2,1)S(1)} %reshape.257), kind=kOutput, calls=%fused_computation.80 | convolution fusion | flops 1073741824 | bytes 19398656 | tf_op jit(solution)/shard_map/bqgh,bsh->bgqs/dot_general | solution.py:253
  233.3 23.6 %fusion.67 = bf16[4,512,128]{1,2,0:T(8,128)(2,1)} fusion(bf16[4,512,4,128]{1,3,2,0:T(8,128)(2,1)} %fusion.27, f32[4,512,512,4]{2,1,3,0:T(8,128)} %fusion.52, f32[4,4,512,512]{2,3,1,0:T(8,128)} %get-tuple-element.44, f32[4,4,512]{2,1,0:T(4,128)S(1)} %get-tuple-element.43), kind=kOutput, calls=%fused_computation.89 | convolution fusion | flops 1103372800 | bytes 36208640 | tf_op jit(solution)/shard_map/bgqs,bqgh->bsh/dot_general | solution.py:253
  256.9 1.3 fusion.71
  258.3 0.4 multiply_reduce_fusion.3
  258.7 1.2 fusion.72
  260.0 1.3 copy.169
  261.3 8.1 %fusion.62 = bf16[4,512,128]{2,1,0:T(8,128)(2,1)S(1)} fusion(bf16[4,512,4,128]{3,2,1,0:T(4,128)(2,1)S(1)} %reshape.257, f32[4,4,512,512]{2,3,1,0:T(8,128)} %get-tuple-element.44, f32[4,4,512]{2,1,0:T(4,128)S(1)} %get-tuple-element.43), kind=kOutput, calls=%fused_computation.88 | convolution fusion | flops 1082392576 | bytes 19431424 | tf_op jit(solution)/shard_map/bgqs,bqgh->bsh/dot_general | solution.py:253
  269.4 3.7 fusion.5
  273.4 0.4 collective-permute-start
  274.1 25.1 %bitcast_multiply_fusion.6 = (f32[4,512,4,128]{1,3,2,0:T(8,128)}, bf16[4,128,4,512]{3,1,2,0:T(8,128)(2,1)}) fusion(f32[512,128]{0,1:T(8,128)S(1)} %copy-done.8, bf16[4,512,128,1]{1,2,3,0:T(8,128)(2,1)} %fusion.81, f32[4,512,512,4]{2,1,3,0:T(8,128)} %fusion.52, f32[4,4,512,512]{2,3,1,0:T(8,128)} %get-tuple-element.44, f32[4,4,512]{2,1,0:T(4,128)S(1)} %get-tuple-element.43), kind=kOutput, calls=%fused_computation.39 | convolution fusion | flops 1106256384 | bytes 40665088 | tf_op jit(solution)/shard_map/bgqs,bsh->bqgh/dot_general | solution.py:253
  299.2 3.2 fusion.100
  302.6 0.7 copy-done.5
  303.3 1.9 multiply_reduce_fusion
  305.2 2.7 fusion.25
  307.9 4.2 copy.165
  312.1 1.4 bitcast_add_fusion
  313.5 0.5 collective-permute-start.1
  314.1 5.5 %fusion.36 = bf16[2048,512]{0,1:T(8,128)(2,1)S(1)} fusion(s32[2048]{0:T(1024)S(1)} %bitcast.220, bf16[256,8,4,128]{3,2,1,0:T(4,128)(2,1)S(1)} %bitcast.204), kind=kOutput, calls=%fused_computation.58 | convolution fusion | flops 4300210176 | bytes 4202496 | tf_op jit(solution)/shard_map/tr,tn->rn/dot_general | solution.py:253
  319.6 2.0 collective-permute-done.1
  321.8 22.6 %convolution_convert_fusion = bf16[2048,4096]{1,0:T(8,128)(2,1)} fusion(bf16[4096,32]{1,0:T(8,128)(2,1)S(1)} %copy-done.12, bf16[4096,32]{1,0:T(8,128)(2,1)S(1)} %copy-done.11, bf16[4096,512]{1,0:T(8,128)(2,1)} %wq.1, bf16[2048,64]{0,1:T(8,128)(2,1)S(1)} %bitcast.208, bf16[2048,512]{0,1:T(8,128)(2,1)S(1)} %fusion.36), kind=kOutput, calls=%fused_computation.14 | convolution fusion | flops 9690939392 | bytes 23855104 | tf_op jit(solution)/shard_map/rn,dn->rd/dot_general | solution.py:253
  344.4 0.7 copy-done.19
  345.2 0.4 copy-done.2
  346.0 8.3 %fusion.78 = f32[128,4096]{1,0:T(8,128)S(1)} fusion(bf16[2048,4096]{1,0:T(8,128)(2,1)} %bitcast.194, s32[2048]{0:T(1024)S(1)} %eq.41, s32[128]{0:T(128)S(1)} %iota_add_fusion), kind=kOutput, calls=%fused_computation.109 | convolution fusion | flops 2147745792 | bytes 18883072 | tf_op jit(solution)/shard_map/rt,td->rd/dot_general | solution.py:253
  354.3 14.9 %convolution_bitcast_fusion = f32[512,4096]{1,0:T(8,128)} fusion(bf16[16,4,32,4096]{3,2,1,0:T(8,128)(2,1)} %bitcast.195, bf16[4,16,32,512]{3,2,1,0:T(8,128)(2,1)S(1)} %copy-done.4), kind=kOutput, calls=%fused_computation.28 | convolution fusion | flops 8589934592 | bytes 27262976 | tf_op jit(solution)/shard_map/tn,td->nd/dot_general | solution.py:253
  369.2 14.4 %fusion.105 = f32[4096,512]{1,0:T(8,128)} fusion(bf16[2048,4096]{1,0:T(8,128)(2,1)S(1)} %bitcast.192, bf16[2048,512]{0,1:T(8,128)(2,1)} %copy-done.31), kind=kOutput, calls=%fused_computation.155 | convolution fusion | flops 8589934592 | bytes 27262976 | tf_op jit(solution)/shard_map/rd,rn->dn/dot_general | solution.py:253
  383.6 3.0 fusion.106
  386.7 1.0 fusion.101
  387.7 2.8 add_convert_fusion
  390.5 49.8 %reduce-scatter.5.cloned.1.call-done = bf16[128,4096]{1,0:T(8,128)(2,1)} async-done(((bf16[2048,4096]{1,0:T(8,128)(2,1)}), bf16[128,4096]{1,0:T(8,128)(2,1)}) %reduce-scatter.5.cloned.1.call-update) | async-done | bytes 1048592 | tf_op jit(solution)/shard_map/reduce_scatter | solution.py:337
  440.3 2.1 fusion.42
  442.4 17.5 %all-gather.2 = f32[16,1,4352]{2,1,0:T(1,128)S(1)} all-gather(f32[1,1,4352]{2,1,0:T(1,128)S(1)} %reshape.269), channel_id=3, replica_groups=mesh['dp'=4,'tp'=16] {'tp'}, dimensions={0}, use_global_device_ids=true | all-gather | bytes 295936 | tf_op jit(solution)/shard_map/all_gather | solution.py:348
  460.1 0.5 fusion.103
  460.6 0.6 slice.74
  461.2 3.1 fusion.43
  (104 shorter events, 3.6 us)
Async XLA Ops:
  7.2 198.7 %all-gather.5.cloned.1.call-start = ((), (), s32[]{:S(2)}) async-start(), calls=%async_computation.4 | async-start | bytes 17825792 | tf_op jit(solution)/shard_map/all_gather | solution.py:296
  8.1 107.2 %copy-start.18 = (s32[4,16,32]{2,0,1:T(4,128)}, s32[4,16,32]{2,0,1:T(4,128)S(1)}, u32[]{:S(2)}) copy-start(s32[4,16,32]{2,0,1:T(4,128)S(1)} %copy.213) | copy-start | bytes 24580
  8.7 106.8 %copy-start.24 = (s32[4,512]{1,0:T(4,128)S(1)}, s32[4,512]{1,0:T(4,128)}, u32[]{:S(2)}) copy-start(s32[4,512]{1,0:T(4,128)} %param.10) | copy-start | bytes 24580
  115.3 272.4 %reduce-scatter.3.cloned.1.call-start = ((), (), s32[]{:S(2)}) async-start(), calls=%async_computation.2 | async-start | bytes 17825792 | tf_op jit(solution)/shard_map/reduce_scatter | solution.py:316
  115.5 6.3 %copy-start.27 = (s32[1,4,4,128]{3,1,2,0:T(4,128)}, s32[1,4,4,128]{3,1,2,0:T(4,128)S(1)}, u32[]{:S(2)}) copy-start(s32[1,4,4,128]{3,1,2,0:T(4,128)S(1)} %copy.194) | copy-start | bytes 24580
  140.0 6.7 %copy-start.29 = (f32[128]{0:T(128)S(1)}, f32[128]{0:T(128)}, u32[]{:S(2)}) copy-start(f32[128]{0:T(128)} %param.14) | copy-start | bytes 1540
  144.8 3.4 copy-start.16
  144.8 3.4 copy-start
  144.8 3.4 copy-start.25
  146.7 3.1 copy-start.7
  146.7 3.1 copy-start.13
  149.8 2.7 copy-start.15
  149.8 2.7 copy-start.22
  152.5 11.0 %copy-start.9 = (bf16[2048,128]{1,0:T(8,128)(2,1)S(1)}, bf16[2048,128]{1,0:T(8,128)(2,1)}, u32[]{:S(2)}) copy-start(bf16[2048,128]{1,0:T(8,128)(2,1)} %get-tuple-element.38) | copy-start | bytes 1572868
  179.0 14.6 %copy-start.3 = (bf16[4,16,32,512]{3,2,1,0:T(8,128)(2,1)}, bf16[4,16,32,512]{3,2,1,0:T(8,128)(2,1)S(1)}, u32[]{:S(2)}) copy-start(bf16[4,16,32,512]{3,2,1,0:T(8,128)(2,1)S(1)} %reshape.252) | copy-start | bytes 6291460
  179.1 2.9 copy-start.30
  193.6 1.0 copy-start.20
  193.6 2.3 copy-start.21
  193.7 246.6 %reduce-scatter.5.cloned.1.call-start = ((), (), s32[]{:S(2)}) async-start(), calls=%async_computation.3 | async-start | bytes 17825792 | tf_op jit(solution)/shard_map/reduce_scatter | solution.py:337
  256.9 1.4 copy-start.6
  261.3 8.1 %copy-start.28 = (s32[1,4,4,128]{3,1,2,0:T(4,128)S(1)}, s32[1,4,4,128]{3,1,2,0:T(4,128)}, u32[]{:S(2)}) copy-start(s32[1,4,4,128]{3,1,2,0:T(4,128)} %copy-done.27) | copy-start | bytes 24580
  273.1 1.0 copy-start.8
  273.4 38.7 %collective-permute-start = (bf16[2,64,2048]{2,1,0:T(8,128)(2,1)S(1)}, bf16[2,64,2048]{2,1,0:T(8,128)(2,1)}, u32[]{:S(2)}, u32[]{:S(2)}) collective-permute-start(bf16[2,64,2048]{2,1,0:T(8,128)(2,1)S(1)} %fusion.80), channel_id=1, source_target_pairs={{0,1},{1,0},{2,3},{3,2},{4,5},{5,4},{6,7},{7,6},{8,9},{9,8},{10,11... | collective-permute-start | bytes 1572872 | tf_op jit(solution)/shard_map/ppermute | solution.py:331
  299.2 3.5 copy-start.1
  299.2 4.1 copy-start.5
  299.2 4.1 copy-start.14
  299.2 4.1 copy-start.26
  303.3 1.9 copy-start.17
  312.1 2.0 copy-start.10
  313.5 8.1 %collective-permute-start.1 = (bf16[64,2048]{1,0:T(8,128)(2,1)S(1)}, bf16[64,2048]{1,0:T(8,128)(2,1)S(1)}, u32[]{:S(2)}, u32[]{:S(2)}) collective-permute-start(bf16[64,2048]{1,0:T(8,128)(2,1)S(1)} %fusion.86), channel_id=1, source_target_pairs={{0,2},{1,3},{2,0},{3,1},{4,6},{5,7},{6,4},{7,5},{8,10},{9,11},{10,... | collective-permute-start | bytes 786440 | tf_op jit(solution)/shard_map/ppermute | solution.py:334
  314.1 7.7 %copy-start.11 = (bf16[4096,32]{1,0:T(8,128)(2,1)S(1)}, bf16[4096,32]{1,0:T(8,128)(2,1)}, u32[]{:S(2)}) copy-start(bf16[4096,32]{1,0:T(8,128)(2,1)} %copy.174) | copy-start | bytes 786436
  314.1 7.7 %copy-start.12 = (bf16[4096,32]{1,0:T(8,128)(2,1)S(1)}, bf16[4096,32]{1,0:T(8,128)(2,1)}, u32[]{:S(2)}) copy-start(bf16[4096,32]{1,0:T(8,128)(2,1)} %copy.175) | copy-start | bytes 786436
  319.6 24.8 %copy-start.31 = (bf16[2048,512]{0,1:T(8,128)(2,1)}, bf16[2048,512]{0,1:T(8,128)(2,1)S(1)}, u32[]{:S(2)}) copy-start(bf16[2048,512]{0,1:T(8,128)(2,1)S(1)} %fusion.36) | copy-start | bytes 6291460
  344.4 0.8 copy-start.19
  344.4 1.2 copy-start.2
  345.9 8.3 %copy-start.4 = (bf16[4,16,32,512]{3,2,1,0:T(8,128)(2,1)S(1)}, bf16[4,16,32,512]{3,2,1,0:T(8,128)(2,1)}, u32[]{:S(2)}) copy-start(bf16[4,16,32,512]{3,2,1,0:T(8,128)(2,1)} %copy-done.3) | copy-start | bytes 6291460
  345.9 23.3 %slice-start = ((s8[16777216]{0:T(1024)(128)(4,1)}), s8[4194304]{0:T(1024)(128)(4,1)S(1)}, s32[]{:S(2)}) async-start(s8[16777216]{0:T(1024)(128)(4,1)} %bitcast.191), calls=%async_computation.5 | async-start | bytes 8388608
  345.9 23.2 %slice-start.1 = ((s8[16777216]{0:T(1024)(128)(4,1)}), s8[4194304]{0:T(1024)(128)(4,1)S(1)}, s32[]{:S(2)}) async-start(s8[16777216]{0:T(1024)(128)(4,1)} %bitcast.191), calls=%async_computation.6 | async-start | bytes 8388608
  354.3 14.9 %slice-start.2 = ((s8[16777216]{0:T(1024)(128)(4,1)}), s8[4194304]{0:T(1024)(128)(4,1)S(1)}, s32[]{:S(2)}) async-start(s8[16777216]{0:T(1024)(128)(4,1)} %bitcast.191), calls=%async_computation.7 | async-start | bytes 8388608
  354.3 14.9 %slice-start.3 = ((s8[16777216]{0:T(1024)(128)(4,1)}), s8[4194304]{0:T(1024)(128)(4,1)S(1)}, s32[]{:S(2)}) async-start(s8[16777216]{0:T(1024)(128)(4,1)} %bitcast.191), calls=%async_computation.8 | async-start | bytes 8388608
  386.7 53.6 %copy-start.23 = (f32[4096]{0:T(1024)S(1)}, f32[4096]{0:T(1024)}, u32[]{:S(2)}) copy-start(f32[4096]{0:T(1024)} %param.12) | copy-start | bytes 49156
Sparse Core Ops, SparseCore 0:
  115.4 90.4 all-gather.4
  208.2 94.8 reduce-scatter.2
  344.6 95.6 reduce-scatter.4

commit v3 on v2

v3 whole, which is shorter than its diff:
```python
import functools
import jax
import numpy as np
import jax.numpy as jnp
from jax import lax
from jax.experimental import pallas as pl
from jax.experimental.pallas import tpu as pltpu
from jax.sharding import PartitionSpec as P


BF = jnp.bfloat16
F32 = jnp.float32
EPS = 1.0e-6
ROPE_BASE = 1.0e6
NEG_BIG = -1.0e30
MESH = pl.DeviceIdType.MESH
ANY = pl.BlockSpec(memory_space=pl.ANY)
VM = pl.BlockSpec(memory_space=pltpu.VMEM)
NT = (((1,), (1,)), ((), ()))
NN = (((1,), (0,)), ((), ()))
TN = (((0,), (0,)), ((), ()))


def dotf(a, b, dims=NN):
    return lax.dot_general(a, b, dims, preferred_element_type=F32)


def rdma(src, dst, ssem, rsem, dev):
    return pltpu.make_async_remote_copy(src_ref=src, dst_ref=dst, send_sem=ssem, recv_sem=rsem, device_id={'tp': dev}, device_id_type=MESH)


def enter(devs):
    barrier = pltpu.get_barrier_semaphore()
    for dev in devs:
        pl.semaphore_signal(barrier, inc=1, device_id={'tp': dev}, device_id_type=MESH)
    pl.semaphore_wait(barrier, len(devs))


def rms_f32(x, gain):
    return x * lax.rsqrt(jnp.mean(x * x, axis=-1, keepdims=True) + EPS) * gain


def rope_f32(raw, gain, cos, sin_s):
    n = rms_f32(raw.astype(F32), gain)
    return n * cos + pltpu.roll(n, n.shape[1] // 2, 1) * sin_s


def masked(scores, first):
    r_i = lax.broadcasted_iota(jnp.int32, scores.shape, 0) + first
    c_i = lax.broadcasted_iota(jnp.int32, scores.shape, 1)
    return jnp.where(r_i >= c_i, scores, NEG_BIG)


def soft(scores):
    e = jnp.exp(scores - jnp.max(scores, axis=-1, keepdims=True))
    return e * (1.0 / jnp.sum(e, axis=-1, keepdims=True))


def ka_body(nz, embed, gy, wq, wk_t, wv_t, wo, gain, qg, kg, cos, sin_s, tok_dev, tok_seq,
            h_out, gy_out, q_tok, kv_tok, q_rot, k_rot, o_out, do_out, x_out,
            table, hbuf, wq_v, wkv_v, wo_v, idcol, kvacc, kvx, gown, gbuf,
            in_sem, h_sem, g_sem, rs, rr, ss, sr, rs2, rr2, ss2, sr2, xs, xr):
    rank = lax.axis_index('tp')
    z, core = rank // 2, lax.rem(rank, 2)
    right = 2 * lax.rem(z + 1, nz) + core
    left = 2 * lax.rem(z + nz - 1, nz) + core
    sib = rank + 1 - 2 * core
    par = lax.rem(z, 2)
    far = rank + 2 - 4 * par
    vrows = embed.shape[0]
    kn = wk_t.shape[0]
    half, sub_rows = vrows // 2, vrows // 4
    vocab = vrows * 2 * nz
    batch, seq = tok_seq.shape
    toks = batch * seq
    qn = wq.shape[1]
    hd = qg.shape[1]
    heads = qn // hd
    events = 2 * nz
    pos = seq // (2 * nz)

    ld = [pltpu.make_async_copy(embed, table.at[pl.ds(pl.multiple_of(rank * vrows, vrows), vrows)], in_sem.at[0]),
          pltpu.make_async_copy(gy, gown, in_sem.at[1]),
          pltpu.make_async_copy(wq, wq_v, in_sem.at[2]),
          pltpu.make_async_copy(wo, wo_v, in_sem.at[3])]
    for i, w in enumerate((wk_t, wv_t, wk_t, wv_t)):
        ld.append(pltpu.make_async_copy(w, wkv_v.at[pl.ds(i * kn, kn)], in_sem.at[4 + i]))
    for c in ld:
        c.start()
    enter((right, left, sib))
    ld[0].wait()

    def zd_of(d, e):
        s = e // 2
        return lax.rem(z + (nz - s if d == 0 else s), nz)

    def row_of(d, e, c):
        return pl.multiple_of(vrows * (2 * zd_of(d, e) + c) + half * d + sub_rows * lax.rem(e, 2), sub_rows)

    def ring(d, e, recv_e):
        a = table.at[pl.ds(row_of(d, e, core), sub_rows)]
        return rdma(a, a, rs.at[d, e], rr.at[d, recv_e], right if d == 0 else left)

    def side(d, e):
        a = table.at[pl.ds(row_of(d, e, core), sub_rows)]
        return rdma(a, a, ss.at[d, e], sr.at[d, e], sib)

    def h_copy(slot, i, row):
        return pltpu.make_async_copy(hbuf.at[slot, pl.ds(i * sub_rows, sub_rows)], h_out.at[pl.ds(row, sub_rows)], h_sem.at[slot, i])

    def g_row(d, e, c):
        return pl.multiple_of(seq * (2 * d + lax.rem(e, 2)) + pos * (2 * zd_of(d, e) + c), pos)

    def g_piece(d, e, c):
        return gy_out.at[pl.ds(g_row(d, e, c), pos)]

    def g_own(d, e):
        return gown.at[pl.ds(pl.multiple_of(pos * (2 * d + lax.rem(e, 2)), pos), pos)]

    def g_ring(d, e, recv_e, first):
        a = g_piece(d, e, core)
        return rdma(g_own(d, e) if first else a, a, rs2.at[d, e], rr2.at[d, recv_e], right if d == 0 else left)

    def g_side(d, e, first):
        a = g_piece(d, e, core)
        return rdma(g_own(d, e) if first else a, a, ss2.at[d, e], sr2.at[d, e], sib)

    def g_home(d, e):
        return pltpu.make_async_copy(g_own(d, e), g_piece(d, e, core), in_sem.at[8 + 2 * d + e])

    def g_load(slot, i, d, c, e):
        return pltpu.make_async_copy(g_piece(d, e, c), gbuf.at[slot, pl.ds(i * pos, pos)], g_sem.at[slot, i])

    for b in range(batch):
        wide = jnp.broadcast_to(tok_seq[b:b + 1, :].astype(F32), (idcol.shape[1], seq))
        idcol[b * seq:(b + 1) * seq, :] = wide.T.astype(jnp.int32)
    q_tok[...] = jnp.zeros_like(q_tok)
    kvacc[...] = jnp.zeros_like(kvacc)

    def work(e):
        slot = lax.rem(e, 2)

        @pl.when(e >= 2)
        def _():
            for i in range(4):
                h_copy(slot, i, row_of(0, e, core)).wait()

        rows = [row_of(d, e, c) for d in (0, 1) for c in (0, 1)]
        for i, row in enumerate(rows):
            x = table[pl.ds(row, sub_rows), :].astype(F32)
            ids = row + lax.broadcasted_iota(jnp.int32, (sub_rows, tok_dev.shape[1]), 0)
            hit = jnp.zeros((sub_rows, tok_dev.shape[1]), F32)
            for j in range(tok_dev.shape[0]):
                hit = jnp.maximum(hit, jnp.where(tok_dev[j:j + 1, :] == ids, 1.0, 0.0))
            used = jnp.max(hit, axis=1, keepdims=True)
            h = jnp.where(used > 0.5, rms_f32(x, gain[...]), 0.0)
            hbuf[slot, pl.ds(i * sub_rows, sub_rows), :] = h.astype(BF)
            h_copy(slot, i, row).start()
        hb = hbuf[slot]
        qkv = jnp.concatenate([dotf(hb, wq_v[...]).astype(BF), dotf(hb, wkv_v[...], NT).astype(BF)], axis=1)
        lane = lax.broadcasted_iota(jnp.int32, (1, vrows), 1)
        rowid = jnp.zeros((1, vrows), jnp.int32)
        for i, row in enumerate(rows):
            rowid = jnp.where(lane // sub_rows == i, row + lane - i * sub_rows, rowid)
        for b in range(batch):
            sl = slice(b * seq, (b + 1) * seq)
            hot = jnp.where(idcol[sl, :] == rowid, 1.0, 0.0).astype(BF)
            got = dotf(hot, qkv)
            q_tok[sl, :] = (q_tok[sl, :].astype(F32) + got[:, :qn]).astype(BF)
            kvacc[sl, :] = (kvacc[sl, :].astype(F32) + got[:, qn:]).astype(BF)

    def step_a(e, _):
        @pl.when((e >= 2) & (e < events))
        def _():
            for d in (0, 1):
                ring(d, e, e).wait_recv()

        @pl.when(e < events - 2)
        def _():
            for d in (0, 1):
                ring(d, e, e + 2).start()

        @pl.when(e < events)
        def _():
            for d in (0, 1):
                side(d, e).start()

        @pl.when(e == 1)
        def _():
            for c in ld[1:]:
                c.wait()
            for d in (0, 1):
                for k in (0, 1):
                    g_home(d, k).start()

        @pl.when(e == events - 2)
        def _():
            for d in (0, 1):
                g_ring(d, 0, 2, True).start()

        @pl.when(e >= 1)
        def _():
            for d in (0, 1):
                side(d, e - 1).wait_recv()
            work(e - 1)
        return 0

    lax.fori_loop(0, events + 1, step_a, 0)

    own = 2 * par + core
    opp = 2 * (1 - par) + core
    low = lax.broadcasted_iota(jnp.int32, (toks // 2, 4 * kn), 1) < 2 * kn
    kvx[own] = jnp.where(low, kvacc[:toks // 2, :].astype(F32), kvacc[toks // 2:, :].astype(F32)).astype(BF)
    to_far = rdma(kvx.at[own], kvx.at[own], xs.at[0], xr.at[0], far)
    to_sib = rdma(kvx.at[own], kvx.at[own], xs.at[1], xr.at[1], sib)
    relay = rdma(kvx.at[opp], kvx.at[opp], xs.at[2], xr.at[2], sib)
    mine = jnp.broadcast_to(tok_dev[pl.ds(rank, 1), :].astype(F32), (vrows, tok_dev.shape[1]))
    col = mine.T.astype(jnp.int32)
    lanes = lax.broadcasted_iota(jnp.int32, col.shape, 1)
    hot_mine = jnp.concatenate([jnp.where(col == lanes + j * vrows, 1.0, 0.0).astype(BF) for j in range(vocab // vrows)], axis=1)
    to_far.start()
    to_sib.start()
    for d in (0, 1):
        g_ring(d, 1, 3, True).start()
        for k in (0, 1):
            g_side(d, k, True).start()
            g_home(d, k).wait()
    width = min(512, embed.shape[1])

    def pick(j, _):
        cols = pl.ds(pl.multiple_of(j * width, width), width)
        x_out[:, cols] = dotf(hot_mine, table[:, cols]).astype(BF)
        return 0

    lax.fori_loop(0, embed.shape[1] // width, pick, 0)
    to_far.wait_recv()
    relay.start()
    to_sib.wait_recv()
    relay.wait_recv()
    for up in (0, 1):
        acc = None
        for r in range(4):
            l_i = lax.broadcasted_iota(jnp.int32, (4 * kn, 2 * hd), 0) - 2 * kn * up
            m_i = lax.broadcasted_iota(jnp.int32, (4 * kn, 2 * hd), 1)
            is_k = (l_i >= 0) & (l_i < kn) & (m_i == l_i + kn * r)
            is_v = (l_i >= kn) & (l_i < 2 * kn) & (m_i == hd + kn * r + l_i - kn)
            t = dotf(kvx[r], jnp.where(is_k | is_v, 1.0, 0.0).astype(BF))
            acc = t if acc is None else acc + t
        kv_tok[up * (toks // 2):(up + 1) * (toks // 2), :] = acc.astype(BF)
    for b in range(batch):
        sl = slice(b * seq, (b + 1) * seq)
        k_rot[sl, :] = rope_f32(kv_tok[sl, :hd], kg[...], cos[...], sin_s[...]).astype(BF)

    scale = hd ** -0.5
    blk = seq // 2

    def unit(u, _):
        rows = pl.ds(pl.multiple_of((u // heads) * seq, seq), seq)
        cols = pl.ds(pl.multiple_of(lax.rem(u, heads) * hd, hd), hd)
        qr = rope_f32(q_tok[rows, cols], qg[...], cos[...], sin_s[...]).astype(BF)
        q_rot[rows, cols] = qr
        kr = k_rot[rows, :]
        v = kv_tok[rows, hd:]
        for i in (0, 1):
            n = blk * (i + 1)
            s = masked(dotf(qr[i * blk:(i + 1) * blk], kr[:n], NT) * scale, i * blk)
            o = dotf(soft(s).astype(BF), v[:n]).astype(BF)
            o_out[pl.ds(pl.multiple_of((u // heads) * seq + i * blk, blk), blk), cols] = o
        return 0

    def do_work(e):
        slot = lax.rem(e, 2)
        places = [(d, c) for d in (0, 1) for c in (0, 1)]
        for i, (d, c) in enumerate(places):
            g_load(slot, i, d, c, e).wait()
        r = dotf(gbuf[slot], wo_v[...], NT).astype(BF)
        for i, (d, c) in enumerate(places):
            do_out[pl.ds(g_row(d, e, c), pos), :] = r[i * pos:(i + 1) * pos]

    units = batch * heads
    slots = events - 3

    def step_b(e, _):
        @pl.when((e >= 2) & (e < events))
        def _():
            for d in (0, 1):
                g_ring(d, e, e, False).wait_recv()

        @pl.when((e >= 2) & (e < events - 2))
        def _():
            for d in (0, 1):
                g_ring(d, e, e + 2, False).start()

        @pl.when((e >= 2) & (e < events))
        def _():
            for d in (0, 1):
                g_side(d, e, False).start()

        @pl.when((e >= 1) & (e <= events))
        def _():
            for d in (0, 1):
                g_side(d, e - 1, False).wait_recv()
            for i, (d, c) in enumerate([(d, c) for d in (0, 1) for c in (0, 1)]):
                g_load(lax.rem(e - 1, 2), i, d, c, e - 1).start()

        lax.fori_loop(jnp.minimum((e * units) // slots, units), jnp.minimum(((e + 1) * units) // slots, units), unit, 0)

        @pl.when(e >= 2)
        def _():
            do_work(e - 2)
        return 0

    lax.fori_loop(0, events + 2, step_b, 0)

    for c in (to_far, to_sib, relay):
        c.wait_send()

    def drain(e, _):
        @pl.when(e < events - 2)
        def _():
            for d in (0, 1):
                ring(d, e, e + 2).wait_send()
                g_ring(d, e, e + 2, False).wait_send()
        for d in (0, 1):
            side(d, e).wait_send()
            g_side(d, e, False).wait_send()
        return 0

    lax.fori_loop(0, events, drain, 0)
    for slot in (0, 1):
        for i in range(4):
            h_copy(slot, i, row_of(0, 0, core)).wait()


def forward_kernel(nz, embed, gy, wq, wk_t, wv_t, wo, gain, qg, kg, cos, sin_s, tok_dev, tok_seq):
    vrows, d = embed.shape
    vocab = vrows * 2 * nz
    qn, kn = wq.shape[1], wk_t.shape[0]
    hd = qg.shape[1]
    batch, seq = tok_seq.shape
    toks = batch * seq
    ev = 2 * nz
    dma = pltpu.SemaphoreType.DMA

    def arr(*shape):
        return jax.ShapeDtypeStruct(shape, BF)

    return pl.pallas_call(
        functools.partial(ka_body, nz),
        name='forward_kernel',
        out_shape=(arr(vocab, d), arr(toks, d), arr(toks, qn), arr(toks, 2 * hd), arr(toks, qn), arr(toks, hd), arr(toks, qn), arr(toks, qn), arr(vrows, d)),
        in_specs=[ANY] * 6 + [VM] * 7,
        out_specs=(ANY, ANY) + (VM,) * 7,
        scratch_shapes=[pltpu.VMEM((vocab, d), BF), pltpu.VMEM((2, vrows, d), BF), pltpu.VMEM((d, qn), BF), pltpu.VMEM((4 * kn, d), BF), pltpu.VMEM((qn, d), BF),
                        pltpu.VMEM((toks, vrows), jnp.int32), pltpu.VMEM((toks, 4 * kn), BF), pltpu.VMEM((4, toks // 2, 4 * kn), BF), pltpu.VMEM((vrows, d), BF), pltpu.VMEM((2, vrows, d), BF),
                        dma((12,)), dma((2, 4)), dma((2, 4))] + [dma((2, ev))] * 8 + [dma((3,)), dma((3,))],
        compiler_params=pltpu.CompilerParams(collective_id=0, has_side_effects=True, vmem_limit_bytes=62 * 1024 * 1024),
        cost_estimate=pl.CostEstimate(flops=2 * vocab * d * (2 * qn + 4 * kn), bytes_accessed=8 * vocab * d, transcendentals=0),
    )(embed, gy, wq, wk_t, wv_t, wo, gain, qg, kg, cos, sin_s, tok_dev, tok_seq)


def rope_consts(seq, hd):
    inv = np.float32(ROPE_BASE) ** (np.float32(-2.0) * np.arange(hd // 2, dtype=np.float32) / np.float32(hd))
    ang = np.arange(seq, dtype=np.float32)[:, None] * inv.astype(np.float32)[None, :]
    ang = np.concatenate([ang, ang], axis=-1)
    sign = np.where(np.arange(hd) < hd // 2, -1.0, 1.0).astype(np.float32)
    return np.cos(ang).astype(np.float32), (np.sin(ang) * sign).astype(np.float32)


def rope_tables(seq_len, head_dim):
    half_dim = head_dim // 2
    inv_freq = ROPE_BASE ** (-2.0 * jnp.arange(half_dim, dtype=F32) / head_dim)
    angles = jnp.arange(seq_len, dtype=F32)[:, None] * inv_freq[None, :]
    angles = jnp.concatenate([angles, angles], axis=-1)
    return jnp.cos(angles), jnp.sin(angles)


def rms_scale(wide_in, gain_vec):
    return wide_in * lax.rsqrt(jnp.mean(wide_in * wide_in, axis=-1, keepdims=True) + EPS) * gain_vec


def norm_rope(raw_heads, gain_vec, cos_tab, sin_tab):
    normed = rms_scale(raw_heads.astype(F32), gain_vec)
    half_dim = normed.shape[-1] // 2
    rotated = jnp.concatenate([-normed[..., half_dim:], normed[..., :half_dim]], axis=-1)
    return normed * cos_tab[:, None, :] + rotated * sin_tab[:, None, :]


def mm(spec, a, b):
    return jnp.einsum(spec, a, b, preferred_element_type=F32)


def attention_core(q_four, k_rot, v_three):
    seq_len = q_four.shape[1]
    scores = mm('bqgh,bsh->bgqs', q_four, k_rot) * q_four.shape[-1] ** -0.5
    causal = jnp.arange(seq_len)[:, None] >= jnp.arange(seq_len)[None, :]
    attn_prob = jax.nn.softmax(jnp.where(causal, scores, NEG_BIG), axis=-1)
    prob_bf = attn_prob.astype(BF)
    attn_out = mm('bgqs,bsh->bqgh', prob_bf, v_three).astype(BF)
    return attn_prob, prob_bf, attn_out


def attention_grad(attn_prob, prob_bf, q_four, k_rot, v_three, grad_four):
    attn_scale = q_four.shape[-1] ** -0.5
    grad_prob = mm('bqgh,bsh->bgqs', grad_four, v_three)
    grad_values = mm('bgqs,bqgh->bsh', prob_bf, grad_four).astype(BF)
    grad_scores = (attn_prob * (grad_prob - jnp.sum(attn_prob * grad_prob, axis=-1, keepdims=True)) * attn_scale).astype(BF)
    grad_q_rot = mm('bgqs,bsh->bqgh', grad_scores, k_rot)
    grad_k_rot = mm('bgqs,bqgh->bsh', grad_scores, q_four)
    return grad_q_rot, grad_k_rot, grad_values


def solution(mesh):
    tp = mesh.shape['tp']

    def local_step(tok_ids, embed_loc, norm_gain, q_gain, k_gain, wq, wk, wv, wo, gy_loc):
        rank = lax.axis_index('tp')
        vrows, d_model = embed_loc.shape
        batch, seq = tok_ids.shape
        seq_dev = seq // tp
        vocab = vrows * tp
        hd = q_gain.shape[0]
        qn = wq.shape[1]
        heads = qn // hd
        kn = wk.shape[1]
        share = hd // kn
        toks = batch * seq
        tok_flat = tok_ids.reshape(toks)

        cos_c, sin_c = rope_consts(seq, hd)
        dev_ids = tok_ids.reshape(batch, tp, seq_dev).transpose(1, 0, 2)
        hidden, gy_all, q_tok, kv_tok, q_rot, k_rot, attn_flat, grad_attn, x_mine = forward_kernel(
            tp // 2, embed_loc, gy_loc.reshape(batch * seq_dev, d_model), wq, wk.T, wv.T, wo, norm_gain[None, :], q_gain[None, :], k_gain[None, :],
            jnp.asarray(cos_c), jnp.asarray(sin_c), dev_ids.reshape(tp, batch * seq_dev), tok_ids)
        onehot = (tok_flat[:, None] == jnp.arange(vocab, dtype=tok_ids.dtype)[None, :]).astype(BF)
        w_all = jnp.concatenate([wq, wk, wv], axis=1)
        swap1 = [(i, i ^ 1) for i in range(tp)]
        swap2 = [(i, i ^ 2) for i in range(tp)]
        odd = (rank & 1) == 1
        far = (rank & 2) == 2
        cos_tab, sin_tab = rope_tables(seq, hd)
        rope_fn = functools.partial(norm_rope, cos_tab=cos_tab, sin_tab=sin_tab)
        _, q_pull = jax.vjp(rope_fn, q_tok.reshape(batch, seq, heads, hd), q_gain)
        _, k_pull = jax.vjp(rope_fn, kv_tok[:, :hd].reshape(batch, seq, 1, hd), k_gain)
        q_four = q_rot.reshape(batch, seq, heads, hd)
        k_rot = k_rot.reshape(batch, seq, hd)
        v_three = kv_tok[:, hd:].reshape(batch, seq, hd)
        attn_prob, prob_bf, _ = attention_core(q_four, k_rot, v_three)
        attn_dev = attn_flat.reshape(batch, tp, seq_dev, qn).transpose(1, 0, 2, 3).reshape(toks, qn)

        out_part = mm('tn,nd->td', attn_dev, wo).astype(BF)
        attn_sum = lax.psum_scatter(out_part, 'tp', scatter_dimension=0, tiled=True)
        y_loc = (x_mine.astype(F32) + attn_sum.astype(F32)).astype(BF).reshape(batch, seq_dev, d_model)

        gw_out = mm('tn,td->nd', attn_flat, gy_all)
        grad_four = grad_attn.reshape(batch, seq, heads, hd)
        gq_rot, gk_rot, g_val = attention_grad(attn_prob, prob_bf, q_four, k_rot, v_three, grad_four)
        gq_raw, gq_gain = q_pull(gq_rot.astype(BF).astype(F32))
        gk_raw, gk_gain = k_pull(gk_rot.astype(BF).astype(F32)[:, :, None])
        gkv_tok = jnp.concatenate([gk_raw.reshape(toks, hd), g_val.reshape(toks, hd)], axis=1)
        gq_rows = mm('tr,tn->rn', onehot, gq_raw.reshape(toks, qn)).astype(BF)
        gkv_t = mm('tn,tr->nr', gkv_tok, onehot).reshape(2, share, kn, vocab).transpose(1, 0, 2, 3)
        gkv_t = gkv_t.reshape(2, 2, 2 * kn, vocab)
        mine1 = jnp.where(odd, gkv_t[:, 1], gkv_t[:, 0])
        send1 = jnp.where(odd, gkv_t[:, 0], gkv_t[:, 1]).astype(BF)
        half = mine1 + lax.ppermute(send1, 'tp', swap1).astype(F32)
        mine2 = jnp.where(far, half[1], half[0])
        send2 = jnp.where(far, half[0], half[1]).astype(BF)
        gkv_rows = (mine2 + lax.ppermute(send2, 'tp', swap2).astype(F32)).astype(BF).T
        g_rows = jnp.concatenate([gq_rows, gkv_rows], axis=1)
        gh_part = mm('rn,dn->rd', g_rows, w_all).astype(BF)
        gh = lax.psum_scatter(gh_part, 'tp', scatter_dimension=0, tiled=True)
        gw_query = mm('rd,rn->dn', hidden, gq_rows)
        gw_kv = mm('rd,rn->dn', hidden, gkv_rows)
        my_rows = rank * vrows + jnp.arange(vrows, dtype=tok_ids.dtype)
        mine_hot = (my_rows[:, None] == tok_flat[None, :]).astype(BF)
        gy_rows = lax.optimization_barrier(mm('rt,td->rd', mine_hot, gy_all))
        _, norm_pull = jax.vjp(rms_scale, embed_loc.astype(F32), norm_gain)
        gx_norm, gn_gain = norm_pull(gh.astype(F32))
        g_embed = lax.optimization_barrier(gy_rows) + gx_norm
        gains = jnp.concatenate([gn_gain, gq_gain, gk_gain])
        gains = jnp.sum(lax.all_gather(gains, 'tp', axis=0, tiled=False), axis=0)
        return (y_loc, g_embed, gains[:d_model], gains[d_model:d_model + hd], gains[d_model + hd:], gw_query, gw_kv[:, :kn], gw_kv[:, kn:], gw_out)

    in_specs = (P('dp', None), P('tp', None), P(), P(), P(), P(None, 'tp'), P(None, 'tp'), P(None, 'tp'), P('tp', None), P('dp', 'tp', None))
    out_specs = (P('dp', 'tp', None), P(('dp', 'tp'), None), P('dp'), P('dp'), P('dp'), P('dp', 'tp'), P('dp', 'tp'), P('dp', 'tp'), P(('dp', 'tp'), None))
    return jax.shard_map(local_step, mesh=mesh, in_specs=in_specs, out_specs=out_specs, check_vma=False)
```

time: 477 us -> 517 us (1.084)
  Pallas kernels: 106 us -> 193 us
  matrix products: 196 us -> 161 us
  waiting for transfers between devices: 60.7 us -> 51.1 us
    pallas_call x1, Pallas kernels: 106 us -> 193 us  [forward_kernel(): pl.pallas_call(functools.partial(ka_body, nz), name='forward_kernel', out...]
    dot_general x16 -> x12, matrix products: 185 us -> 151 us  [mm(): return jnp.einsum(spec, a, b, preferred_element_type=F32)]
    all_gather x1 -> x0, waiting for transfers between devices: 8.66 us -> none  [local_step(): lax.all_gather(gy_in, 'tp', axis=0, tiled=False).reshape(toks, d_model)]
    reshape x3 -> x4, local copies, waits for them, and re-layouts: 6.86 us -> 12.6 us  [the longest x2 8.21 us: local_step(): q_four = q_rot.reshape(batch, seq, heads, hd)]
    convert_element_type x6 -> x5, local copies, waits for them, and re-layouts: 16.7 us -> 16.3 us  [norm_rope(): normed = rms_scale(raw_heads.astype(F32), gain_vec)]
  transfers between devices with their start and end apart: 5 -> 4, of which waited for: 3 -> 1; matrix products, arithmetic and copies ran while one was open for 54% -> 40% of each run, Pallas kernels for 0% -> 0%
where the time goes in v3:
time: 517 us; the launch traced here: 507 us
  Pallas kernels  193 us (37%)
  matrix products  161 us (31%)
  waiting for transfers between devices  51.1 us (10%)
  local copies, waits for them, and re-layouts  36.8 us (7%)
  other arithmetic  31.6 us (6%)
  blocking collectives  17.5 us (3%)
  between operations  15 us (3%)
    pallas_call x1, Pallas kernels, forward_kernel(): pl.pallas_call(functools.partial(ka_body, nz), name='forward_kernel', out...  193 us
    dot_general x12, matrix products, mm(): return jnp.einsum(spec, a, b, preferred_element_type=F32)  151 us
    reduce_scatter x1, waiting for transfers between devices, local_step(): gh = lax.psum_scatter(gh_part, 'tp', scatter_dimension=0, tiled=True)  51 us
    all_gather x1, blocking collectives, local_step(): gains = jnp.sum(lax.all_gather(gains, 'tp', axis=0, tiled=False), axis=0)  17.5 us
    convert_element_type x5, local copies, waits for them, and re-layouts, norm_rope(): normed = rms_scale(raw_heads.astype(F32), gain_vec)  16.3 us
    sub x1, matrix products, attention_core(): attn_prob = jax.nn.softmax(jnp.where(causal, scores, NEG_BIG), axis=-1)  10.8 us
  transfers between devices with their start and end apart: 4, of which 1 were waited for; matrix products, arithmetic and copies ran while one was open for 40% of the time, Pallas kernels for 0%

profile of v3, /device:TPU:21, one launch (start us, length us, event | category | flops | bytes accessed | tf_op | source)
XLA Modules:
  0.0 507.4 jit_solution(4130515199071241791)
XLA Ops:
  7.3 0.8 reshape.223
  8.1 0.7 reshape.224.tok_dev
  8.7 192.8 %forward_kernel.1 = (bf16[2048,4096]{1,0:T(8,128)(2,1)}, bf16[2048,4096]{1,0:T(8,128)(2,1)}, bf16[2048,512]{1,0:T(8,128)(2,1)}, bf16[2048,256]{1,0:T(8,128)(2,1)...) custom-call(bf16[128,4096]{1,0:T(8,128)(2,1)} %embed.1, ...), custom_call_target="tpu_custom_call" | custom-call | flops 19327352832 | bytes 67108864 | tf_op jit(solution)/shard_map/forward_kernel/pallas_call | solution.py:348
  201.6 1.9 copy.110
  203.5 0.9 copy-done.13
  204.4 11.6 %convolution_convert_fusion.1 = bf16[2048,4096]{1,0:T(8,128)(2,1)} fusion(bf16[2048,512]{1,0:T(8,128)(2,1)S(1)} %bitcast.177, bf16[512,4096]{1,0:T(8,128)(2,1)S(1)} %copy-done.13), kind=kOutput, calls=%fused_computation.13 | convolution fusion | flops 8598323200 | bytes 23068672 | tf_op jit(solution)/shard_map/tn,nd->td/dot_general | solution.py:390
  216.1 0.3 reduce-scatter.5.cloned.1.call-start
  216.3 0.3 copy-done.10
  216.7 0.5 copy-done.4
  217.2 0.3 multiply_reduce_fusion.5
  217.6 0.9 fusion.85
  218.6 0.3 copy.122
  218.9 2.6 reshape.231
  221.5 4.0 reshape.229
  225.4 4.3 copy.120
  229.7 0.8 iota_compare_fusion.5
  230.5 0.1 iota_multiply_fusion
  230.5 1.6 fusion.71
  232.2 9.2 %fusion.39 = f32[4,512,512,4]{2,1,3,0:T(8,128)} fusion(bf16[4,512,128,1]{2,1,3,0:T(8,128)(2,1)} %bitcast.173, bf16[4,512,4,128]{3,2,1,0:T(4,128)(2,1)S(1)} %reshape.231), kind=kOutput, calls=%fused_computation.62 | convolution fusion | flops 1073741824 | bytes 19398656 | tf_op jit(solution)/shard_map/bqgh,bsh->bgqs/dot_general | solution.py:390
  241.3 10.8 %fusion.87 = (f32[4,4,512]{2,1,0:T(4,128)S(1)}, f32[4,4,512,512]{2,3,1,0:T(8,128)}) fusion(pred[512,512]{0,1:T(8,128)(4,1)} %iota_compare_fusion.5, bf16[4,512,128,1]{2,1,3,0:T(8,128)(2,1)} %bitcast.192, bf16[4,512,4,128]{1,3,2,0:T(8,128)(2,1)} %copy.120), kind=kOutput, calls=%fused_computation.128 | convolution fusion | flops 1090519552 | bytes 19693568 | tf_op jit(solution)/shard_map/sub | solution.py:397
  252.2 23.7 %fusion.54 = bf16[4,512,128]{1,2,0:T(8,128)(2,1)} fusion(bf16[4,512,4,128]{1,3,2,0:T(8,128)(2,1)} %copy.120, f32[4,512,512,4]{2,1,3,0:T(8,128)} %fusion.39, f32[4,4,512,512]{2,3,1,0:T(8,128)} %get-tuple-element.46, f32[4,4,512]{2,1,0:T(4,128)S(1)} %get-tuple-element.45), kind=kOutput, calls=%fused_computation.71 | convolution fusion | flops 1103372800 | bytes 36208640 | tf_op jit(solution)/shard_map/bgqs,bqgh->bsh/dot_general | solution.py:390
  275.9 1.3 fusion.58
  277.2 0.1 fusion.84
  277.3 0.4 multiply_reduce_fusion.3
  277.7 1.2 fusion.59
  279.0 1.3 copy.123
  280.3 8.1 %fusion.49 = bf16[4,512,128]{2,1,0:T(8,128)(2,1)S(1)} fusion(bf16[4,512,4,128]{3,2,1,0:T(4,128)(2,1)S(1)} %reshape.231, f32[4,4,512,512]{2,3,1,0:T(8,128)} %get-tuple-element.46, f32[4,4,512]{2,1,0:T(4,128)S(1)} %get-tuple-element.45), kind=kOutput, calls=%fused_computation.70 | convolution fusion | flops 1082392576 | bytes 19431424 | tf_op jit(solution)/shard_map/bgqs,bqgh->bsh/dot_general | solution.py:390
  288.4 3.7 fusion.5
  292.1 0.1 copy.125
  292.2 0.9 fusion.65
  293.1 0.3 collective-permute-start
  293.4 5.2 %reshape.237 = f32[4,512,4,128]{3,2,1,0:T(4,128)} reshape(bf16[2048,512]{1,0:T(8,128)(2,1)} %get-tuple-element.25) | data formatting | bytes 6291456 | tf_op jit(solution)/shard_map/jvp()/convert_element_type | solution.py:383
  298.5 5.2 %copy.117 = f32[4,512,4,128]{1,3,2,0:T(8,128)} copy(f32[4,512,4,128]{3,2,1,0:T(4,128)} %reshape.237) | data formatting | bytes 8388608 | tf_op jit(solution)/shard_map/jvp()/convert_element_type | solution.py:383
  303.7 4.5 multiply_reduce_fusion.2
  308.2 0.3 copy.115
  308.6 25.2 %bitcast_multiply_fusion.6 = (f32[4,512,4,128]{1,3,2,0:T(8,128)}, bf16[4,128,4,512]{3,1,2,0:T(8,128)(2,1)}) fusion(f32[512,128]{0,1:T(8,128)} %get-tuple-element.42, bf16[4,512,128,1]{2,1,3,0:T(8,128)(2,1)} %bitcast.193, f32[4,512,512,4]{2,1,3,0:T(8,128)} %fusion.39, f32[4,4,512,512]{2,3,1,0:T(8,128)} %get-tuple-element.46, ...), kind=kOutput, calls=%fused_computation.33 | convolution fusion | flops 1106256384 | bytes 40665088 | tf_op jit(solution)/shard_map/bgqs,bsh->bqgh/dot_general | solution.py:390
  333.9 3.2 fusion.82
  337.0 0.3 copy-done
  337.3 0.7 copy-done.2
  338.0 1.9 multiply_reduce_fusion
  339.9 2.7 fusion.23
  342.5 4.2 copy.118
  346.8 1.4 bitcast_add_fusion
  348.1 0.8 fusion.69
  348.9 0.7 collective-permute-start.1
  349.6 6.8 %fusion.26 = bf16[2048,512]{0,1:T(8,128)(2,1)} fusion(s32[2048]{0:T(1024)S(1)} %bitcast.184, bf16[256,8,4,128]{3,2,1,0:T(4,128)(2,1)S(1)} %bitcast.175), kind=kOutput, calls=%fused_computation.45 | convolution fusion | flops 4300210176 | bytes 4202496 | tf_op jit(solution)/shard_map/tr,tn->rn/dot_general | solution.py:390
  356.4 0.5 copy.128
  356.9 0.5 copy.129
  357.4 1.0 fusion.66
  358.4 21.3 %convolution_convert_fusion = bf16[2048,4096]{1,0:T(8,128)(2,1)} fusion(bf16[4096,32]{1,0:T(8,128)(2,1)S(1)} %copy.129, bf16[4096,32]{1,0:T(8,128)(2,1)S(1)} %copy.128, bf16[4096,512]{1,0:T(8,128)(2,1)} %wq.1, bf16[2048,64]{0,1:T(8,128)(2,1)S(1)} %bitcast.178, bf16[2048,512]{0,1:T(8,128)(2,1)} %fusion.26), kind=kOutput, calls=%fused_computation.12 | convolution fusion | flops 9690939392 | bytes 23855104 | tf_op jit(solution)/shard_map/rn,dn->rd/dot_general | solution.py:390
  379.8 8.3 %fusion.63 = f32[128,4096]{1,0:T(8,128)S(1)} fusion(bf16[2048,4096]{1,0:T(8,128)(2,1)} %get-tuple-element.20, s32[2048]{0:T(1024)S(1)} %bitcast.185, s32[128]{0:T(128)S(1)} %iota_add_fusion), kind=kOutput, calls=%fused_computation.88 | convolution fusion | flops 2147745792 | bytes 18883072 | tf_op jit(solution)/shard_map/rt,td->rd/dot_general | solution.py:390
  388.1 0.3 fusion.33
  388.4 15.2 %fusion.89 = f32[512,4096]{1,0:T(8,128)} fusion(bf16[2048,512]{1,0:T(8,128)(2,1)S(1)} %copy-done.5, bf16[2048,4096]{1,0:T(8,128)(2,1)} %get-tuple-element.20), kind=kOutput, calls=%fused_computation.130 | convolution fusion | flops 8589934592 | bytes 27262976 | tf_op jit(solution)/shard_map/tn,td->nd/dot_general | solution.py:390
  403.6 14.5 %fusion.88 = f32[4096,512]{1,0:T(8,128)} fusion(bf16[2048,4096]{1,0:T(8,128)(2,1)S(1)} %bitcast.169, bf16[2048,512]{0,1:T(8,128)(2,1)} %fusion.26), kind=kOutput, calls=%fused_computation.129 | convolution fusion | flops 8589934592 | bytes 27262976 | tf_op jit(solution)/shard_map/rd,rn->dn/dot_general | solution.py:390
  418.1 3.0 fusion.90
  421.2 1.0 fusion.83
  422.2 2.8 add_convert_fusion
  425.0 51.0 %reduce-scatter.5.cloned.1.call-done = bf16[128,4096]{1,0:T(8,128)(2,1)} async-done(((bf16[2048,4096]{1,0:T(8,128)(2,1)}), bf16[128,4096]{1,0:T(8,128)(2,1)}) %reduce-scatter.5.cloned.1.call-update) | async-done | bytes 1048592 | tf_op jit(solution)/shard_map/reduce_scatter | solution.py:472
  475.9 2.1 fusion.31
  478.1 17.5 %all-gather.1 = f32[16,1,4352]{2,1,0:T(1,128)S(1)} all-gather(f32[1,1,4352]{2,1,0:T(1,128)S(1)} %reshape.240), channel_id=2, replica_groups=mesh['dp'=4,'tp'=16] {'tp'}, dimensions={0}, use_global_device_ids=true | all-gather | bytes 295936 | tf_op jit(solution)/shard_map/all_gather | solution.py:482
  495.6 0.2 reduce_sum.125
  495.8 0.5 fusion.86
  496.3 0.6 slice.52
  496.9 3.1 fusion.32
  (52 shorter events, 0.4 us)
Async XLA Ops:
  7.2 415.0 %reduce-scatter.3.cloned.1.call-start = ((), (), s32[]{:S(2)}) async-start(), calls=%async_computation.2 | async-start | bytes 17825792 | tf_op jit(solution)/shard_map/reduce_scatter | solution.py:452
  201.6 2.8 copy-start.13
  216.0 0.7 copy-start.10
  216.0 1.2 copy-start.4
  216.1 259.9 %reduce-scatter.5.cloned.1.call-start = ((), (), s32[]{:S(2)}) async-start(), calls=%async_computation.3 | async-start | bytes 17825792 | tf_op jit(solution)/shard_map/reduce_scatter | solution.py:472
  252.2 25.1 %copy-start.12 = (f32[128]{0:T(128)S(1)}, f32[128]{0:T(128)}, u32[]{:S(2)}) copy-start(f32[128]{0:T(128)} %param.16) | copy-start | bytes 1540
  275.9 1.4 copy-start.3
  293.1 53.7 %collective-permute-start = (bf16[2,64,2048]{2,1,0:T(8,128)(2,1)}, bf16[2,64,2048]{2,1,0:T(8,128)(2,1)}, u32[]{:S(2)}, u32[]{:S(2)}) collective-permute-start(bf16[2,64,2048]{2,1,0:T(8,128)(2,1)} %fusion.65), channel_id=1, source_target_pairs={{0,1},{1,0},{2,3},{3,2},{4,5},{5,4},{6,7},{7,6},{8,9},{9,8},{10,11... | collective-permute-start | bytes 1572872 | tf_op jit(solution)/shard_map/ppermute | solution.py:466
  333.8 3.5 copy-start
  333.8 4.1 copy-start.2
  333.9 4.1 copy-start.11
  346.8 2.8 copy-start.6
  348.9 8.4 %collective-permute-start.1 = (bf16[64,2048]{1,0:T(8,128)(2,1)}, bf16[64,2048]{1,0:T(8,128)(2,1)}, u32[]{:S(2)}, u32[]{:S(2)}) collective-permute-start(bf16[64,2048]{1,0:T(8,128)(2,1)} %fusion.69), channel_id=1, source_target_pairs={{0,2},{1,3},{2,0},{3,1},{4,6},{5,7},{6,4},{7,5},{8,10},{9,11},{10,... | collective-permute-start | bytes 786440 | tf_op jit(solution)/shard_map/ppermute | solution.py:469
  349.6 6.8 %copy-start.7 = (bf16[4096,32]{0,1:T(8,128)(2,1)S(1)}, bf16[4096,32]{0,1:T(8,128)(2,1)}, u32[]{:S(2)}) copy-start(bf16[4096,32]{0,1:T(8,128)(2,1)} %param.18) | copy-start | bytes 786436
  349.6 7.3 %copy-start.8 = (bf16[4096,32]{0,1:T(8,128)(2,1)S(1)}, bf16[4096,32]{0,1:T(8,128)(2,1)}, u32[]{:S(2)}) copy-start(bf16[4096,32]{0,1:T(8,128)(2,1)} %param.19) | copy-start | bytes 786436
  379.7 8.3 %copy-start.1 = (bf16[128,4096]{1,0:T(8,128)(2,1)S(1)}, bf16[128,4096]{1,0:T(8,128)(2,1)}, u32[]{:S(2)}) copy-start(bf16[128,4096]{1,0:T(8,128)(2,1)} %embed.1) | copy-start | bytes 3145732
  379.7 8.6 %copy-start.5 = (bf16[2048,512]{1,0:T(8,128)(2,1)S(1)}, bf16[2048,512]{1,0:T(8,128)(2,1)}, u32[]{:S(2)}) copy-start(bf16[2048,512]{1,0:T(8,128)(2,1)} %get-tuple-element.19) | copy-start | bytes 6291460
  379.8 23.8 %slice-start = ((s8[16777216]{0:T(1024)(128)(4,1)}), s8[4194304]{0:T(1024)(128)(4,1)S(1)}, s32[]{:S(2)}) async-start(s8[16777216]{0:T(1024)(128)(4,1)} %bitcast.168), calls=%async_computation.4 | async-start | bytes 8388608
  379.8 23.8 %slice-start.1 = ((s8[16777216]{0:T(1024)(128)(4,1)}), s8[4194304]{0:T(1024)(128)(4,1)S(1)}, s32[]{:S(2)}) async-start(s8[16777216]{0:T(1024)(128)(4,1)} %bitcast.168), calls=%async_computation.5 | async-start | bytes 8388608
  388.4 15.2 %slice-start.2 = ((s8[16777216]{0:T(1024)(128)(4,1)}), s8[4194304]{0:T(1024)(128)(4,1)S(1)}, s32[]{:S(2)}) async-start(s8[16777216]{0:T(1024)(128)(4,1)} %bitcast.168), calls=%async_computation.6 | async-start | bytes 8388608
  388.4 15.2 %slice-start.3 = ((s8[16777216]{0:T(1024)(128)(4,1)}), s8[4194304]{0:T(1024)(128)(4,1)S(1)}, s32[]{:S(2)}) async-start(s8[16777216]{0:T(1024)(128)(4,1)} %bitcast.168), calls=%async_computation.7 | async-start | bytes 8388608
  421.1 54.8 %copy-start.9 = (f32[4096]{0:T(1024)S(1)}, f32[4096]{0:T(1024)}, u32[]{:S(2)}) copy-start(f32[4096]{0:T(1024)} %param.14) | copy-start | bytes 49156
Sparse Core Ops, SparseCore 0:
  216.2 95.0 reduce-scatter.2
  379.8 96.0 reduce-scatter.4

commit v4 on v3

--- a/solution.py
+++ b/solution.py
@@ -1,12 +1,11 @@
 import functools
 import jax
+import jax.numpy as jnp
 import numpy as np
-import jax.numpy as jnp
 from jax import lax
 from jax.experimental import pallas as pl
 from jax.experimental.pallas import tpu as pltpu
 from jax.sharding import PartitionSpec as P
-
 
 BF = jnp.bfloat16
 F32 = jnp.float32
@@ -57,9 +56,9 @@
 
 
 def ka_body(nz, embed, gy, wq, wk_t, wv_t, wo, gain, qg, kg, cos, sin_s, tok_dev, tok_seq,
-            h_out, gy_out, q_tok, kv_tok, q_rot, k_rot, o_out, do_out, x_out,
-            table, hbuf, wq_v, wkv_v, wo_v, idcol, kvacc, kvx, gown, gbuf,
-            in_sem, h_sem, g_sem, rs, rr, ss, sr, rs2, rr2, ss2, sr2, xs, xr):
+            h_out, gy_out, osib_out, wosib_out, wqt_out, wqtsib_out, wkvsib_out, q_tok, kv_tok, q_rot, k_rot, o_out, do_out, x_out,
+            table, hbuf, wq_v, wkv_v, wo_v, idcol, kvacc, kvx, gown, gbuf, tbuf,
+            in_sem, h_sem, g_sem, rs, rr, ss, sr, rs2, rr2, ss2, sr2, xs, xr, ts, wos, wor, wqs, wqr, wks, wkr, os_, or_):
     rank = lax.axis_index('tp')
     z, core = rank // 2, lax.rem(rank, 2)
     right = 2 * lax.rem(z + 1, nz) + core
@@ -130,6 +129,28 @@
 
     def g_load(slot, i, d, c, e):
         return pltpu.make_async_copy(g_piece(d, e, c), gbuf.at[slot, pl.ds(i * pos, pos)], g_sem.at[slot, i])
+
+    parts = 8
+    wo_p, wq_p = qn // parts, embed.shape[1] // parts
+
+    def wo_push(k):
+        rows = pl.ds(pl.multiple_of(k * wo_p, wo_p), wo_p)
+        return rdma(wo.at[rows], wosib_out.at[rows], wos.at[k], wor.at[k], sib)
+
+    def wq_push(k):
+        cols = pl.ds(pl.multiple_of(k * wq_p, wq_p), wq_p)
+        return rdma(tbuf.at[lax.rem(k, 2)], wqtsib_out.at[:, cols], wqs.at[k], wqr.at[k], sib)
+
+    def wq_home(k):
+        cols = pl.ds(pl.multiple_of(k * wq_p, wq_p), wq_p)
+        return pltpu.make_async_copy(tbuf.at[lax.rem(k, 2)], wqt_out.at[:, cols], ts.at[k])
+
+    def wk_push(k):
+        return rdma((wk_t, wv_t)[k], wkvsib_out.at[pl.ds(k * kn, kn)], wks.at[k], wkr.at[k], sib)
+
+    def o_push(b):
+        rows = pl.ds(pl.multiple_of(b * seq, seq), seq)
+        return rdma(o_out.at[rows], osib_out.at[rows], os_.at[b], or_.at[b], sib)
 
     for b in range(batch):
         wide = jnp.broadcast_to(tok_seq[b:b + 1, :].astype(F32), (idcol.shape[1], seq))
@@ -198,6 +219,25 @@
             for d in (0, 1):
                 g_ring(d, 0, 2, True).start()
 
+        @pl.when((e >= 2) & (e < 2 + parts))
+        def _():
+            k = e - 2
+
+            @pl.when(k >= 2)
+            def _():
+                wq_push(k - 2).wait_send()
+                wq_home(k - 2).wait()
+            block = wq_v[pl.ds(pl.multiple_of(k * wq_p, wq_p), wq_p), :]
+            tbuf[lax.rem(k, 2)] = block.astype(F32).T.astype(BF)
+            wo_push(k).start()
+            wq_push(k).start()
+            wq_home(k).start()
+
+        @pl.when(e == 2 + parts)
+        def _():
+            for k in (0, 1):
+                wk_push(k).start()
+
         @pl.when(e >= 1)
         def _():
             for d in (0, 1):
@@ -303,6 +343,11 @@
             for i, (d, c) in enumerate([(d, c) for d in (0, 1) for c in (0, 1)]):
                 g_load(lax.rem(e - 1, 2), i, d, c, e - 1).start()
 
+        def give(b, _):
+            o_push(b).start()
+            return 0
+
+        lax.fori_loop(jnp.minimum((jnp.maximum(e - 1, 0) * units) // slots, units) // heads, jnp.minimum((e * units) // slots, units) // heads, give, 0)
         lax.fori_loop(jnp.minimum((e * units) // slots, units), jnp.minimum(((e + 1) * units) // slots, units), unit, 0)
 
         @pl.when(e >= 2)
@@ -314,6 +359,16 @@
 
     for c in (to_far, to_sib, relay):
         c.wait_send()
+    for k in range(parts):
+        if k >= parts - 2:
+            wq_push(k).wait_send()
+            wq_home(k).wait()
+        wq_push(k).wait_recv()
+        wo_push(k).wait()
+    for k in (0, 1):
+        wk_push(k).wait()
+    for b in range(batch):
+        o_push(b).wait()
 
     def drain(e, _):
         @pl.when(e < events - 2)
@@ -348,12 +403,12 @@
     return pl.pallas_call(
         functools.partial(ka_body, nz),
         name='forward_kernel',
-        out_shape=(arr(vocab, d), arr(toks, d), arr(toks, qn), arr(toks, 2 * hd), arr(toks, qn), arr(toks, hd), arr(toks, qn), arr(toks, qn), arr(vrows, d)),
+        out_shape=(arr(vocab, d), arr(toks, d), arr(toks, qn), arr(qn, d), arr(qn, d), arr(qn, d), arr(2 * kn, d), arr(toks, qn), arr(toks, 2 * hd), arr(toks, qn), arr(toks, hd), arr(toks, qn), arr(toks, qn), arr(vrows, d)),
         in_specs=[ANY] * 6 + [VM] * 7,
-        out_specs=(ANY, ANY) + (VM,) * 7,
+        out_specs=(ANY,) * 7 + (VM,) * 7,
         scratch_shapes=[pltpu.VMEM((vocab, d), BF), pltpu.VMEM((2, vrows, d), BF), pltpu.VMEM((d, qn), BF), pltpu.VMEM((4 * kn, d), BF), pltpu.VMEM((qn, d), BF),
-                        pltpu.VMEM((toks, vrows), jnp.int32), pltpu.VMEM((toks, 4 * kn), BF), pltpu.VMEM((4, toks // 2, 4 * kn), BF), pltpu.VMEM((vrows, d), BF), pltpu.VMEM((2, vrows, d), BF),
-                        dma((12,)), dma((2, 4)), dma((2, 4))] + [dma((2, ev))] * 8 + [dma((3,)), dma((3,))],
+                        pltpu.VMEM((toks, vrows), jnp.int32), pltpu.VMEM((toks, 4 * kn), BF), pltpu.VMEM((4, toks // 2, 4 * kn), BF), pltpu.VMEM((vrows, d), BF), pltpu.VMEM((2, vrows, d), BF), pltpu.VMEM((2, qn, d // 8), BF),
+                        dma((12,)), dma((2, 4)), dma((2, 4))] + [dma((2, ev))] * 8 + [dma((3,)), dma((3,))] + [dma((8,))] * 5 + [dma((2,)), dma((2,)), dma((batch,)), dma((batch,))],
         compiler_params=pltpu.CompilerParams(collective_id=0, has_side_effects=True, vmem_limit_bytes=62 * 1024 * 1024),
         cost_estimate=pl.CostEstimate(flops=2 * vocab * d * (2 * qn + 4 * kn), bytes_accessed=8 * vocab * d, transcendentals=0),
     )(embed, gy, wq, wk_t, wv_t, wo, gain, qg, kg, cos, sin_s, tok_dev, tok_seq)
@@ -367,120 +422,477 @@
     return np.cos(ang).astype(np.float32), (np.sin(ang) * sign).astype(np.float32)
 
 
-def rope_tables(seq_len, head_dim):
-    half_dim = head_dim // 2
-    inv_freq = ROPE_BASE ** (-2.0 * jnp.arange(half_dim, dtype=F32) / head_dim)
-    angles = jnp.arange(seq_len, dtype=F32)[:, None] * inv_freq[None, :]
-    angles = jnp.concatenate([angles, angles], axis=-1)
-    return jnp.cos(angles), jnp.sin(angles)
-
-
-def rms_scale(wide_in, gain_vec):
-    return wide_in * lax.rsqrt(jnp.mean(wide_in * wide_in, axis=-1, keepdims=True) + EPS) * gain_vec
-
-
-def norm_rope(raw_heads, gain_vec, cos_tab, sin_tab):
-    normed = rms_scale(raw_heads.astype(F32), gain_vec)
-    half_dim = normed.shape[-1] // 2
-    rotated = jnp.concatenate([-normed[..., half_dim:], normed[..., :half_dim]], axis=-1)
-    return normed * cos_tab[:, None, :] + rotated * sin_tab[:, None, :]
-
-
-def mm(spec, a, b):
-    return jnp.einsum(spec, a, b, preferred_element_type=F32)
-
-
-def attention_core(q_four, k_rot, v_three):
-    seq_len = q_four.shape[1]
-    scores = mm('bqgh,bsh->bgqs', q_four, k_rot) * q_four.shape[-1] ** -0.5
-    causal = jnp.arange(seq_len)[:, None] >= jnp.arange(seq_len)[None, :]
-    attn_prob = jax.nn.softmax(jnp.where(causal, scores, NEG_BIG), axis=-1)
-    prob_bf = attn_prob.astype(BF)
-    attn_out = mm('bgqs,bsh->bqgh', prob_bf, v_three).astype(BF)
-    return attn_prob, prob_bf, attn_out
-
-
-def attention_grad(attn_prob, prob_bf, q_four, k_rot, v_three, grad_four):
-    attn_scale = q_four.shape[-1] ** -0.5
-    grad_prob = mm('bqgh,bsh->bgqs', grad_four, v_three)
-    grad_values = mm('bgqs,bqgh->bsh', prob_bf, grad_four).astype(BF)
-    grad_scores = (attn_prob * (grad_prob - jnp.sum(attn_prob * grad_prob, axis=-1, keepdims=True)) * attn_scale).astype(BF)
-    grad_q_rot = mm('bgqs,bsh->bqgh', grad_scores, k_rot)
-    grad_k_rot = mm('bgqs,bqgh->bsh', grad_scores, q_four)
-    return grad_q_rot, grad_k_rot, grad_values
+def kb_body(nz, o_own, o_sib, wo, wo_sib, wqt, wqt_sib, wk_t, wv_t, wkv_sib, gy, hid, q_in, kv_tok, qr_in, k_rot, do_in, x_mine, embed,
+            gain, qg, kg, cos, sin_s, tok_seq,
+            y_out, ge_out, gq_out, gkv_out, gwo_out, gains_out,
+            opair, wpair, qt, qr, gd, d_rows, kvrow, sq, skv, part, lhs, rbuf, sbuf, gblk, hblk, swo, swq, hotm, dk_acc, dv_acc, pk, rk1, fk, hk, rk2, kvt, gn, qga, kga, gall,
+            in_sem, rs, rr, p1s, p1r, p2s, p2r, qs, qv, gls, hls, wos, wqs, gs, gr):
+    rank = lax.axis_index('tp')
+    z, core = rank // 2, lax.rem(rank, 2)
+    right = 2 * lax.rem(z + 1, nz) + core
+    left = 2 * lax.rem(z + nz - 1, nz) + core
+    sib = rank + 1 - 2 * core
+    par = lax.rem(z, 2)
+    far = rank + 2 - 4 * par
+    vrows, d = embed.shape
+    kn = wk_t.shape[0]
+    half, sub_rows = vrows // 2, vrows // 4
+    vocab = vrows * 2 * nz
+    batch, seq = tok_seq.shape
+    toks = batch * seq
+    qn = q_in.shape[1]
+    hd = qg.shape[1]
+    heads = qn // hd
+    events = 2 * nz
+    pos = seq // (2 * nz)
+    blk = seq // 2
+    scale = hd ** -0.5
+    cw = min(512, d)
+    bw = d // events
+
+    ld = [pltpu.make_async_copy(s, t, in_sem.at[i]) for i, (s, t) in enumerate((
+        (wo, wpair.at[pl.ds(0, qn)]), (wo_sib, wpair.at[pl.ds(qn, qn)]), (o_own, opair.at[0]), (o_sib, opair.at[1]),
+        (q_in, qt), (qr_in, qr), (do_in, gd),
+        (wk_t, wpair.at[pl.ds(2 * qn, kn)]), (wv_t, wpair.at[pl.ds(2 * qn + kn, kn)]), (wkv_sib, wpair.at[pl.ds(2 * qn + 2 * kn, 2 * kn)])))]
+    ld2 = [pltpu.make_async_copy(s, t, in_sem.at[10 + i]) for i, (s, t) in enumerate((
+        (wqt, wpair.at[pl.ds(0, qn)]), (wqt_sib, wpair.at[pl.ds(qn, qn)])))]
+    for c in ld:
+        c.start()
+    barrier = pltpu.get_barrier_semaphore()
+    for k in range(1, 2 * nz):
+        pl.semaphore_signal(barrier, inc=1, device_id={'tp': lax.rem(rank + k, 2 * nz)}, device_id_type=MESH)
+    pl.semaphore_wait(barrier, 2 * nz - 1)
+
+    def zd_of(dr, s):
+        return lax.rem(z + (2 * nz - 1 - s if dr == 0 else 1 + s), nz)
+
+    def send(ph, dr, e):
+        sl = sbuf.at[ph, lax.rem(e // 2, 2), dr, lax.rem(e, 2)]
+        return rdma(sl, rbuf.at[dr, e], rs.at[ph, dr, e], rr.at[ph, dr, e], right if dr == 0 else left)
+
+    pieces = [(dr, sub) for dr in (0, 1) for sub in (0, 1)]
+
+    def times(k):
+        def tile(j, _):
+            cols = pl.ds(pl.multiple_of(j * cw, cw), cw)
+            part[:, cols] = dotf(lhs[:, :k], wpair[:k, cols])
+            return 0
+        lax.fori_loop(0, d // cw, tile, 0)
+
+    def part_y(s):
+        for i, (dr, sub) in enumerate(pieces):
+            row = pl.multiple_of(seq * (2 * dr + sub) + pos * (2 * zd_of(dr, s) + core), pos)
+            lhs[i * pos:(i + 1) * pos, :qn] = opair[0, pl.ds(row, pos), :]
+            lhs[i * pos:(i + 1) * pos, qn:2 * qn] = opair[1, pl.ds(row, pos), :]
+        times(2 * qn)
+
+    def part_h(s):
+        for i, (dr, sub) in enumerate(pieces):
+            zd = zd_of(dr, s)
+            off = half * dr + sub_rows * sub
+            row = pl.multiple_of(vrows * (2 * zd + core) + off, sub_rows)
+            row2 = pl.multiple_of(vrows * zd + off, sub_rows)
+            at = slice(i * sub_rows, (i + 1) * sub_rows)
+            lhs[at, :qn] = qt[pl.ds(row, sub_rows), :]
+            lhs[at, qn:2 * qn] = sq[pl.ds(row2, sub_rows), :]
+            lhs[at, 2 * qn:] = (kvrow[pl.ds(row, sub_rows), :].astype(F32) + pltpu.roll(skv[pl.ds(row2, sub_rows), :].astype(F32), 2 * kn, 1)).astype(BF)
+        times(2 * qn + 4 * kn)
+
+    def serve(ph, e, final):
+        s, sub = e // 2, lax.rem(e, 2)
+
+        @pl.when(e >= 2)
+        def _():
+            for dr in (0, 1):
+                send(ph, dr, e - 2).wait_recv()
+
+        def mine(dr):
+            return part[pl.ds(pl.multiple_of((2 * dr + sub) * sub_rows, sub_rows), sub_rows), :]
+
+        @pl.when(e < 2)
+        def _():
+            for dr in (0, 1):
+                sbuf[ph, lax.rem(s, 2), dr, sub] = mine(dr).astype(BF)
+
+        @pl.when((e >= 2) & (e < events - 2))
+        def _():
+            @pl.when(e >= 4)
+            def _():
+                for dr in (0, 1):
+                    send(ph, dr, e - 4).wait_send()
+            for dr in (0, 1):
+                sbuf[ph, lax.rem(s, 2), dr, sub] = (mine(dr) + rbuf[dr, e - 2].astype(F32)).astype(BF)
+
+        @pl.when(e < events - 2)
+        def _():
+            for dr in (0, 1):
+                send(ph, dr, e).start()
+
+        @pl.when(e >= events - 2)
+        def _():
+            for dr in (0, 1):
+                final(dr, sub, mine(dr) + rbuf[dr, e - 2].astype(F32))
+
+    def final_y(dr, sub, acc):
+        rows = pl.ds(pl.multiple_of((2 * dr + sub) * pos, pos), pos)
+        y_out[rows, :] = (x_mine[rows, :].astype(F32) + acc).astype(BF)
+
+    def final_h(dr, sub, gh):
+        rows = pl.ds(pl.multiple_of(half * dr + sub_rows * sub, sub_rows), sub_rows)
+        x = embed[rows, :].astype(F32)
+        r = lax.rsqrt(jnp.mean(x * x, axis=-1, keepdims=True) + EPS)
+        dxr = gh * gain[...]
+        ge_out[rows, :] += r * dxr - x * (r * r * r * jnp.mean(x * dxr, axis=-1, keepdims=True))
+        gn[...] += jnp.sum(gh * (x * r), axis=0, keepdims=True)
+
+    def pull(raw, dout, g):
+        x = raw.astype(F32)
+        r = lax.rsqrt(jnp.mean(x * x, axis=-1, keepdims=True) + EPS)
+        dn = dout * cos[...] + pltpu.roll(dout * sin_s[...], hd // 2, 1)
+        dxr = dn * g
+        dx = r * dxr - x * (r * r * r * jnp.mean(x * dxr, axis=-1, keepdims=True))
+        return dx.astype(BF), jnp.sum(dn * (x * r), axis=0, keepdims=True)
+
+    def unit(u):
+        b, h = u // heads, lax.rem(u, heads)
+        rows = pl.ds(pl.multiple_of(b * seq, seq), seq)
+        cols = pl.ds(pl.multiple_of(h * hd, hd), hd)
+
+        @pl.when(h == 0)
+        def _():
+            dk_acc[...] = jnp.zeros_like(dk_acc)
+            dv_acc[...] = jnp.zeros_like(dv_acc)
+        q, g = qr[rows, cols], gd[rows, cols]
+        kr, v = k_rot[rows, :], kv_tok[rows, hd:]
+        dqs = []
+        for i in (0, 1):
+            n = blk * (i + 1)
+            qi, gi = q[i * blk:(i + 1) * blk], g[i * blk:(i + 1) * blk]
+            p = soft(masked(dotf(qi, kr[:n], NT) * scale, i * blk))
+            dp = dotf(gi, v[:n], NT)
+            dv_acc[:n, :] += dotf(p.astype(BF), gi, TN)
+            ds = (p * (dp - jnp.sum(p * dp, axis=-1, keepdims=True)) * scale).astype(BF)
+            dqs.append(dotf(ds, kr[:n]))
+            dk_acc[:n, :] += dotf(ds, qi, TN)
+        dq = jnp.concatenate(dqs, axis=0).astype(BF).astype(F32)
+        dx, dg = pull(qt[rows, cols], dq, qg[...])
+        gd[rows, cols] = dx
+        qga[...] += dg
+
+    def pick(r, up):
+        m_i = lax.broadcasted_iota(jnp.int32, (2 * hd, 4 * kn), 0)
+        l_i = lax.broadcasted_iota(jnp.int32, (2 * hd, 4 * kn), 1) - 2 * kn * up
+        is_k = (l_i >= 0) & (l_i < kn) & (m_i == l_i + kn * r)
+        is_v = (l_i >= kn) & (l_i < 2 * kn) & (m_i == hd + kn * r + l_i - kn)
+        return jnp.where(is_k | is_v, 1.0, 0.0).astype(BF)
+
+    def to_side(b, p):
+        return rdma(pk.at[b, 2 * p + 1 - core], rk1.at[b, p], p1s.at[b, p], p1r.at[b, p], sib)
+
+    def to_far(b):
+        return rdma(fk.at[b], rk2.at[b], p2s.at[b], p2r.at[b], far)
+
+    def kv_one(b):
+        rows = pl.ds(pl.multiple_of(b * seq, seq), seq)
+        dk = dk_acc[...].astype(BF).astype(F32)
+        dx, dg = pull(kv_tok[rows, :hd], dk, kg[...])
+        kga[...] += dg
+        gkv = jnp.concatenate([dx, dv_acc[...].astype(BF)], axis=1)
+        for r in range(4):
+            pk[b, r] = (dotf(gkv[:blk], pick(r, 0)) + dotf(gkv[blk:], pick(r, 1))).astype(BF)
+        for p in (0, 1):
+            to_side(b, p).start()
+
+    def kv_two(b):
+        for p in (0, 1):
+            to_side(b, p).wait_recv()
+        a = pk[b, 2 * (1 - par) + core].astype(F32) + rk1[b, 1 - par].astype(F32)
+        fk[b] = a.astype(BF)
+        hk[b] = pk[b, 2 * par + core].astype(F32) + rk1[b, par].astype(F32)
+        to_far(b).start()
+
+    def kv_three(b):
+        to_far(b).wait_recv()
+        t = hk[b] + rk2[b].astype(F32)
+        low = lax.broadcasted_iota(jnp.int32, t.shape, 1) < 2 * kn
+        kvt[b, :blk, :] = jnp.where(low, t, 0.0).astype(BF)
+        kvt[b, blk:, :] = jnp.where(low, pltpu.roll(t, 2 * kn, 1), 0.0).astype(BF)
+
+    def fold(b, tile):
+        rows = pl.ds(pl.multiple_of(tile * seq, seq), seq)
+        ids = tile * seq + lax.broadcasted_iota(jnp.int32, (seq, seq), 0)
+        hot = jnp.where(ids == tok_seq[pl.ds(b, 1), :], 1.0, 0.0).astype(BF)
+        d_rows[rows, :qn] += dotf(hot, gd[pl.ds(pl.multiple_of(b * seq, seq), seq), :])
+        d_rows[rows, qn:] += dotf(hot, kvt[b])
+
+    def g_load(j):
+        return pltpu.make_async_copy(gy.at[:, pl.ds(pl.multiple_of(j * bw, bw), bw)], gblk.at[lax.rem(j, 2)], gls.at[lax.rem(j, 2)])
+
+    def h_load(j):
+        return pltpu.make_async_copy(hid.at[:, pl.ds(pl.multiple_of(j * bw, bw), bw)], hblk.at[lax.rem(j, 2)], hls.at[lax.rem(j, 2)])
+
+    def wo_store(j):
+        return pltpu.make_async_copy(swo.at[lax.rem(j, 2)], gwo_out.at[:, pl.ds(pl.multiple_of(j * bw, bw), bw)], wos.at[lax.rem(j, 2)])
+
+    def wq_store(j):
+        return pltpu.make_async_copy(swq.at[lax.rem(j, 2)], gq_out.at[pl.ds(pl.multiple_of(j * bw, bw), bw)], wqs.at[lax.rem(j, 2)])
+
+    def wo_block(j):
+        sl = lax.rem(j, 2)
+        g_load(j).wait()
+
+        @pl.when(j + 1 < events)
+        def _():
+            g_load(j + 1).start()
+
+        @pl.when(j >= 2)
+        def _():
+            wo_store(j - 2).wait()
+        swo[sl] = dotf(opair[0], gblk[sl], TN)
+        ge_out[:, pl.ds(pl.multiple_of(j * bw, bw), bw)] = dotf(hotm[...], gblk[sl])
+        wo_store(j).start()
+
+    def wq_block(j):
+        sl = lax.rem(j, 2)
+        h_load(j).wait()
+
+        @pl.when(j + 1 < events)
+        def _():
+            h_load(j + 1).start()
+
+        @pl.when(j >= 2)
+        def _():
+            wq_store(j - 2).wait()
+        swq[sl] = dotf(hblk[sl], qt[...], TN)
+        gkv_out[:, pl.ds(pl.multiple_of(j * bw, bw), bw)] = dotf(kvrow[...], hblk[sl], TN)[:2 * kn]
+        wq_store(j).start()
+
+    for c in ld[:4]:
+        c.wait()
+    part_y(0)
+    d_rows[...] = jnp.zeros_like(d_rows)
+    for b in range(batch):
+        ids = rank * vrows + lax.broadcasted_iota(jnp.int32, (vrows, seq), 0)
+        hotm[:, b * seq:(b + 1) * seq] = jnp.where(ids == tok_seq[b:b + 1, :], 1.0, 0.0).astype(BF)
+    gn[...] = jnp.zeros_like(gn)
+    qga[...] = jnp.zeros_like(qga)
+    kga[...] = jnp.zeros_like(kga)
+    g_load(0).start()
+    h_load(0).start()
+
+    def phase_y(e, _):
+        serve(0, e, final_y)
+
+        @pl.when((lax.rem(e, 2) == 1) & (e < events - 2))
+        def _():
+            part_y(e // 2 + 1)
+
+        @pl.when(e == events - 3)
+        def _():
+            for c in ld2:
+                c.start()
+
+        @pl.when(e == 0)
+        def _():
+            for c in ld[4:]:
+                c.wait()
+        unit(e)
+        b, h = e // heads, lax.rem(e, heads)
+
+        @pl.when(h == heads - 1)
+        def _():
+            kv_one(b)
+
+        @pl.when(b >= 1)
+        def _():
+            @pl.when(h == 0)
+            def _():
+                kv_two(b - 1)
+
+            @pl.when(h == 1)
+            def _():
+                kv_three(b - 1)
+
+            @pl.when(h >= 2)
+            def _():
+                fold(b - 1, 2 * (h - 2))
+                fold(b - 1, 2 * (h - 2) + 1)
+        return 0
+
+    lax.fori_loop(0, events, phase_y, 0)
+    early = 3
+
+    def blocks(lo, hi, f):
+        def go(j, _):
+            f(j)
+            return 0
+        lax.fori_loop(lo, hi, go, 0)
+
+    blocks(0, 1, wo_block)
+    kv_two(batch - 1)
+    blocks(1, early, wo_block)
+    kv_three(batch - 1)
+
+    def last(t, _):
+        fold(batch - 1, t)
+        return 0
+
+    lax.fori_loop(0, vocab // seq, last, 0)
+
+    def settle(t, _):
+        rows = pl.ds(pl.multiple_of(t * vrows, vrows), vrows)
+        qt[rows, :] = d_rows[rows, :qn].astype(BF)
+        kvrow[rows, :] = d_rows[rows, qn:].astype(BF)
+        return 0
+
+    lax.fori_loop(0, 2 * nz, settle, 0)
+
+    def q_side(k, kk):
+        src = pl.ds(pl.multiple_of(vrows * (2 * k + 1 - core), vrows), vrows)
+        dst = pl.ds(pl.multiple_of(vrows * k, vrows), vrows)
+        return rdma((qt, kvrow)[kk].at[src], (sq, skv)[kk].at[dst], qs.at[kk, k], qv.at[kk, k], sib)
+
+    def swap(k, _):
+        for kk in (0, 1):
+            q_side(k, kk).start()
+        return 0
+
+    lax.fori_loop(0, nz, swap, 0)
+    for c in ld2:
+        c.wait()
+
+    def swapped(k, _):
+        for kk in (0, 1):
+            q_side(k, kk).wait_recv()
+        return 0
+
+    lax.fori_loop(0, nz, swapped, 0)
+    part_h(0)
+
+    def phase_h(e, _):
+        serve(1, e, final_h)
+
+        @pl.when((lax.rem(e, 2) == 1) & (e < events - 2))
+        def _():
+            part_h(e // 2 + 1)
+
+        @pl.when(e < events - 3)
+        def _():
+            @pl.when(e + early < events)
+            def _():
+                wo_block(e + early)
+
+            @pl.when(e < events - 6)
+            def _():
+                wq_block(e)
+
+            @pl.when(e >= events - 6)
+            def _():
+                wq_block(2 * e - events + 6)
+                wq_block(2 * e - events + 7)
+        return 0
+
+    lax.fori_loop(0, events, phase_h, 0)
+
+    wide = gains_out.shape[1]
+    for j in range(d // wide):
+        gall[rank, j:j + 1, :] = gn[:, j * wide:(j + 1) * wide]
+    gall[rank, d // wide:d // wide + 1, :] = qga[...]
+    gall[rank, d // wide + 1:d // wide + 2, :] = kga[...]
+    for j in (events - 2, events - 1):
+        wo_store(j).wait()
+        wq_store(j).wait()
+
+    def spread(k):
+        return rdma(gall.at[rank], gall.at[rank], gs.at[k], gr.at[k], lax.rem(rank + k, 2 * nz))
+
+    def spread_from(k):
+        src = lax.rem(rank + 2 * nz - k, 2 * nz)
+        return rdma(gall.at[src], gall.at[src], gs.at[k], gr.at[k], sib)
+
+    for k in range(1, 2 * nz):
+        spread(k).start()
+
+    def drain(e, _):
+        for dr in (0, 1):
+            @pl.when(e >= events - 6)
+            def _():
+                send(0, dr, e).wait_send()
+                send(1, dr, e).wait_send()
+        return 0
+
+    lax.fori_loop(0, events - 2, drain, 0)
+    for b in range(batch):
+        for p in (0, 1):
+            to_side(b, p).wait_send()
+        to_far(b).wait_send()
+
+    def swept(k, _):
+        for kk in (0, 1):
+            q_side(k, kk).wait_send()
+        return 0
+
+    lax.fori_loop(0, nz, swept, 0)
+    for k in range(1, 2 * nz):
+        spread_from(k).wait_recv()
+    gains_out[...] = jnp.sum(gall[...], axis=0)
+    for k in range(1, 2 * nz):
+        spread(k).wait_send()
+
+
+def backward_kernel(nz, o_own, o_sib, wo, wo_sib, wqt, wqt_sib, wk_t, wv_t, wkv_sib, gy, hid, q_in, kv_tok, qr_in, k_rot, do_in, x_mine, embed, gain, qg, kg, cos, sin_s, tok_seq):
+    vrows, d = embed.shape
+    vocab = vrows * 2 * nz
+    qn, kn = q_in.shape[1], wk_t.shape[0]
+    hd = qg.shape[1]
+    batch, seq = tok_seq.shape
+    toks = batch * seq
+    ev = 2 * nz
+    bw = d // ev
+    grow = (d // hd + 2 + 7) // 8 * 8
+    dma = pltpu.SemaphoreType.DMA
+    v = pltpu.VMEM
+
+    def arr(*shape):
+        return jax.ShapeDtypeStruct(shape, F32)
+
+    return pl.pallas_call(
+        functools.partial(kb_body, nz),
+        name='backward_kernel',
+        out_shape=(jax.ShapeDtypeStruct((vrows, d), BF), arr(vrows, d), arr(d, qn), arr(2 * kn, d), arr(qn, d), arr(grow, hd)),
+        in_specs=[ANY] * 12 + [VM, ANY, VM, ANY] + [VM] * 8,
+        out_specs=(VM, VM, ANY, VM, ANY, VM),
+        scratch_shapes=[v((2, toks, qn), BF), v((2 * qn + 4 * kn, d), BF), v((vocab, qn), BF), v((toks, qn), BF), v((toks, qn), BF), v((vocab, qn + 4 * kn), F32),
+                        v((vocab, 4 * kn), BF), v((vocab // 2, qn), BF), v((vocab // 2, 4 * kn), BF), v((vrows, d), F32), v((vrows, 2 * qn + 4 * kn), BF),
+                        v((2, ev - 2, vrows // 4, d), BF), v((2, 2, 2, 2, vrows // 4, d), BF), v((2, toks, bw), BF), v((2, vocab, bw), BF), v((2, qn, bw), F32), v((2, bw, qn), F32),
+                        v((vrows, toks), BF), v((seq, hd), F32), v((seq, hd), F32), v((batch, 4, seq // 2, 4 * kn), BF), v((batch, 2, seq // 2, 4 * kn), BF), v((batch, seq // 2, 4 * kn), BF),
+                        v((batch, seq // 2, 4 * kn), F32), v((batch, seq // 2, 4 * kn), BF), v((batch, seq, 4 * kn), BF), v((1, d), F32), v((1, hd), F32), v((1, hd), F32), v((ev, grow, hd), F32),
+                        dma((12,)), dma((2, 2, ev - 2)), dma((2, 2, ev - 2)), dma((batch, 2)), dma((batch, 2)), dma((batch,)), dma((batch,)), dma((2, nz)), dma((2, nz)),
+                        dma((2,)), dma((2,)), dma((2,)), dma((2,)), dma((ev,)), dma((ev,))],
+        compiler_params=pltpu.CompilerParams(collective_id=1, has_side_effects=True, vmem_limit_bytes=63 * 1024 * 1024),
+        cost_estimate=pl.CostEstimate(flops=2 * vocab * d * (5 * qn), bytes_accessed=12 * vocab * d, transcendentals=0),
+    )(o_own, o_sib, wo, wo_sib, wqt, wqt_sib, wk_t, wv_t, wkv_sib, gy, hid, q_in, kv_tok, qr_in, k_rot, do_in, x_mine, embed, gain, qg, kg, cos, sin_s, tok_seq)
 
 
 def solution(mesh):
     tp = mesh.shape['tp']
+    nz = tp // 2
 
     def local_step(tok_ids, embed_loc, norm_gain, q_gain, k_gain, wq, wk, wv, wo, gy_loc):
-        rank = lax.axis_index('tp')
         vrows, d_model = embed_loc.shape
         batch, seq = tok_ids.shape
         seq_dev = seq // tp
-        vocab = vrows * tp
         hd = q_gain.shape[0]
-        qn = wq.shape[1]
-        heads = qn // hd
         kn = wk.shape[1]
-        share = hd // kn
-        toks = batch * seq
-        tok_flat = tok_ids.reshape(toks)
-
-        cos_c, sin_c = rope_consts(seq, hd)
-        dev_ids = tok_ids.reshape(batch, tp, seq_dev).transpose(1, 0, 2)
-        hidden, gy_all, q_tok, kv_tok, q_rot, k_rot, attn_flat, grad_attn, x_mine = forward_kernel(
-            tp // 2, embed_loc, gy_loc.reshape(batch * seq_dev, d_model), wq, wk.T, wv.T, wo, norm_gain[None, :], q_gain[None, :], k_gain[None, :],
-            jnp.asarray(cos_c), jnp.asarray(sin_c), dev_ids.reshape(tp, batch * seq_dev), tok_ids)
-        onehot = (tok_flat[:, None] == jnp.arange(vocab, dtype=tok_ids.dtype)[None, :]).astype(BF)
-        w_all = jnp.concatenate([wq, wk, wv], axis=1)
-        swap1 = [(i, i ^ 1) for i in range(tp)]
-        swap2 = [(i, i ^ 2) for i in range(tp)]
-        odd = (rank & 1) == 1
-        far = (rank & 2) == 2
-        cos_tab, sin_tab = rope_tables(seq, hd)
-        rope_fn = functools.partial(norm_rope, cos_tab=cos_tab, sin_tab=sin_tab)
-        _, q_pull = jax.vjp(rope_fn, q_tok.reshape(batch, seq, heads, hd), q_gain)
-        _, k_pull = jax.vjp(rope_fn, kv_tok[:, :hd].reshape(batch, seq, 1, hd), k_gain)
-        q_four = q_rot.reshape(batch, seq, heads, hd)
-        k_rot = k_rot.reshape(batch, seq, hd)
-        v_three = kv_tok[:, hd:].reshape(batch, seq, hd)
-        attn_prob, prob_bf, _ = attention_core(q_four, k_rot, v_three)
-        attn_dev = attn_flat.reshape(batch, tp, seq_dev, qn).transpose(1, 0, 2, 3).reshape(toks, qn)
-
-        out_part = mm('tn,nd->td', attn_dev, wo).astype(BF)
-        attn_sum = lax.psum_scatter(out_part, 'tp', scatter_dimension=0, tiled=True)
-        y_loc = (x_mine.astype(F32) + attn_sum.astype(F32)).astype(BF).reshape(batch, seq_dev, d_model)
-
-        gw_out = mm('tn,td->nd', attn_flat, gy_all)
-        grad_four = grad_attn.reshape(batch, seq, heads, hd)
-        gq_rot, gk_rot, g_val = attention_grad(attn_prob, prob_bf, q_four, k_rot, v_three, grad_four)
-        gq_raw, gq_gain = q_pull(gq_rot.astype(BF).astype(F32))
-        gk_raw, gk_gain = k_pull(gk_rot.astype(BF).astype(F32)[:, :, None])
-        gkv_tok = jnp.concatenate([gk_raw.reshape(toks, hd), g_val.reshape(toks, hd)], axis=1)
-        gq_rows = mm('tr,tn->rn', onehot, gq_raw.reshape(toks, qn)).astype(BF)
-        gkv_t = mm('tn,tr->nr', gkv_tok, onehot).reshape(2, share, kn, vocab).transpose(1, 0, 2, 3)
-        gkv_t = gkv_t.reshape(2, 2, 2 * kn, vocab)
-        mine1 = jnp.where(odd, gkv_t[:, 1], gkv_t[:, 0])
-        send1 = jnp.where(odd, gkv_t[:, 0], gkv_t[:, 1]).astype(BF)
-        half = mine1 + lax.ppermute(send1, 'tp', swap1).astype(F32)
-        mine2 = jnp.where(far, half[1], half[0])
-        send2 = jnp.where(far, half[0], half[1]).astype(BF)
-        gkv_rows = (mine2 + lax.ppermute(send2, 'tp', swap2).astype(F32)).astype(BF).T
-        g_rows = jnp.concatenate([gq_rows, gkv_rows], axis=1)
-        gh_part = mm('rn,dn->rd', g_rows, w_all).astype(BF)
-        gh = lax.psum_scatter(gh_part, 'tp', scatter_dimension=0, tiled=True)
-        gw_query = mm('rd,rn->dn', hidden, gq_rows)
-        gw_kv = mm('rd,rn->dn', hidden, gkv_rows)
-        my_rows = rank * vrows + jnp.arange(vrows, dtype=tok_ids.dtype)
-        mine_hot = (my_rows[:, None] == tok_flat[None, :]).astype(BF)
-        gy_rows = lax.optimization_barrier(mm('rt,td->rd', mine_hot, gy_all))
-        _, norm_pull = jax.vjp(rms_scale, embed_loc.astype(F32), norm_gain)
-        gx_norm, gn_gain = norm_pull(gh.astype(F32))
-        g_embed = lax.optimization_barrier(gy_rows) + gx_norm
-        gains = jnp.concatenate([gn_gain, gq_gain, gk_gain])
-        gains = jnp.sum(lax.all_gather(gains, 'tp', axis=0, tiled=False), axis=0)
-        return (y_loc, g_embed, gains[:d_model], gains[d_model:d_model + hd], gains[d_model + hd:], gw_query, gw_kv[:, :kn], gw_kv[:, kn:], gw_out)
+        cos_c, sin_c = (jnp.asarray(t) for t in rope_consts(seq, hd))
+        tok_dev = tok_ids.reshape(batch, tp, seq_dev).transpose(1, 0, 2).reshape(tp, batch * seq_dev)
+        gains = (norm_gain[None, :], q_gain[None, :], k_gain[None, :])
+        hid, gy, o_sib, wo_sib, wqt, wqt_sib, wkv_sib, q_tok, kv_tok, q_rot, k_rot, o_own, d_o, x_mine = forward_kernel(
+            nz, embed_loc, gy_loc.reshape(batch * seq_dev, d_model), wq, wk.T, wv.T, wo, *gains, cos_c, sin_c, tok_dev, tok_ids)
+        y, g_embed, g_wq, g_kv, g_wo, g_gain = backward_kernel(
+            nz, o_own, o_sib, wo, wo_sib, wqt, wqt_sib, wk.T, wv.T, wkv_sib, gy, hid, q_tok, kv_tok, q_rot, k_rot, d_o, x_mine, embed_loc, *gains, cos_c, sin_c, tok_ids)
+        n = d_model // hd
+        return (y.reshape(batch, seq_dev, d_model), g_embed, g_gain[:n].reshape(d_model), g_gain[n], g_gain[n + 1], g_wq, g_kv[:kn].T, g_kv[kn:].T, g_wo)
 
     in_specs = (P('dp', None), P('tp', None), P(), P(), P(), P(None, 'tp'), P(None, 'tp'), P(None, 'tp'), P('tp', None), P('dp', 'tp', None))
     out_specs = (P('dp', 'tp', None), P(('dp', 'tp'), None), P('dp'), P('dp'), P('dp'), P('dp', 'tp'), P('dp', 'tp'), P('dp', 'tp'), P(('dp', 'tp'), None))

time: 517 us -> 424 us (0.82); the launches traced: 507 us -> 424 us
  Pallas kernels: 193 us -> 402 us
  matrix products: 161 us -> 0 us
  waiting for transfers between devices: 51.1 us -> 0 us
  other arithmetic: 31.6 us -> 0.01 us
  blocking collectives: 17.5 us -> 0 us
  local copies, waits for them, and re-layouts: 36.8 us -> 21.3 us
  between operations: 15 us -> 0.67 us
    pallas_call x0 -> x1, Pallas kernels: none -> 208 us  [backward_kernel(): pl.pallas_call(functools.partial(kb_body, nz), name='backward_kernel', ou...]
    dot_general x12 -> x0, matrix products: 151 us -> none  [mm(): return jnp.einsum(spec, a, b, preferred_element_type=F32)]
    reduce_scatter x2 -> x0, waiting for transfers between devices: 51 us -> none  [the longest x1 51 us: local_step(): gh = lax.psum_scatter(gh_part, 'tp', scatter_dimension=0, tiled=True)]
    all_gather x1 -> x0, blocking collectives: 17.5 us -> none  [local_step(): gains = jnp.sum(lax.all_gather(gains, 'tp', axis=0, tiled=False), axis=0)]
    convert_element_type x5 -> x0, local copies, waits for them, and re-layouts: 16.3 us -> none  [norm_rope(): normed = rms_scale(raw_heads.astype(F32), gain_vec)]
    reshape x8 -> x4, local copies, waits for them, and re-layouts: 14.3 us -> 2.8 us  [the longest x3 1.48 us: local_step(): tok_ids.reshape(batch, tp, seq_dev).transpose(1, 0, 2)]
    unnamed x40 -> x10, local copies, waits for them, and re-layouts: 3.79 us -> 14.8 us
    sub x1 -> x0, matrix products: 10.8 us -> none  [attention_core(): attn_prob = jax.nn.softmax(jnp.where(causal, scores, NEG_BIG), axis=-1)]
  transfers between devices with their start and end apart: 4 -> 0, of which waited for: 1 -> 0; matrix products, arithmetic and copies ran while one was open for 40% -> 0% of each run, Pallas kernels for 0% -> 0%
where the time goes in v4:
time: 424 us
  Pallas kernels  402 us (95%)
  local copies, waits for them, and re-layouts  21.3 us (5%)
    pallas_call x1, Pallas kernels, backward_kernel(): pl.pallas_call(functools.partial(kb_body, nz), name='backward_kernel', ou...  208 us
    pallas_call x1, Pallas kernels, forward_kernel(): pl.pallas_call(functools.partial(ka_body, nz), name='forward_kernel', out...  193 us
    unnamed x10, local copies, waits for them, and re-layouts  14.8 us

profile of v4, /device:TPU:21, one launch (start us, length us, event | category | flops | bytes accessed | tf_op | source)
XLA Modules:
  0.0 423.6 jit_solution(245066366651073870)
XLA Ops:
  0.6 0.8 reshape.34
  1.4 0.7 reshape.35.tok_dev
  2.1 193.5 %forward_kernel.1 = (bf16[2048,4096]{1,0:T(8,128)(2,1)}, bf16[2048,4096]{1,0:T(8,128)(2,1)}, bf16[2048,512]{1,0:T(8,128)(2,1)}, bf16[512,4096]{1,0:T(8,128)(2,1)...) custom-call(bf16[128,4096]{1,0:T(8,128)(2,1)} %embed.3, ...), custom_call_target="tpu_custom_call" | custom-call | flops 19327352832 | bytes 67108864 | tf_op jit(solution)/shard_map/forward_kernel/pallas_call | solution.py:403
  195.6 208.1 %backward_kernel.1 = (bf16[128,4096]{1,0:T(8,128)(2,1)}, f32[128,4096]{1,0:T(8,128)}, f32[4096,512]{1,0:T(8,128)}, f32[64,4096]{1,0:T(8,128)}, f32[512,4096]{1,0:T(8,128)}, /*index=5*/f32[40,128]{1,0:T(8,128)}) custom-call(bf16[2048,512]{1,0:T(8,128)(2,1)} %get-tuple-element.29.o_own, bf16[2048,512]{1,0:T(8,128)(2,1)} %get-tuple-element.30.o_sib, ...), custom_call_target="tpu_custom_call" | custom-call | flops 42949672960 | bytes 100663296 | tf_op jit(solution)/shard_map/backward_kernel/pallas_call | solution.py:859
  403.7 1.3 slice_bitcast_fusion.3
  405.0 1.3 slice_bitcast_fusion.2
  406.3 0.0 copy-start
  406.3 2.4 slice_bitcast_fusion
  408.7 3.0 copy.28
  411.7 0.0 slice-start
  411.7 3.3 copy.29
  414.9 0.0 copy-done
  414.9 0.0 slice-start.1
  415.0 4.3 %copy.30 = f32[4096,512]{1,0:T(8,128)} copy(f32[4096,512]{1,0:T(8,128)S(1)} %copy-done) | data formatting | bytes 16777216
  419.2 0.0 slice-done
  419.2 1.0 slice-done.1
  420.2 3.4 copy.31
  (2 shorter events, 0.0 us)
Async XLA Ops:
  406.3 8.6 %copy-start = (f32[4096,512]{1,0:T(8,128)S(1)}, f32[4096,512]{1,0:T(8,128)}, u32[]{:S(2)}) copy-start(f32[4096,512]{1,0:T(8,128)} %get-tuple-element.67) | copy-start | bytes 25165828
  411.7 7.5 %slice-start = ((s8[8388608]{0:T(1024)(128)(4,1)}), s8[4194304]{0:T(1024)(128)(4,1)S(1)}, s32[]{:S(2)}) async-start(s8[8388608]{0:T(1024)(128)(4,1)} %bitcast.20), calls=%async_computation | async-start | bytes 8388608
  414.9 5.2 %slice-start.1 = ((s8[8388608]{0:T(1024)(128)(4,1)}), s8[4194304]{0:T(1024)(128)(4,1)S(1)}, s32[]{:S(2)}) async-start(s8[8388608]{0:T(1024)(128)(4,1)} %bitcast.20), calls=%async_computation.1 | async-start | bytes 8388608

commit v5 on v1

v5 whole, which is shorter than its diff:
```python
import functools
import jax
import jax.numpy as jnp
import numpy as np
from jax import lax
from jax.experimental import pallas as pl
from jax.experimental.pallas import tpu as pltpu
from jax.sharding import PartitionSpec as P

BF = jnp.bfloat16
F32 = jnp.float32
EPS = 1.0e-6
ROPE_BASE = 1.0e6
NEG_BIG = -1.0e30
MESH = pl.DeviceIdType.MESH
ANY = pl.BlockSpec(memory_space=pl.ANY)
VM = pl.BlockSpec(memory_space=pltpu.VMEM)
NT = (((1,), (1,)), ((), ()))
NN = (((1,), (0,)), ((), ()))
TN = (((0,), (0,)), ((), ()))


def dotf(a, b, dims=NN):
    return lax.dot_general(a, b, dims, preferred_element_type=F32)


def rdma(src, dst, ssem, rsem, dev):
    return pltpu.make_async_remote_copy(src_ref=src, dst_ref=dst, send_sem=ssem, recv_sem=rsem, device_id={'tp': dev}, device_id_type=MESH)


def span(start, size):
    return pl.ds(pl.multiple_of(start, size), size)


def each(lo, hi, f):
    def go(j, _):
        f(j)
        return 0
    lax.fori_loop(lo, hi, go, 0)


def rms_f32(x, gain):
    return x * lax.rsqrt(jnp.mean(x * x, axis=-1, keepdims=True) + EPS) * gain


def rms_pull(x, dxr, r):
    return r * dxr - x * (r * r * r * jnp.mean(x * dxr, axis=-1, keepdims=True))


def masked(scores, first):
    r_i = lax.broadcasted_iota(jnp.int32, scores.shape, 0) + first
    c_i = lax.broadcasted_iota(jnp.int32, scores.shape, 1)
    return jnp.where(r_i >= c_i, scores, NEG_BIG)


def soft(scores):
    e = jnp.exp(scores - jnp.max(scores, axis=-1, keepdims=True))
    return e * (1.0 / jnp.sum(e, axis=-1, keepdims=True))


def body(nz, embed, gy, wq, wk_t, wv_t, wo, gain, qg, kg, cos, sin_s, tok_dev, tok_seq,
         y_hbm, ge_hbm, gq_hbm, gk_hbm, gv_hbm, gwo_hbm, gains_out, hid, gy_out, wqt_out, wqts_out, py_out, ph_out,
         table, wpair, wq_v, qt, o_own, o_sib, sq, kv_tok, k_rot, kvacc, farkv, kvrow, skv, kvc, d_rows, pbuf, hbuf, gown, hotm,
         dk_acc, dv_acc, pk, rk1, fk, hk, rk2, kvt, gn, qga, kga, gall, y_v, ge_v, gkv_v,
         in_sem, h_sem, g_sem, a_rs, a_rr, a_ss, a_sr, b_rs, b_rr, b_ss, b_sr, xs, xr, ts, wos, wor, wqs, wqr, wks, wkr, o_s, o_r,
         pt_sem, pl_sem, rs, rr, p1s, p1r, p2s, p2r, qs, qv, gls, hls, swos, swqs, gs, gr, out_sem):
    rank = lax.axis_index('tp')
    z, core = rank // 2, lax.rem(rank, 2)
    right = 2 * lax.rem(z + 1, nz) + core
    left = 2 * lax.rem(z + nz - 1, nz) + core
    sib = rank + 1 - 2 * core
    par = lax.rem(z, 2)
    far = rank + 2 - 4 * par
    vrows, d = embed.shape
    kn = wk_t.shape[0]
    sub_rows = vrows // 4
    vocab = vrows * 2 * nz
    vhalf = vocab // 2
    batch, seq = tok_seq.shape
    toks = batch * seq
    qn = wq.shape[1]
    hd = qg.shape[1]
    heads = qn // hd
    events = 2 * nz
    pos = seq // events
    blk = seq // 2
    bw = d // events
    scale = hd ** -0.5
    units = batch * heads
    parts = 8
    wo_p, wq_p = qn // parts, d // parts
    both = (0, 1)
    places = [(dr, c) for dr in both for c in both]
    qr = wq_v.at[pl.ds(0, toks)]
    gd = wq_v.at[pl.ds(toks, toks)]
    w_q = wq_v.at[pl.ds(0, d)]

    ld = [pltpu.make_async_copy(s, t, in_sem.at[i]) for i, (s, t) in enumerate((
        (embed, table.at[span(rank * vrows, vrows)]), (gy, gown), (wq, w_q), (wo, wpair.at[pl.ds(0, qn)]),
        (wk_t, wpair.at[pl.ds(2 * qn, kn)]), (wv_t, wpair.at[pl.ds(2 * qn + kn, kn)])))]
    ld2 = [pltpu.make_async_copy(s, t, in_sem.at[i]) for i, (s, t) in enumerate((
        (wqt_out, wpair.at[pl.ds(0, qn)]), (wqts_out, wpair.at[pl.ds(qn, qn)]), (embed, gown)))]
    for c in ld:
        c.start()
    barrier = pltpu.get_barrier_semaphore()
    for k in range(1, 2 * nz):
        pl.semaphore_signal(barrier, inc=1, device_id={'tp': lax.rem(rank + k, 2 * nz)}, device_id_type=MESH)
    pl.semaphore_wait(barrier, 2 * nz - 1)
    ld[0].wait()

    def nbr(dr):
        return right if dr == 0 else left

    def zd_of(dr, e):
        s = e // 2
        return lax.rem(z + (nz - s if dr == 0 else s), nz)

    def row_of(dr, e, c):
        return pl.multiple_of(vrows * (2 * zd_of(dr, e) + c) + sub_rows * (2 * dr + lax.rem(e, 2)), sub_rows)

    def ring(dr, e, recv_e):
        a = table.at[pl.ds(row_of(dr, e, core), sub_rows)]
        return rdma(a, a, a_rs.at[dr, e], a_rr.at[dr, recv_e], nbr(dr))

    def side(dr, e):
        a = table.at[pl.ds(row_of(dr, e, core), sub_rows)]
        return rdma(a, a, a_ss.at[dr, e], a_sr.at[dr, e], sib)

    def h_copy(slot, i, row):
        return pltpu.make_async_copy(hbuf.at[slot, pl.ds(i * sub_rows, sub_rows)], hid.at[pl.ds(row, sub_rows)], h_sem.at[slot, i])

    def g_row(dr, e, c):
        return pl.multiple_of(seq * (2 * dr + lax.rem(e, 2)) + pos * (2 * zd_of(dr, e) + c), pos)

    def g_piece(dr, e, c):
        return gy_out.at[pl.ds(g_row(dr, e, c), pos)]

    def g_own(dr, e):
        return gown.at[span(pos * (2 * dr + lax.rem(e, 2)), pos)]

    def g_ring(dr, e, recv_e, first):
        a = g_piece(dr, e, core)
        return rdma(g_own(dr, e) if first else a, a, b_rs.at[dr, e], b_rr.at[dr, recv_e], nbr(dr))

    def g_side(dr, e, first):
        a = g_piece(dr, e, core)
        return rdma(g_own(dr, e) if first else a, a, b_ss.at[dr, e], b_sr.at[dr, e], sib)

    def g_home(dr, e):
        return pltpu.make_async_copy(g_own(dr, e), g_piece(dr, e, core), in_sem.at[8 + 2 * dr + e])

    def g_fetch(slot, i, dr, c, e):
        return pltpu.make_async_copy(g_piece(dr, e, c), hbuf.at[slot, pl.ds(i * pos, pos)], g_sem.at[slot, i])

    def wo_push(k):
        return rdma(wpair.at[span(k * wo_p, wo_p)], wpair.at[pl.ds(pl.multiple_of(qn + k * wo_p, wo_p), wo_p)], wos.at[k], wor.at[k], sib)

    def tb(k):
        return o_own.at[span(lax.rem(k, 2) * qn, qn), pl.ds(0, wq_p)]

    def wq_push(k):
        return rdma(tb(k), wqts_out.at[:, span(k * wq_p, wq_p)], wqs.at[k], wqr.at[k], sib)

    def wq_home(k):
        return pltpu.make_async_copy(tb(k), wqt_out.at[:, span(k * wq_p, wq_p)], ts.at[k])

    def wk_push(k):
        return rdma((wk_t, wv_t)[k], wpair.at[pl.ds(2 * qn + (2 + k) * kn, kn)], wks.at[k], wkr.at[k], sib)

    def o_push(b, k):
        src = pl.multiple_of(b * seq + pos * (2 * k + 1 - core), pos)
        dst = pl.multiple_of(vrows * k + pos * b, pos)
        return rdma(o_own.at[pl.ds(src, pos)], o_sib.at[pl.ds(dst, pos)], o_s.at[b, k], o_r.at[b, k], sib)

    for k in both:
        wk_push(k).start()
    for b in range(batch):
        wide = jnp.broadcast_to(tok_seq[b:b + 1, :].astype(F32), (vrows, seq))
        d_rows[b * seq:(b + 1) * seq, :vrows] = wide.T
    qt[...] = jnp.zeros_like(qt)
    kvacc[...] = jnp.zeros_like(kvacc)

    def project(e):
        slot = lax.rem(e, 2)

        @pl.when(e >= 2)
        def _():
            for i in range(4):
                h_copy(slot, i, row_of(0, e, core)).wait()

        rows = [row_of(dr, e, c) for dr, c in places]
        for i, row in enumerate(rows):
            x = table[pl.ds(row, sub_rows), :].astype(F32)
            ids = row + lax.broadcasted_iota(jnp.int32, (sub_rows, tok_dev.shape[1]), 0)
            hit = jnp.zeros((sub_rows, tok_dev.shape[1]), F32)
            for j in range(tok_dev.shape[0]):
                hit = jnp.maximum(hit, jnp.where(tok_dev[j:j + 1, :] == ids, 1.0, 0.0))
            used = jnp.max(hit, axis=1, keepdims=True)
            h = jnp.where(used > 0.5, rms_f32(x, gain[...]), 0.0)
            hbuf[slot, pl.ds(i * sub_rows, sub_rows), :] = h.astype(BF)
            h_copy(slot, i, row).start()
        hb = hbuf[slot]
        qkv = jnp.concatenate([dotf(hb, w_q[...]).astype(BF), dotf(hb, wpair[2 * qn:2 * qn + 4 * kn, :], NT).astype(BF)], axis=1)
        lane = lax.broadcasted_iota(jnp.int32, (1, vrows), 1)
        rowid = jnp.zeros((1, vrows), jnp.int32)
        for i, row in enumerate(rows):
            rowid = jnp.where(lane // sub_rows == i, row + lane - i * sub_rows, rowid)
        rowid = rowid.astype(F32)
        for b in range(batch):
            sl = slice(b * seq, (b + 1) * seq)
            hot = jnp.where(d_rows[sl, :vrows] == rowid, 1.0, 0.0).astype(BF)
            got = dotf(hot, qkv)
            qt[sl, :] = (qt[sl, :].astype(F32) + got[:, :qn]).astype(BF)
            at = slice((b % 2) * seq, (b % 2 + 1) * seq)
            kvacc[b // 2, at, :] = (kvacc[b // 2, at, :].astype(F32) + got[:, qn:]).astype(BF)

    def step_a(e):
        @pl.when((e >= 2) & (e < events))
        def _():
            for dr in both:
                ring(dr, e, e).wait_recv()

        @pl.when(e < events - 2)
        def _():
            for dr in both:
                ring(dr, e, e + 2).start()

        @pl.when(e < events)
        def _():
            for dr in both:
                side(dr, e).start()

        @pl.when(e == 1)
        def _():
            for c in ld[1:]:
                c.wait()
            for k in both:
                wk_push(k).wait_recv()
            for dr in both:
                for k in both:
                    g_home(dr, k).start()

        @pl.when(e == events - 2)
        def _():
            for dr in both:
                g_ring(dr, 0, 2, True).start()

        @pl.when((e >= 2) & (e < 4 + parts))
        def _():
            @pl.when(e >= 4)
            def _():
                wq_push(e - 4).wait_send()
                wq_home(e - 4).wait()

            @pl.when(e < 2 + parts)
            def _():
                k = e - 2
                block = wq_v[span(k * wq_p, wq_p), :]
                tb(k)[...] = block.astype(F32).T.astype(BF)
                wo_push(k).start()
                wq_push(k).start()
                wq_home(k).start()

        @pl.when(e >= 1)
        def _():
            for dr in both:
                side(dr, e - 1).wait_recv()
            project(e - 1)

    each(0, events + 1, step_a)

    to_far = rdma(kvacc.at[core], farkv.at[core], xs.at[0], xr.at[0], far)
    relay = rdma(farkv.at[core], farkv.at[core], xs.at[1], xr.at[1], sib)
    mine = jnp.broadcast_to(tok_dev[pl.ds(rank, 1), :].astype(F32), (vrows, tok_dev.shape[1]))
    col = mine.T.astype(jnp.int32)
    lanes = lax.broadcasted_iota(jnp.int32, col.shape, 1)
    hot_mine = jnp.concatenate([jnp.where(col == lanes + j * vrows, 1.0, 0.0).astype(BF) for j in range(vocab // vrows)], axis=1)
    to_far.start()
    for dr in both:
        g_ring(dr, 1, 3, True).start()
        for k in both:
            g_side(dr, k, True).start()
            g_home(dr, k).wait()
    cw = min(512, d)

    def own_rows(j):
        y_v[:, span(j * cw, cw)] = dotf(hot_mine, table[:, span(j * cw, cw)]).astype(BF)

    each(0, d // cw, own_rows)
    for b in range(batch):
        ids = rank * vrows + lax.broadcasted_iota(jnp.int32, (vrows, seq), 0)
        hotm[:, b * seq:(b + 1) * seq] = jnp.where(ids == tok_seq[b:b + 1, :], 1.0, 0.0).astype(BF)
    to_far.wait_recv()
    relay.start()

    def place(p, first):
        l_i = lax.broadcasted_iota(jnp.int32, (4 * kn, 2 * hd), 0)
        m_i = lax.broadcasted_iota(jnp.int32, (4 * kn, 2 * hd), 1)
        upper = jnp.where(l_i >= 2 * kn, 1, 0)
        owner = jnp.where(upper == 1, 1 - first, first)
        l_i = l_i - 2 * kn * upper
        base = kn * (2 * p + owner)
        want = jnp.where(l_i < kn, base + l_i, hd + base + l_i - kn)
        return jnp.where(m_i == want, 1.0, 0.0).astype(BF)

    rdma(farkv.at[1 - core], farkv.at[1 - core], xs.at[1], xr.at[1], sib).wait_recv()
    for hf in both:
        kv_tok[hf * (toks // 2):(hf + 1) * (toks // 2), :] = (dotf(kvacc[hf], place(par, core)) + dotf(farkv[hf], place(1 - par, hf))).astype(BF)

    def rope(raw, g):
        n = rms_f32(raw.astype(F32), g)
        return (n * cos[...] + pltpu.roll(n, hd // 2, 1) * sin_s[...]).astype(BF)

    for b in range(batch):
        sl = slice(b * seq, (b + 1) * seq)
        k_rot[sl, :] = rope(kv_tok[sl, :hd], kg[...])

    def attend(u):
        base = (u // heads) * seq
        rows = span(base, seq)
        cols = span(lax.rem(u, heads) * hd, hd)
        q = rope(qt[rows, cols], qg[...])
        qr[rows, cols] = q
        kr = k_rot[rows, :]
        v = kv_tok[rows, hd:]
        for i in both:
            n = blk * (i + 1)
            s = masked(dotf(q[i * blk:(i + 1) * blk], kr[:n], NT) * scale, i * blk)
            o_own[pl.ds(pl.multiple_of(base + i * blk, blk), blk), cols] = dotf(soft(s).astype(BF), v[:n]).astype(BF)

    def grad_attend(e):
        slot = lax.rem(e, 2)
        for i, (dr, c) in enumerate(places):
            g_fetch(slot, i, dr, c, e).wait()
        r = dotf(hbuf[slot], wpair[:qn, :], NT).astype(BF)
        for i, (dr, c) in enumerate(places):
            gd[pl.ds(g_row(dr, e, c), pos), :] = r[i * pos:(i + 1) * pos]

    def pstage(j):
        return d_rows.at[span(lax.rem(j, 2) * vhalf, vhalf), pl.ds(0, bw)]

    def pstore(dst, j):
        return pltpu.make_async_copy(pstage(j), dst.at[:, span(j * bw, bw)], pt_sem.at[lax.rem(j, 2)])

    def pblock(dst, j, pairs):
        @pl.when(j >= 2)
        def _():
            pstore(dst, j - 2).wait()
        cols = span(j * bw, bw)
        acc = None
        for a, lo, n in pairs:
            t = dotf(a[...], wpair[lo:lo + n, cols])
            acc = t if acc is None else acc + t
        pstage(j)[...] = acc
        pstore(dst, j).start()

    y_pairs = [(sq, 0, qn), (o_sib, qn, qn)]
    h_pairs = [(o_sib, 0, qn), (sq, qn, qn), (kvc, 2 * qn, 4 * kn)]

    def pslot(ph, e, dr):
        return pbuf.at[2 * ph + lax.rem(e, 2), dr]

    def pfetch(ph, e, dr):
        s = e // 2
        zd = lax.rem(z + (2 * nz - 1 - s if dr == 0 else 1 + s), nz)
        row = pl.multiple_of(vrows * zd + sub_rows * (2 * dr + lax.rem(e, 2)), sub_rows)
        return pltpu.make_async_copy((py_out, ph_out)[ph].at[pl.ds(row, sub_rows)], pslot(ph, e, dr), pl_sem.at[ph, lax.rem(e, 2), dr])

    def rslot(dr, e):
        return table.at[span((dr * (events - 2) + e) * sub_rows, sub_rows)]

    def sslot(ph, dr, e):
        k = 2 * (events - 2) + 8 * ph + 4 * lax.rem(e // 2, 2) + 2 * dr + lax.rem(e, 2)
        return table.at[span(k * sub_rows, sub_rows)]

    def send(ph, dr, e):
        return rdma(sslot(ph, dr, e), rslot(dr, e), rs.at[ph, dr, e], rr.at[ph, dr, e], nbr(dr))

    def first_fetch(ph, dst):
        for j in (events - 2, events - 1):
            pstore(dst, j).wait()
        for e in both:
            for dr in both:
                pfetch(ph, e, dr).start()

    def first_sends(ph):
        for e in both:
            for dr in both:
                pfetch(ph, e, dr).wait()
                sslot(ph, dr, e)[...] = pslot(ph, e, dr)[...].astype(BF)
        for e in both:
            for dr in both:
                send(ph, dr, e).start()
                pfetch(ph, e + 2, dr).start()

    def serve(ph, e, final):
        for dr in both:
            send(ph, dr, e - 2).wait_recv()
            pfetch(ph, e, dr).wait()

        @pl.when(e < events - 2)
        def _():
            @pl.when(e >= 4)
            def _():
                for dr in both:
                    send(ph, dr, e - 4).wait_send()
            for dr in both:
                sslot(ph, dr, e)[...] = (pslot(ph, e, dr)[...] + rslot(dr, e - 2)[...].astype(F32)).astype(BF)
            for dr in both:
                send(ph, dr, e).start()
                pfetch(ph, e + 2, dr).start()

        @pl.when(e >= events - 2)
        def _():
            for dr in both:
                final(dr, lax.rem(e, 2), pslot(ph, e, dr)[...] + rslot(dr, e - 2)[...].astype(F32))

    slots = 9

    def gather_o(k):
        for b in range(batch):
            src = pl.multiple_of(b * seq + pos * (2 * k + core), pos)
            sq[pl.ds(pl.multiple_of(vrows * k + pos * b, pos), pos), :] = o_own[pl.ds(src, pos), :]

    def upto(e, n, over):
        return jnp.minimum((e * n) // over, n)

    def step_b(e):
        @pl.when(e == events - 2)
        def _():
            first_sends(0)

        @pl.when((e >= 2) & (e < events))
        def _():
            for dr in both:
                g_ring(dr, e, e, False).wait_recv()

        @pl.when((e >= 2) & (e < events - 2))
        def _():
            for dr in both:
                g_ring(dr, e, e + 2, False).start()

        @pl.when((e >= 2) & (e < events))
        def _():
            for dr in both:
                g_side(dr, e, False).start()

        @pl.when((e >= 1) & (e <= events))
        def _():
            for dr in both:
                g_side(dr, e - 1, False).wait_recv()
            for i, (dr, c) in enumerate(places):
                g_fetch(lax.rem(e - 1, 2), i, dr, c, e - 1).start()

        def give(b):
            each(0, nz, lambda k: o_push(b, k).start())

        each(upto(jnp.maximum(e - 1, 0), units, slots) // heads, upto(e, units, slots) // heads, give)
        each(upto(e, units, slots), upto(e + 1, units, slots), attend)

        @pl.when(e == 4)
        def _():
            def drain(k):
                @pl.when(k < events - 2)
                def _():
                    for dr in both:
                        ring(dr, k, k + 2).wait_send()
                for dr in both:
                    side(dr, k).wait_send()
            each(0, events, drain)

        @pl.when(e == slots + 1)
        def _():
            for k in range(parts):
                wo_push(k).wait_recv()
            for b in range(batch):
                each(0, nz, lambda k: o_push(b, k).wait_recv())
            each(0, nz, gather_o)

        @pl.when((e > slots) & (e <= slots + 4))
        def _():
            each(4 * (e - slots - 1), 4 * (e - slots), lambda j: pblock(py_out, j, y_pairs))

        @pl.when(e == slots + 4)
        def _():
            first_fetch(0, py_out)

        @pl.when(e >= 2)
        def _():
            grad_attend(e - 2)

    for slot in both:
        for i in range(4):
            h_copy(slot, i, row_of(0, 0, core)).wait()
    each(0, events + 2, step_b)

    def pull(raw, dout, g):
        x = raw.astype(F32)
        r = lax.rsqrt(jnp.mean(x * x, axis=-1, keepdims=True) + EPS)
        dn = dout * cos[...] + pltpu.roll(dout * sin_s[...], hd // 2, 1)
        return rms_pull(x, dn * g, r).astype(BF), jnp.sum(dn * (x * r), axis=0, keepdims=True)

    def unit(u):
        b, h = u // heads, lax.rem(u, heads)
        rows = span(b * seq, seq)
        cols = span(h * hd, hd)

        @pl.when(h == 0)
        def _():
            dk_acc[...] = jnp.zeros_like(dk_acc)
            dv_acc[...] = jnp.zeros_like(dv_acc)
        q, g = qr[rows, cols], gd[rows, cols]
        kr, v = k_rot[rows, :], kv_tok[rows, hd:]
        dqs = []
        for i in both:
            n = blk * (i + 1)
            qi, gi = q[i * blk:(i + 1) * blk], g[i * blk:(i + 1) * blk]
            p = soft(masked(dotf(qi, kr[:n], NT) * scale, i * blk))
            dp = dotf(gi, v[:n], NT)
            dv_acc[:n, :] += dotf(p.astype(BF), gi, TN)
            ds = (p * (dp - jnp.sum(p * dp, axis=-1, keepdims=True)) * scale).astype(BF)
            dqs.append(dotf(ds, kr[:n]))
            dk_acc[:n, :] += dotf(ds, qi, TN)
        dq = jnp.concatenate(dqs, axis=0).astype(BF).astype(F32)
        dx, dg = pull(qt[rows, cols], dq, qg[...])
        gd[rows, cols] = dx
        qga[...] += dg

    def pick(r, up):
        m_i = lax.broadcasted_iota(jnp.int32, (2 * hd, 4 * kn), 0)
        l_i = lax.broadcasted_iota(jnp.int32, (2 * hd, 4 * kn), 1) - 2 * kn * up
        is_k = (l_i >= 0) & (l_i < kn) & (m_i == l_i + kn * r)
        is_v = (l_i >= kn) & (l_i < 2 * kn) & (m_i == hd + kn * r + l_i - kn)
        return jnp.where(is_k | is_v, 1.0, 0.0).astype(BF)

    def to_side(b, p):
        return rdma(pk.at[b, 2 * p + 1 - core], rk1.at[b, p], p1s.at[b, p], p1r.at[b, p], sib)

    def to_far2(b):
        return rdma(fk.at[b], rk2.at[b], p2s.at[b], p2r.at[b], far)

    def kv_one(b):
        dk = dk_acc[...].astype(BF).astype(F32)
        dx, dg = pull(kv_tok[span(b * seq, seq), :hd], dk, kg[...])
        kga[...] += dg
        gkv = jnp.concatenate([dx, dv_acc[...].astype(BF)], axis=1)
        for r in range(4):
            pk[b, r] = (dotf(gkv[:blk], pick(r, 0)) + dotf(gkv[blk:], pick(r, 1))).astype(BF)
        for p in both:
            to_side(b, p).start()

    def kv_two(b):
        for p in both:
            to_side(b, p).wait_recv()
        fk[b] = (pk[b, 2 * (1 - par) + core].astype(F32) + rk1[b, 1 - par].astype(F32)).astype(BF)
        hk[b] = pk[b, 2 * par + core].astype(F32) + rk1[b, par].astype(F32)
        to_far2(b).start()

    def kv_three(b):
        to_far2(b).wait_recv()
        t = hk[b] + rk2[b].astype(F32)
        low = lax.broadcasted_iota(jnp.int32, t.shape, 1) < 2 * kn
        kvt[b, :blk, :] = jnp.where(low, t, 0.0).astype(BF)
        kvt[b, blk:, :] = jnp.where(low, pltpu.roll(t, 2 * kn, 1), 0.0).astype(BF)

    def fold(b, tile):
        rows = span(tile * seq, seq)
        ids = tile * seq + lax.broadcasted_iota(jnp.int32, (seq, seq), 0)
        hot = jnp.where(ids == tok_seq[pl.ds(b, 1), :], 1.0, 0.0).astype(BF)
        d_rows[rows, :qn] += dotf(hot, gd[span(b * seq, seq), :])
        d_rows[rows, qn:] += dotf(hot, kvt[b])

    tiles = vocab // seq // 2

    def job(k):
        @pl.when(k < units)
        def _():
            unit(k)

        @pl.when((k < units) & (lax.rem(k, heads) == heads - 1))
        def _():
            kv_one(k // heads)

        @pl.when(k >= heads)
        def _():
            b, h = k // heads - 1, lax.rem(k, heads)

            @pl.when(h == 0)
            def _():
                kv_two(b)

            @pl.when(h == 1)
            def _():
                kv_three(b)

            @pl.when(h >= 2)
            def _():
                each(tiles * (h - 2), tiles * (h - 1), lambda t: fold(b, t))

    def settle(t):
        rows = span(t * vrows, vrows)
        qt[rows, :] = d_rows[rows, :qn].astype(BF)
        kvrow[rows, :] = d_rows[rows, qn:].astype(BF)

    def swap(k, kk):
        src = pl.multiple_of(vrows * (2 * k + 1 - core), vrows)
        return rdma((qt, kvrow)[kk].at[pl.ds(src, vrows)], (sq, skv)[kk].at[span(vrows * k, vrows)], qs.at[kk, k], qv.at[kk, k], sib)

    def gather_h(k):
        src = pl.multiple_of(vrows * (2 * k + core), vrows)
        dst = span(vrows * k, vrows)
        o_sib[dst, :] = qt[pl.ds(src, vrows), :]
        kvc[dst, :] = (kvrow[pl.ds(src, vrows), :].astype(F32) + pltpu.roll(skv[dst, :].astype(F32), 2 * kn, 1)).astype(BF)

    def final_y(dr, sub, acc):
        rows = span((2 * dr + sub) * pos, pos)
        y_v[rows, :] = (y_v[rows, :].astype(F32) + acc).astype(BF)

    paced = 9

    def step_c(e):
        @pl.when(e == events - 2)
        def _():
            first_sends(1)

        @pl.when(e >= 2)
        def _():
            serve(0, e, final_y)

        @pl.when(e == 0)
        def _():
            for dr in both:
                for k in both:
                    g_ring(dr, k, k + 2, True).wait_send()
                    g_side(dr, k, True).wait_send()
            for k in range(parts):
                wq_push(k).wait_recv()
                wo_push(k).wait_send()
            for c in ld2:
                c.start()
            d_rows[...] = jnp.zeros_like(d_rows)
            gn[...] = jnp.zeros_like(gn)
            qga[...] = jnp.zeros_like(qga)
            kga[...] = jnp.zeros_like(kga)

        each(upto(e, units + heads, paced), upto(e + 1, units + heads, paced), job)

        @pl.when(e == paced)
        def _():
            each(0, 2 * nz, settle)
            each(0, nz, lambda k: [swap(k, kk).start() for kk in both])

        @pl.when(e == paced + 1)
        def _():
            for c in ld2:
                c.wait()
            each(0, nz, lambda k: [swap(k, kk).wait_recv() for kk in both])
            each(0, nz, gather_h)

        @pl.when((e > paced) & (e <= paced + 4))
        def _():
            each(4 * (e - paced - 1), 4 * (e - paced), lambda j: pblock(ph_out, j, h_pairs))

        @pl.when(e == paced + 4)
        def _():
            first_fetch(1, ph_out)

    each(0, events, step_c)

    def gblk(j):
        return qr.at[:, span(lax.rem(j, 2) * bw, bw)]

    def hblk(j):
        return gd.at[:, span(lax.rem(j, 2) * bw, bw)]

    def swo(j):
        return d_rows.at[pl.ds(0, qn), span(lax.rem(j, 2) * bw, bw)]

    def swq(j):
        return d_rows.at[pl.ds(pl.multiple_of(qn + lax.rem(j, 2) * bw, bw), bw), pl.ds(0, qn)]

    def g_load(j):
        return pltpu.make_async_copy(gy_out.at[:, span(j * bw, bw)], gblk(j), gls.at[lax.rem(j, 2)])

    def h_load(j):
        return pltpu.make_async_copy(hid.at[:, span(j * bw, bw)], hblk(j), hls.at[lax.rem(j, 2)])

    def wo_store(j):
        return pltpu.make_async_copy(swo(j), gwo_hbm.at[:, span(j * bw, bw)], swos.at[lax.rem(j, 2)])

    def wq_store(j):
        return pltpu.make_async_copy(swq(j), gq_hbm.at[span(j * bw, bw)], swqs.at[lax.rem(j, 2)])

    def block(j):
        g_load(j).wait()
        h_load(j).wait()

        @pl.when(j + 1 < events)
        def _():
            g_load(j + 1).start()
            h_load(j + 1).start()

        @pl.when(j >= 2)
        def _():
            wo_store(j - 2).wait()
            wq_store(j - 2).wait()
        cols = span(j * bw, bw)
        swo(j)[...] = dotf(o_own[...], gblk(j)[...], TN)
        ge_v[:, cols] = dotf(hotm[...], gblk(j)[...])
        wo_store(j).start()
        swq(j)[...] = dotf(hblk(j)[...], qt[...], TN)
        gkv_v[:, cols] = dotf(kvrow[...], hblk(j)[...], TN)[:2 * kn]
        wq_store(j).start()

    def final_h(dr, sub, gh):
        rows = span((2 * dr + sub) * sub_rows, sub_rows)
        x = gown[rows, :].astype(F32)
        r = lax.rsqrt(jnp.mean(x * x, axis=-1, keepdims=True) + EPS)
        ge_v[rows, :] += rms_pull(x, gh * gain[...], r)
        gn[...] += jnp.sum(gh * (x * r), axis=0, keepdims=True)

    outs = [pltpu.make_async_copy(s, t, out_sem.at[i]) for i, (s, t) in enumerate((
        (y_v, y_hbm), (gkv_v.at[pl.ds(0, kn)], gk_hbm), (gkv_v.at[pl.ds(kn, kn)], gv_hbm), (ge_v, ge_hbm)))]
    g_load(0).start()
    h_load(0).start()
    outs[0].start()
    work_d = events - 3

    def step_d(e):
        @pl.when(e >= 2)
        def _():
            serve(1, e, final_h)

        each(upto(e, events, work_d), upto(e + 1, events, work_d), block)

    each(0, events, step_d)

    outs[3].start()
    wide = gains_out.shape[1]
    for j in range(d // wide):
        gall[rank, j:j + 1, :] = gn[:, j * wide:(j + 1) * wide]
    gall[rank, d // wide:d // wide + 1, :] = qga[...]
    gall[rank, d // wide + 1:d // wide + 2, :] = kga[...]
    outs[1].start()
    outs[2].start()
    for j in (events - 2, events - 1):
        wo_store(j).wait()
        wq_store(j).wait()

    def spread(k, src):
        return rdma(gall.at[src], gall.at[src], gs.at[k], gr.at[k], lax.rem(rank + k, 2 * nz))

    for k in range(1, 2 * nz):
        spread(k, rank).start()

    def drain_c(e):
        for ph in both:
            for dr in both:
                send(ph, dr, e).wait_send()

    each(events - 6, events - 2, drain_c)

    def drain_b(e):
        @pl.when(e < events - 2)
        def _():
            for dr in both:
                g_ring(dr, e, e + 2, False).wait_send()
        for dr in both:
            g_side(dr, e, False).wait_send()

    each(2, events, drain_b)
    to_far.wait_send()
    relay.wait_send()
    for k in both:
        wk_push(k).wait_send()
    for b in range(batch):
        each(0, nz, lambda k: o_push(b, k).wait_send())
        for p in both:
            to_side(b, p).wait_send()
        to_far2(b).wait_send()
    each(0, nz, lambda k: [swap(k, kk).wait_send() for kk in both])
    for k in range(1, 2 * nz):
        spread(k, lax.rem(rank + 2 * nz - k, 2 * nz)).wait_recv()
    gains_out[...] = jnp.sum(gall[...], axis=0)
    for k in range(1, 2 * nz):
        spread(k, rank).wait_send()
    for c in outs:
        c.wait()


def step_kernel(nz, embed, gy, wq, wk_t, wv_t, wo, gain, qg, kg, cos, sin_s, tok_dev, tok_seq):
    vrows, d = embed.shape
    vocab = vrows * 2 * nz
    qn, kn = wq.shape[1], wk_t.shape[0]
    hd = qg.shape[1]
    batch, seq = tok_seq.shape
    toks = batch * seq
    ev = 2 * nz
    sr, hb, vh = vrows // 4, seq // 2, vocab // 2
    grow = (d // hd + 2 + 7) // 8 * 8
    dma = pltpu.SemaphoreType.DMA
    v = pltpu.VMEM

    def arr(dt, *shape):
        return jax.ShapeDtypeStruct(shape, dt)

    outs = (arr(BF, vrows, d), arr(F32, vrows, d), arr(F32, d, qn), arr(F32, kn, d), arr(F32, kn, d), arr(F32, qn, d), arr(F32, grow, hd),
            arr(BF, vocab, d), arr(BF, toks, d), arr(BF, qn, d), arr(BF, qn, d), arr(F32, vh, d), arr(F32, vh, d))
    return pl.pallas_call(
        functools.partial(body, nz),
        name='step_kernel',
        out_shape=outs,
        in_specs=[ANY] * 6 + [VM] * 7,
        out_specs=(ANY,) * 6 + (VM,) + (ANY,) * 6,
        scratch_shapes=[v((vocab, d), BF), v((2 * qn + 4 * kn, d), BF), v((max(d, 2 * toks), qn), BF), v((vocab, qn), BF), v((toks, qn), BF), v((vh, qn), BF), v((vh, qn), BF),
                        v((toks, 2 * hd), BF), v((toks, hd), BF), v((2, toks // 2, 4 * kn), BF), v((2, toks // 2, 4 * kn), BF), v((vocab, 4 * kn), BF), v((vh, 4 * kn), BF), v((vh, 4 * kn), BF),
                        v((vocab, qn + 4 * kn), F32), v((4, 2, sr, d), F32), v((2, vrows, d), BF), v((vrows, d), BF), v((vrows, toks), BF),
                        v((seq, hd), F32), v((seq, hd), F32), v((batch, 4, hb, 4 * kn), BF), v((batch, 2, hb, 4 * kn), BF), v((batch, hb, 4 * kn), BF), v((batch, hb, 4 * kn), F32),
                        v((batch, hb, 4 * kn), BF), v((batch, seq, 4 * kn), BF), v((1, d), F32), v((1, hd), F32), v((1, hd), F32), v((ev, grow, hd), F32), v((vrows, d), BF), v((vrows, d), F32), v((2 * kn, d), F32),
                        dma((12,)), dma((2, 4)), dma((2, 4))] + [dma((2, ev))] * 8 + [dma((2,)), dma((2,))] + [dma((8,))] * 5 + [dma((2,)), dma((2,)), dma((batch, nz)), dma((batch, nz)),
                        dma((2,)), dma((2, 2, 2)), dma((2, 2, ev - 2)), dma((2, 2, ev - 2)), dma((batch, 2)), dma((batch, 2)), dma((batch,)), dma((batch,)), dma((2, nz)), dma((2, nz)),
                        dma((2,)), dma((2,)), dma((2,)), dma((2,)), dma((ev,)), dma((ev,)), dma((4,))],
        compiler_params=pltpu.CompilerParams(collective_id=0, has_side_effects=True, vmem_limit_bytes=67043328),
        cost_estimate=pl.CostEstimate(flops=2 * vocab * d * 8 * qn, bytes_accessed=20 * vocab * d, transcendentals=0),
    )(embed, gy, wq, wk_t, wv_t, wo, gain, qg, kg, cos, sin_s, tok_dev, tok_seq)


def emit_body(cuts, *refs):
    n = len(cuts)
    src, dst = refs[:n], refs[n:2 * n]
    bufs, s_in, s_out = refs[2 * n:-2], refs[-2], refs[-1]
    ins, outs = [], []
    for i, c in enumerate(cuts):
        step = src[i].shape[0] // c
        for j in range(c):
            b = bufs[i].at[pl.ds(j * step, step)]
            ins.append(pltpu.make_async_copy(src[i].at[pl.ds(j * step, step)], b, s_in.at[len(ins)]))
            outs.append(pltpu.make_async_copy(b, dst[i].at[pl.ds(j * step, step)], s_out.at[len(outs)]))
    for c in ins:
        c.start()
    for a, b in zip(ins, outs):
        a.wait()
        b.start()
    for b in outs:
        b.wait()


def emit(*arrays):
    size = 1 << 21
    cuts = tuple(max(1, a.size * a.dtype.itemsize // size) for a in arrays)
    return pl.pallas_call(
        functools.partial(emit_body, cuts),
        name='emit',
        out_shape=tuple(jax.ShapeDtypeStruct(a.shape, a.dtype) for a in arrays),
        in_specs=[ANY] * len(arrays),
        out_specs=(ANY,) * len(arrays),
        scratch_shapes=[pltpu.VMEM(a.shape, a.dtype) for a in arrays] + [pltpu.SemaphoreType.DMA((sum(cuts),))] * 2,
        compiler_params=pltpu.CompilerParams(vmem_limit_bytes=60 * 1024 * 1024),
        cost_estimate=pl.CostEstimate(flops=0, bytes_accessed=2 * sum(a.size * a.dtype.itemsize for a in arrays), transcendentals=0),
    )(*arrays)


def rope_consts(seq, hd):
    inv = np.float32(ROPE_BASE) ** (np.float32(-2.0) * np.arange(hd // 2, dtype=np.float32) / np.float32(hd))
    ang = np.arange(seq, dtype=np.float32)[:, None] * inv.astype(np.float32)[None, :]
    ang = np.concatenate([ang, ang], axis=-1)
    sign = np.where(np.arange(hd) < hd // 2, -1.0, 1.0).astype(np.float32)
    return np.cos(ang).astype(np.float32), (np.sin(ang) * sign).astype(np.float32)


def solution(mesh):
    tp = mesh.shape['tp']
    nz = tp // 2

    def local_step(tok_ids, embed_loc, norm_gain, q_gain, k_gain, wq, wk, wv, wo, gy_loc):
        d_model = embed_loc.shape[1]
        batch, seq = tok_ids.shape
        seq_dev = seq // tp
        hd = q_gain.shape[0]
        cos_c, sin_c = (jnp.asarray(t) for t in rope_consts(seq, hd))
        tok_dev = tok_ids.reshape(batch, tp, seq_dev).transpose(1, 0, 2).reshape(tp, batch * seq_dev)
        r = step_kernel(nz, embed_loc, gy_loc.reshape(batch * seq_dev, d_model), wq, wk.T, wv.T, wo, norm_gain[None, :], q_gain[None, :], k_gain[None, :], cos_c, sin_c, tok_dev, tok_ids)
        y, g_embed, g_wq, g_wk, g_wv, g_wo = emit(*r[:6])
        g_gain = r[6]
        n = d_model // hd
        return (y.reshape(batch, seq_dev, d_model), g_embed, g_gain[:n].reshape(d_model), g_gain[n], g_gain[n + 1], g_wq, g_wk.T, g_wv.T, g_wo)

    in_specs = (P('dp', None), P('tp', None), P(), P(), P(), P(None, 'tp'), P(None, 'tp'), P(None, 'tp'), P('tp', None), P('dp', 'tp', None))
    out_specs = (P('dp', 'tp', None), P(('dp', 'tp'), None), P('dp'), P('dp'), P('dp'), P('dp', 'tp'), P('dp', 'tp'), P('dp', 'tp'), P(('dp', 'tp'), None))
    return jax.shard_map(local_step, mesh=mesh, in_specs=in_specs, out_specs=out_specs, check_vma=False)
```

time: 523 us -> 395 us (0.76); the launches traced: 514 us -> 394 us
  Pallas kernels: 0 us -> 391 us
  matrix products: 214 us -> 0 us
  waiting for transfers between devices: 152 us -> 0 us
  local copies, waits for them, and re-layouts: 58.1 us -> 2.61 us
  other arithmetic: 54.6 us -> 0 us
  blocking collectives: 17.5 us -> 0 us
  between operations: 14.9 us -> 0.68 us
    pallas_call x0 -> x2, Pallas kernels: none -> 391 us  [the longest x1 376 us: step_kernel(): pl.pallas_call(functools.partial(body, nz), name='step_kernel', out_shape...]
    dot_general x17 -> x0, matrix products: 203 us -> none  [mm(): return jnp.einsum(spec, a, b, preferred_element_type=F32)]
    all_gather x2 -> x0, waiting for transfers between devices: 90 us -> none  [the longest x1 90 us: local_step(): table = lax.all_gather(embed_loc, 'tp', axis=0, tiled=True)]
    reduce_scatter x2 -> x0, waiting for transfers between devices: 37.2 us -> none  [the longest x1 37.2 us: local_step(): gh = lax.psum_scatter(gh_part, 'tp', scatter_dimension=0, tiled=True)]
    ppermute x4 -> x0, waiting for transfers between devices: 23.4 us -> none  [the longest x1 21.1 us: local_step(): pair_o = lax.ppermute(pair, 'tp', swap2)]
    convert_element_type x10 -> x0, other arithmetic: 20.8 us -> none  [the longest x1 10.6 us: local_step(): jnp.where(used[:, None], rms_scale(table.astype(F32), norm_gain), 0.0)]
    convert_element_type x7 -> x0, local copies, waits for them, and re-layouts: 19.9 us -> none  [the longest x6 15.6 us: norm_rope(): normed = rms_scale(raw_heads.astype(F32), gain_vec)]
    all_gather x1 -> x0, blocking collectives: 17.5 us -> none  [local_step(): gains = jnp.sum(lax.all_gather(gains, 'tp', axis=0, tiled=False), axis=0)]
  transfers between devices with their start and end apart: 8 -> 0, of which waited for: 4 -> 0; matrix products, arithmetic and copies ran while one was open for 61% -> 0% of each run, Pallas kernels for 0% -> 0%
where the time goes in v5:
time: 395 us; the launch traced here: 394 us
  Pallas kernels  391 us (99%)
    pallas_call x1, Pallas kernels, step_kernel(): pl.pallas_call(functools.partial(body, nz), name='step_kernel', out_shape...  376 us
    pallas_call x1, Pallas kernels, emit(): pl.pallas_call(functools.partial(emit_body, cuts), name='emit', out_shape...  14.9 us

profile of v5, /device:TPU:21, one launch (start us, length us, event | category | flops | bytes accessed | tf_op | source)
XLA Modules:
  0.0 394.3 jit_solution(8399837062080809681)
XLA Ops:
  0.6 0.8 reshape.34
  1.4 0.7 reshape.35.tok_dev
  2.1 376.1 %step_kernel.1 = (bf16[128,4096]{1,0:T(8,128)(2,1)}, f32[128,4096]{1,0:T(8,128)}, f32[4096,512]{1,0:T(8,128)}, f32[32,4096]{1,0:T(8,128)}, f32[32,4096]{1,0:T(8,...) custom-call(bf16[128,4096]{1,0:T(8,128)(2,1)} %embed.1, ...), custom_call_target="tpu_custom_call" | custom-call | flops 68719476736 | bytes 167772160 | tf_op jit(solution)/shard_map/step_kernel/pallas_call | solution.py:809
  378.2 0.0 copy-start
  378.2 14.9 %emit.1 = (bf16[128,4096]{1,0:T(8,128)(2,1)}, f32[128,4096]{1,0:T(8,128)}, f32[4096,512]{1,0:T(8,128)}, f32[32,4096]{1,0:T(8,128)}, f32[32,4096]{1,0:T(8,128)}, /*index=5*/f32[512,4096]{1,0:T(8,128)}) custom-call(bf16[128,4096]{1,0:T(8,128)(2,1)} %get-tuple-element.22.refs_0_, f32[128,4096]{1,0:T(8,128)} %get-tuple-element.23.refs_1_, ...), custom_call_target="tpu_custom_call" | custom-call | bytes 41943040 | tf_op jit(solution)/shard_map/emit/pallas_call | solution.py:851
  393.1 0.0 copy-done
  393.1 0.5 slice_bitcast_fusion.1
  393.7 0.6 slice_bitcast_fusion
  (1 shorter events, 0.0 us)
Async XLA Ops:
  378.2 14.9 %copy-start = (f32[40,128]{1,0:T(8,128)S(1)}, f32[40,128]{1,0:T(8,128)}, u32[]{:S(2)}) copy-start(f32[40,128]{1,0:T(8,128)} %get-tuple-element.30) | copy-start | bytes 61444
